TPU v7x, 32 devices: a whole 2x2x4 slice. The times are simulated.
32 devices in a mesh: expert: 4 (over x, core), shard: 8 (over z, y).
Axes of the slice: x: 2, y: 2, z: 4, core: 2. Of those that a mesh axis runs over, the one named last changes fastest.
Arguments:
- hidden_in: float32 [8192, 1024], P(('expert', 'shard')), may hold values from -6 to 6
- cotangent: float32 [8192, 1024], P(('expert', 'shard')), may hold values from -6 to 6
- doc_lengths: int32 [4, 4], replicated, may hold values from 1 to 1280, 2048 in all within a row
- routes: int32 [2, 8192, 8], P(None, ('expert', 'shard')), may hold values from 0 to 15, all different within a row; in each aligned block of 256 rows (0 to 255, 256 to 511, ..., all dimensions but the last counted through in order) at most 160 rows name the same one
- gains: float32 [2, 2, 1024], P(None, None, 'shard'), may hold values from 0.5 to 1.5
- gains_first: float32 [2, 2, 1024], P(None, None, 'shard'), may hold values from -149.34096 to 149.34096
- gains_second: float32 [2, 2, 1024], P(None, None, 'shard'), may hold values from 5406.72 to 21299.2
- w_qkv: float32 [2, 1024, 2048], P(None, 'shard'), may hold values from -0.1875 to 0.1875
- w_qkv_first: float32 [2, 1024, 2048], P(None, 'shard'), may hold values from -90.96222 to 90.96222
- w_qkv_second: float32 [2, 1024, 2048], P(None, 'shard'), may hold values from 1945.6 to 7782.4
- w_out: float32 [2, 1024, 1024], P(None, 'shard'), may hold values from -1.5 to 1.5
- w_out_first: float32 [2, 1024, 1024], P(None, 'shard'), may hold values from -9.96 to 9.96
- w_out_second: float32 [2, 1024, 1024], P(None, 'shard'), may hold values from 24 to 96
- router: float32 [2, 1024, 16], P(None, 'shard'), may hold values from -0.1875 to 0.1875
- router_first: float32 [2, 1024, 16], P(None, 'shard'), may hold values from -192 to 192
- router_second: float32 [2, 1024, 16], P(None, 'shard'), may hold values from 9216 to 36864
- w_in: float32 [2, 16, 1024, 1024], P(None, 'expert', 'shard'), may hold values from -0.1875 to 0.1875
- w_in_first: float32 [2, 16, 1024, 1024], P(None, 'expert', 'shard'), may hold values from -12.48 to 12.48
- w_in_second: float32 [2, 16, 1024, 1024], P(None, 'expert', 'shard'), may hold values from 35.84 to 143.36
- w_down: float32 [2, 16, 512, 1024], P(None, 'expert', 'shard'), may hold values from -0.75 to 0.75
- w_down_first: float32 [2, 16, 512, 1024], P(None, 'expert', 'shard'), may hold values from -3.36 to 3.36
- w_down_second: float32 [2, 16, 512, 1024], P(None, 'expert', 'shard'), may hold values from 2.56 to 10.24
Outputs:
- hidden_out: float32 [8192, 1024], P(('expert', 'shard'))
- input_grad: float32 [8192, 1024], P(('expert', 'shard'))
- gains_grad: float32 [2, 2, 1024], P(None, None, 'shard')
- gains_first_new: float32 [2, 2, 1024], P(None, None, 'shard')
- gains_second_new: float32 [2, 2, 1024], P(None, None, 'shard')
- gains_step: float32 [2, 2, 1024], P(None, None, 'shard')
- w_qkv_grad: float32 [2, 1024, 2048], P(None, 'shard')
- w_qkv_first_new: float32 [2, 1024, 2048], P(None, 'shard')
- w_qkv_second_new: float32 [2, 1024, 2048], P(None, 'shard')
- w_qkv_step: float32 [2, 1024, 2048], P(None, 'shard')
- w_out_grad: float32 [2, 1024, 1024], P(None, 'shard')
- w_out_first_new: float32 [2, 1024, 1024], P(None, 'shard')
- w_out_second_new: float32 [2, 1024, 1024], P(None, 'shard')
- w_out_step: float32 [2, 1024, 1024], P(None, 'shard')
- router_grad: float32 [2, 1024, 16], P(None, 'shard')
- router_first_new: float32 [2, 1024, 16], P(None, 'shard')
- router_second_new: float32 [2, 1024, 16], P(None, 'shard')
- router_step: float32 [2, 1024, 16], P(None, 'shard')
- w_in_grad: float32 [2, 16, 1024, 1024], P(None, 'expert', 'shard')
- w_in_first_new: float32 [2, 16, 1024, 1024], P(None, 'expert', 'shard')
- w_in_second_new: float32 [2, 16, 1024, 1024], P(None, 'expert', 'shard')
- w_in_step: float32 [2, 16, 1024, 1024], P(None, 'expert', 'shard')
- w_down_grad: float32 [2, 16, 512, 1024], P(None, 'expert', 'shard')
- w_down_first_new: float32 [2, 16, 512, 1024], P(None, 'expert', 'shard')
- w_down_second_new: float32 [2, 16, 512, 1024], P(None, 'expert', 'shard')
- w_down_step: float32 [2, 16, 512, 1024], P(None, 'expert', 'shard')
Inputs may be any that keep to these rules, and one draw needn't show every extreme that they name: `routes`: each row names 8 different experts; within the 256 tokens of one device, in each layer, no expert is named by more than 160 rows, a bound that some block reaches. `doc_lengths`: each row sums to 2048; its longest document has exactly 1280 tokens.
All inputs are finite; a program needn't handle non-finite values.
Results may differ from a plain program's by a relative error of at most 0.03.
Values may be sent and summed in bfloat16 or wider, within the bound.
A program may use at most 384 MiB of HBM per device.

v0:
```python
from functools import partial

import jax
import jax.numpy as jnp
from jax import lax
from jax.sharding import PartitionSpec as P

HEADS = 16
KV_HEADS = 8
HEAD = 64
TOP = 8
LAYERS = 2
WINDOW = 1024
SPAN = 8


norm_eps = 1e-05
masked_score = -1e30
beta_one = 0.9
beta_two = 0.95
adam_eps = 1e-08
learn_rate = 0.05
decay_rate = 0.1
adam_step = 10.0


def shifted(block, axis, distance):
    devices = range(lax.axis_size(axis))
    route = [(i - distance, i) for i in devices if i - distance in devices]
    return lax.ppermute(block, axis, route)


def rms_scale(values, gain_row):
    return (
        values * lax.rsqrt(jnp.mean(values * values, axis=-1, keepdims=True) + norm_eps) * gain_row
    )


def select_softmax(pick_table, logits):
    chosen = jnp.sum(pick_table * logits[:, None, :], axis=-1)
    return jax.nn.softmax(chosen, axis=-1)


def swiglu(gate_up):
    half_width = gate_up.shape[-1] // 2
    return jax.nn.silu(gate_up[..., :half_width]) * gate_up[..., half_width:]


def inner_rows(left_side, right_side):
    return lax.dot_general(
        left_side, right_side, (((0,), (0,)), ((), ())), preferred_element_type=jnp.float32
    )


def outer_cols(left_side, right_side):
    return lax.dot_general(
        left_side, right_side, (((1,), (1,)), ((), ())), preferred_element_type=jnp.float32
    )


def adam_update(weight, gradient, first_moment, second_moment):
    new_first = beta_one * first_moment + (1.0 - beta_one) * gradient
    new_second = beta_two * second_moment + (1.0 - beta_two) * gradient * gradient
    corr_first = new_first / (1.0 - beta_one**adam_step)
    corr_second = new_second / (1.0 - beta_two**adam_step)
    weight_step = -learn_rate * (
        corr_first / (jnp.sqrt(corr_second) + adam_eps) + decay_rate * weight
    )
    return [gradient, new_first, new_second, weight_step]


def on_device(
    hidden_in,
    cotangent,
    doc_lengths,
    routes,
    gains,
    gains_first,
    gains_second,
    w_qkv,
    w_qkv_first,
    w_qkv_second,
    w_out,
    w_out_first,
    w_out_second,
    router,
    router_first,
    router_second,
    w_in,
    w_in_first,
    w_in_second,
    w_down,
    w_down_first,
    w_down_second,
):
    tok_rows = hidden_in.shape[0]
    owners = lax.axis_size("expert")
    shards = lax.axis_size("shard")
    local_experts = w_in.shape[1]
    experts_total = local_experts * owners
    capacity = tok_rows * TOP * 5 // (4 * experts_total)
    seq_len = tok_rows * SPAN
    hop_count = min(-(-WINDOW // tok_rows), SPAN - 1)
    key_count = (hop_count + 1) * tok_rows
    q_width = HEADS * HEAD
    kv_width = KV_HEADS * HEAD
    groups = HEADS // KV_HEADS
    score_scale = HEAD ** (-0.5)
    width = hidden_in.shape[1]
    row_start = (lax.axis_index("expert") * shards + lax.axis_index("shard")) * tok_rows
    my_seq = row_start // seq_len
    doc_ends = jnp.cumsum(lax.dynamic_slice_in_dim(doc_lengths, my_seq, 1, 0)[0])
    query_rows = row_start + jnp.arange(tok_rows, dtype=jnp.int32)
    key_rows = row_start - hop_count * tok_rows + jnp.arange(key_count, dtype=jnp.int32)
    query_docs = jnp.sum(
        (query_rows[:, None] % seq_len >= doc_ends[None, :]).astype(jnp.int32), axis=1
    )
    key_docs = jnp.sum((key_rows[:, None] % seq_len >= doc_ends[None, :]).astype(jnp.int32), axis=1)
    distance = query_rows[:, None] - key_rows[None, :]
    allowed = (
        (query_rows[:, None] // seq_len == key_rows[None, :] // seq_len)
        & (query_docs[:, None] == key_docs[None, :])
        & (distance >= 0)
        & (distance < WINDOW)
    )
    expert_ids = jnp.arange(experts_total, dtype=jnp.int32)

    def layer_shards(layer_no):
        return (
            gains[layer_no].astype(jnp.bfloat16),
            w_qkv[layer_no].astype(jnp.bfloat16),
            w_out[layer_no].astype(jnp.bfloat16),
            router[layer_no].astype(jnp.bfloat16),
            w_in[layer_no].astype(jnp.bfloat16),
            w_down[layer_no].astype(jnp.bfloat16),
        )

    kept_layers = []
    stream = hidden_in
    for layer_no in range(LAYERS):
        pieces = layer_shards(layer_no)
        layer_full = (
            lax.all_gather(pieces[0], "shard", axis=1, tiled=True),
            lax.all_gather(pieces[1], "shard", axis=0, tiled=True),
            lax.all_gather(pieces[2], "shard", axis=0, tiled=True),
            lax.all_gather(pieces[3], "shard", axis=0, tiled=True),
            lax.all_gather(pieces[4], "shard", axis=1, tiled=True),
            lax.all_gather(pieces[5], "shard", axis=1, tiled=True),
        )
        layer_routes = routes[layer_no]
        flat_routes = layer_routes.reshape(-1)
        route_hits = (flat_routes[:, None] == expert_ids[None, :]).astype(jnp.int32)
        slot_index = jnp.sum((jnp.cumsum(route_hits, axis=0) - 1) * route_hits, axis=1)
        places = flat_routes * capacity + slot_index
        assigns = jnp.arange(tok_rows * TOP, dtype=jnp.int32)
        token_of = (
            jnp.full((experts_total * capacity,), tok_rows, jnp.int32)
            .at[places]
            .set(assigns // TOP)
        )
        assign_of = (
            jnp.full((experts_total * capacity,), tok_rows * TOP, jnp.int32).at[places].set(assigns)
        )
        pick_table = (layer_routes[:, :, None] == expert_ids[None, None, :]).astype(jnp.float32)
        places, token_of, assign_of, pick_table = (places, token_of, assign_of, pick_table)
        gain_pair = layer_full[0].astype(jnp.float32)
        normed_one = rms_scale(stream, gain_pair[0]).astype(jnp.bfloat16)
        qkv_rows = jnp.dot(normed_one, layer_full[1], preferred_element_type=jnp.float32).astype(
            jnp.bfloat16
        )
        queries = qkv_rows[:, :q_width].reshape(tok_rows, KV_HEADS, groups, HEAD)
        arriving = (qkv_rows[:, q_width : q_width + kv_width], qkv_rows[:, q_width + kv_width :])
        key_parts = [arriving[0]]
        value_parts = [arriving[1]]
        for step_no in range(hop_count):
            arriving = shifted((arriving[0], arriving[1]), "shard", 1)
            key_parts.insert(0, arriving[0])
            value_parts.insert(0, arriving[1])
        ext_keys = jnp.concatenate(key_parts, 0).reshape(key_count, KV_HEADS, HEAD)
        ext_values = jnp.concatenate(value_parts, 0).reshape(key_count, KV_HEADS, HEAD)
        scores = (
            jnp.einsum("tngd,snd->ngts", queries, ext_keys, preferred_element_type=jnp.float32)
            * score_scale
        )
        masked = jnp.where(allowed, scores, masked_score)
        row_top = jnp.max(masked, axis=-1, keepdims=True)
        log_total = row_top + jnp.log(jnp.sum(jnp.exp(masked - row_top), axis=-1, keepdims=True))
        prob_rows = jnp.exp(masked - log_total).astype(jnp.bfloat16)
        attended = (
            jnp.einsum("ngts,snd->tngd", prob_rows, ext_values, preferred_element_type=jnp.float32)
            .astype(jnp.bfloat16)
            .reshape(tok_rows, q_width)
        )
        mixed = stream + jnp.dot(attended, layer_full[2], preferred_element_type=jnp.float32)
        normed_two = rms_scale(mixed, gain_pair[1]).astype(jnp.bfloat16)
        logits = jnp.dot(normed_two, layer_full[3], preferred_element_type=jnp.float32)
        weights = select_softmax(pick_table, logits)
        padded = jnp.concatenate([normed_two, jnp.zeros((1, width), jnp.bfloat16)], 0)
        send_rows = padded[token_of].reshape(owners, local_experts, capacity, width)

        def expert_forward(slot_rows, w_in_full=layer_full[4], w_down_full=layer_full[5]):
            gate_up = jnp.einsum(
                "sekd,edf->sekf", slot_rows, w_in_full, preferred_element_type=jnp.float32
            )
            outputs = jnp.einsum(
                "sekf,efd->sekd",
                swiglu(gate_up).astype(jnp.bfloat16),
                w_down_full,
                preferred_element_type=jnp.float32,
            ).astype(jnp.bfloat16)
            return (outputs, gate_up, slot_rows)

        outputs, gate_up, slot_rows = expert_forward(
            lax.all_to_all(send_rows, "expert", split_axis=0, concat_axis=0, tiled=True)
        )
        returned = lax.all_to_all(
            outputs, "expert", split_axis=0, concat_axis=0, tiled=True
        ).reshape(experts_total * capacity, width)
        picked = returned[places].reshape(tok_rows, TOP, width)
        stream = mixed + jnp.sum(weights[:, :, None] * picked.astype(jnp.float32), axis=1)
        kept_full = None
        kept_layers.append(
            (
                normed_one,
                queries,
                ext_keys,
                ext_values,
                log_total,
                attended,
                mixed,
                normed_two,
                logits,
                weights,
                picked,
                gate_up,
                slot_rows,
                places,
                assign_of,
                pick_table,
                kept_full,
            )
        )
    grad_stream = cotangent
    collected = [None] * LAYERS
    for layer_no in reversed(range(LAYERS)):
        (
            normed_one,
            queries,
            ext_keys,
            ext_values,
            log_total,
            attended,
            mixed,
            normed_two,
            logits,
            weights,
            picked,
            gate_up,
            slot_rows,
            places,
            assign_of,
            pick_table,
            kept_full,
        ) = kept_layers[layer_no]
        pieces = layer_shards(layer_no)
        layer_full = (
            lax.all_gather(pieces[0], "shard", axis=1, tiled=True),
            lax.all_gather(pieces[1], "shard", axis=0, tiled=True),
            lax.all_gather(pieces[2], "shard", axis=0, tiled=True),
            lax.all_gather(pieces[3], "shard", axis=0, tiled=True),
            lax.all_gather(pieces[4], "shard", axis=1, tiled=True),
            lax.all_gather(pieces[5], "shard", axis=1, tiled=True),
        )
        gain_pair = layer_full[0].astype(jnp.float32)
        if layer_no == 0:
            layer_input = hidden_in
        else:
            layer_input = kept_layers[layer_no - 1][6] + jnp.sum(
                kept_layers[layer_no - 1][9][:, :, None]
                * kept_layers[layer_no - 1][10].astype(jnp.float32),
                axis=1,
            )
        d_weights = jnp.sum(grad_stream[:, None, :] * picked.astype(jnp.float32), axis=-1)
        d_picked = (
            (weights[:, :, None] * grad_stream[:, None, :])
            .astype(jnp.bfloat16)
            .reshape(tok_rows * TOP, width)
        )
        d_padded = jnp.concatenate([d_picked, jnp.zeros((1, width), jnp.bfloat16)], 0)
        d_send = d_padded[assign_of].reshape(owners, local_experts, capacity, width)
        d_outputs = lax.all_to_all(d_send, "expert", split_axis=0, concat_axis=0, tiled=True)
        hidden_val, swiglu_back = jax.vjp(swiglu, gate_up)
        d_w_down = jnp.einsum(
            "sekf,sekd->efd",
            hidden_val.astype(jnp.bfloat16),
            d_outputs,
            preferred_element_type=jnp.float32,
        )
        d_hidden = jnp.einsum(
            "sekd,efd->sekf", d_outputs, layer_full[5], preferred_element_type=jnp.float32
        )
        d_gate_up = swiglu_back(d_hidden)[0].astype(jnp.bfloat16)
        d_w_in = jnp.einsum(
            "sekd,sekf->edf", slot_rows, d_gate_up, preferred_element_type=jnp.float32
        )
        d_items = jnp.einsum(
            "sekf,edf->sekd", d_gate_up, layer_full[4], preferred_element_type=jnp.float32
        ).astype(jnp.bfloat16)
        d_returned = lax.all_to_all(
            d_items, "expert", split_axis=0, concat_axis=0, tiled=True
        ).reshape(experts_total * capacity, width)
        d_normed_two = jnp.sum(
            d_returned[places].reshape(tok_rows, TOP, width).astype(jnp.float32), axis=1
        )
        weights_again, select_back = jax.vjp(partial(select_softmax, pick_table), logits)
        d_logits = select_back(d_weights)[0].astype(jnp.bfloat16)
        d_router = inner_rows(normed_two, d_logits)
        d_normed_two = d_normed_two + outer_cols(d_logits, layer_full[3])
        normed_again, norm_back = jax.vjp(rms_scale, mixed, gain_pair[1])
        d_mixed_norm, d_gain_two = norm_back(d_normed_two)
        grad_mixed = grad_stream + d_mixed_norm
        d_att = grad_mixed.astype(jnp.bfloat16)
        d_w_out = inner_rows(attended, d_att)
        d_attended = (
            outer_cols(d_att, layer_full[2])
            .astype(jnp.bfloat16)
            .reshape(tok_rows, KV_HEADS, groups, HEAD)
        )
        scores = (
            jnp.einsum("tngd,snd->ngts", queries, ext_keys, preferred_element_type=jnp.float32)
            * score_scale
        )
        prob_rows = jnp.exp(jnp.where(allowed, scores, masked_score) - log_total)
        d_probs = jnp.einsum(
            "tngd,snd->ngts", d_attended, ext_values, preferred_element_type=jnp.float32
        )
        d_scores = (
            prob_rows * (d_probs - jnp.sum(prob_rows * d_probs, axis=-1, keepdims=True))
        ).astype(jnp.bfloat16)
        d_queries = (
            jnp.einsum("ngts,snd->tngd", d_scores, ext_keys, preferred_element_type=jnp.float32)
            * score_scale
        )
        d_keys = (
            jnp.einsum("ngts,tngd->snd", d_scores, queries, preferred_element_type=jnp.float32)
            * score_scale
        )
        d_values = jnp.einsum(
            "ngts,tngd->snd",
            prob_rows.astype(jnp.bfloat16),
            d_attended,
            preferred_element_type=jnp.float32,
        )
        key_blocks = d_keys.reshape(hop_count + 1, tok_rows, kv_width)
        value_blocks = d_values.reshape(hop_count + 1, tok_rows, kv_width)
        carried = (key_blocks[0], value_blocks[0])
        for step_no in range(hop_count):
            arrived = (
                shifted(carried[0].astype(jnp.bfloat16), "shard", -1).astype(jnp.float32),
                shifted(carried[1].astype(jnp.bfloat16), "shard", -1).astype(jnp.float32),
            )
            carried = (arrived[0] + key_blocks[step_no + 1], arrived[1] + value_blocks[step_no + 1])
        d_qkv = jnp.concatenate(
            [d_queries.reshape(tok_rows, q_width), carried[0], carried[1]], 1
        ).astype(jnp.bfloat16)
        d_w_qkv = inner_rows(normed_one, d_qkv)
        d_normed_one = outer_cols(d_qkv, layer_full[1])
        normed_again, norm_back = jax.vjp(rms_scale, layer_input, gain_pair[0])
        d_input_norm, d_gain_one = norm_back(d_normed_one)
        grad_stream = grad_mixed + d_input_norm
        d_gains = jnp.stack([d_gain_one, d_gain_two], 0)
        reduced = (
            lax.psum_scatter(
                d_gains.astype(jnp.bfloat16), "shard", scatter_dimension=1, tiled=True
            ).astype(jnp.float32),
            lax.psum_scatter(
                d_w_qkv.astype(jnp.bfloat16), "shard", scatter_dimension=0, tiled=True
            ).astype(jnp.float32),
            lax.psum_scatter(
                d_w_out.astype(jnp.bfloat16), "shard", scatter_dimension=0, tiled=True
            ).astype(jnp.float32),
            lax.psum_scatter(
                d_router.astype(jnp.bfloat16), "shard", scatter_dimension=0, tiled=True
            ).astype(jnp.float32),
            lax.psum_scatter(
                d_w_in.astype(jnp.bfloat16), "shard", scatter_dimension=1, tiled=True
            ).astype(jnp.float32),
            lax.psum_scatter(
                d_w_down.astype(jnp.bfloat16), "shard", scatter_dimension=1, tiled=True
            ).astype(jnp.float32),
        )
        mixer_sums = (
            lax.psum(reduced[0].astype(jnp.bfloat16), "expert").astype(jnp.float32),
            lax.psum(reduced[1].astype(jnp.bfloat16), "expert").astype(jnp.float32),
            lax.psum(reduced[2].astype(jnp.bfloat16), "expert").astype(jnp.float32),
            lax.psum(reduced[3].astype(jnp.bfloat16), "expert").astype(jnp.float32),
        )
        collected[layer_no] = (
            mixer_sums[0],
            mixer_sums[1],
            mixer_sums[2],
            mixer_sums[3],
            reduced[4],
            reduced[5],
        )
    stacked = [
        jnp.stack([collected[layer_no][member] for layer_no in range(LAYERS)], 0)
        for member in range(6)
    ]
    results = [stream, grad_stream]
    results.extend(adam_update(gains, stacked[0], gains_first, gains_second))
    results.extend(adam_update(w_qkv, stacked[1], w_qkv_first, w_qkv_second))
    results.extend(adam_update(w_out, stacked[2], w_out_first, w_out_second))
    results.extend(adam_update(router, stacked[3], router_first, router_second))
    results.extend(adam_update(w_in, stacked[4], w_in_first, w_in_second))
    results.extend(adam_update(w_down, stacked[5], w_down_first, w_down_second))
    return tuple(results)


def solution(mesh):
    return jax.shard_map(
        on_device,
        mesh=mesh,
        in_specs=(
            P(("expert", "shard"), None),
            P(("expert", "shard"), None),
            P(),
            P(None, ("expert", "shard"), None),
            P(None, None, "shard"),
            P(None, None, "shard"),
            P(None, None, "shard"),
            P(None, "shard", None),
            P(None, "shard", None),
            P(None, "shard", None),
            P(None, "shard", None),
            P(None, "shard", None),
            P(None, "shard", None),
            P(None, "shard", None),
            P(None, "shard", None),
            P(None, "shard", None),
            P(None, "expert", "shard", None),
            P(None, "expert", "shard", None),
            P(None, "expert", "shard", None),
            P(None, "expert", "shard", None),
            P(None, "expert", "shard", None),
            P(None, "expert", "shard", None),
        ),
        out_specs=(
            P(("expert", "shard"), None),
            P(("expert", "shard"), None),
            P(None, None, "shard"),
            P(None, None, "shard"),
            P(None, None, "shard"),
            P(None, None, "shard"),
            P(None, "shard", None),
            P(None, "shard", None),
            P(None, "shard", None),
            P(None, "shard", None),
            P(None, "shard", None),
            P(None, "shard", None),
            P(None, "shard", None),
            P(None, "shard", None),
            P(None, "shard", None),
            P(None, "shard", None),
            P(None, "shard", None),
            P(None, "shard", None),
            P(None, "expert", "shard", None),
            P(None, "expert", "shard", None),
            P(None, "expert", "shard", None),
            P(None, "expert", "shard", None),
            P(None, "expert", "shard", None),
            P(None, "expert", "shard", None),
            P(None, "expert", "shard", None),
            P(None, "expert", "shard", None),
        ),
        check_vma=False,
    )
```

profile of v0, /device:TPU:0, one launch (start us, length us, event | category | flops | bytes accessed | tf_op | source)
XLA Modules:
  0.0 2220.4 jit_solution(17610870860888980895)
XLA Ops:
  19.7 22.8 %all-gather = bf16[1,2,1024]{2,1,0:T(2,128)(2,1)S(1)} all-gather(bf16[1,2,128]{2,1,0:T(2,128)(2,1)S(1)} %get-tuple-element.122), channel_id=2, replica_groups=mesh['expert'=4,'shard'=8] {'shard'}, dimensions={2}, use_global_device_ids=true | all-gather | bytes 4608 | tf_op jit(solution)/shard_map/all_gather | solution.py:143
  55.8 30.4 %all-gather.21.cloned.1.call-done = bf16[1,1024,2048]{2,1,0:T(8,128)(2,1)} async-done(((bf16[1,128,2048]{2,1,0:T(8,128)(2,1)}), bf16[1,1024,2048]{2,1,0:T(8,128)(2,1)}) %all-gather.21.cloned.1.call-update) | async-done | bytes 4194320 | tf_op jit(solution)/shard_map/all_gather | solution.py:144
  106.8 10.4 collective-permute-start.5
  122.8 8.1 scatter_custom_fusion
  130.9 8.1 scatter_custom_fusion.1
  148.6 7.1 collective-permute-start.7
  187.7 8.9 gather_fusion
  203.0 58.1 %all-to-all-done = bf16[4,4,160,1024]{3,2,1,0:T(8,128)(2,1)} async-done(((bf16[4,4,160,1024]{3,2,1,0:T(8,128)(2,1)}), bf16[4,4,160,1024]{3,2,1,0:T(8,128)(2,1)}, u32[]{:S(2)}, u32[]{:S(2)}) %all-to-all-start) | async-done | bytes 5242912 | tf_op jit(solution)/shard_map/all_to_all | solution.py:214
  261.1 16.5 all-gather.25.cloned.1.call-done
  277.6 9.5 fusion.60
  293.9 57.3 %all-gather.27.cloned.1.call-done = bf16[1,4,512,1024]{3,2,1,0:T(8,128)(2,1)} async-done(((bf16[1,4,64,1024]{3,2,1,0:T(8,128)(2,1)}), bf16[1,4,512,1024]{3,2,1,0:T(8,128)(2,1)}) %all-gather.27.cloned.1.call-update) | async-done | bytes 4194320 | tf_op jit(solution)/shard_map/all_gather | solution.py:148
  365.7 18.6 all-gather.6
  384.9 27.3 %all-gather.3 = bf16[1,1024,16]{1,2,0:T(8,128)(2,1)S(1)} all-gather(bf16[1,128,16]{1,2,0:T(8,128)(2,1)S(1)} %get-tuple-element.116), channel_id=5, replica_groups=mesh['expert'=4,'shard'=8] {'shard'}, dimensions={1}, use_global_device_ids=true | all-gather | bytes 36864 | tf_op jit(solution)/shard_map/all_gather | solution.py:146
  414.1 10.9 all-to-all-done.1
  425.1 14.1 gather_fusion.1
  455.1 6.6 collective-permute-done.8
  466.1 6.8 collective-permute-done.12
  480.1 7.4 collective-permute-start.10
  487.5 8.5 collective-permute-start.14
  515.4 6.3 collective-permute-done.15
  548.1 8.9 gather_fusion.2
  562.9 8.2 scatter_custom_fusion.3
  571.2 8.1 scatter_custom_fusion.2
  579.3 43.0 %all-gather.9 = bf16[1,1024,16]{1,2,0:T(8,128)(2,1)S(1)} all-gather(bf16[1,128,16]{1,2,0:T(8,128)(2,1)S(1)} %copy-done.93), channel_id=11, replica_groups=mesh['expert'=4,'shard'=8] {'shard'}, dimensions={1}, use_global_device_ids=true | all-gather | bytes 36864 | tf_op jit(solution)/shard_map/all_gather | solution.py:146
  626.5 14.8 gather_fusion.4
  646.5 12.4 fusion.55
  658.9 42.1 %all-gather.35.cloned.1.call-done = bf16[1,4,512,1024]{3,2,1,0:T(8,128)(2,1)} async-done(((bf16[1,4,64,1024]{3,2,1,0:T(8,128)(2,1)}), bf16[1,4,512,1024]{3,2,1,0:T(8,128)(2,1)}) %all-gather.35.cloned.1.call-update) | async-done | bytes 4194320 | tf_op jit(solution)/shard_map/all_gather | solution.py:148
  705.9 12.3 bitcast_multiply_fusion.7
  718.1 12.3 convert_bitcast_fusion.1
  750.6 50.3 %all-to-all-done.5 = bf16[4,4,160,1024]{3,2,1,0:T(8,128)(2,1)} async-done(((bf16[4,4,160,1024]{3,2,1,0:T(8,128)(2,1)}), bf16[4,4,160,1024]{3,2,1,0:T(8,128)(2,1)}, u32[]{:S(2)}, u32[]{:S(2)}) %all-to-all-start.5) | async-done | bytes 5242912 | tf_op jit(solution)/shard_map/all_to_all | solution.py:309
  806.0 14.1 gather_fusion.5
  825.6 39.8 %all-to-all-done.3 = bf16[4,4,160,1024]{3,2,1,0:T(8,128)(2,1)} async-done(((bf16[4,4,160,1024]{3,2,1,0:T(8,128)(2,1)}), bf16[4,4,160,1024]{3,2,1,0:T(8,128)(2,1)}, u32[]{:S(2)}, u32[]{:S(2)}) %all-to-all-start.3) | async-done | bytes 5242912 | tf_op jit(solution)/shard_map/all_to_all | solution.py:216
  865.4 14.1 gather_fusion.3
  890.5 8.7 convolution_bitcast_fusion.2
  900.7 13.4 fusion.3
  915.4 14.3 fusion.5
  938.4 7.1 collective-permute-done.16
  988.2 14.8 gather_fusion.6
  1011.8 55.9 %all-to-all-done.6 = bf16[4,4,160,1024]{3,2,1,0:T(8,128)(2,1)} async-done(((bf16[4,4,160,1024]{3,2,1,0:T(8,128)(2,1)}), bf16[4,4,160,1024]{3,2,1,0:T(8,128)(2,1)}, u32[]{:S(2)}, u32[]{:S(2)}) %all-to-all-start.6) | async-done | bytes 5242912 | tf_op jit(solution)/shard_map/all_to_all | solution.py:291
  1067.7 11.9 bitcast_multiply_fusion.5
  1079.6 12.5 convert_bitcast_fusion
  1106.4 56.0 %all-to-all-done.7 = bf16[4,4,160,1024]{3,2,1,0:T(8,128)(2,1)} async-done(((bf16[4,4,160,1024]{3,2,1,0:T(8,128)(2,1)}), bf16[4,4,160,1024]{3,2,1,0:T(8,128)(2,1)}, u32[]{:S(2)}, u32[]{:S(2)}) %all-to-all-start.7) | async-done | bytes 5242912 | tf_op jit(solution)/shard_map/all_to_all | solution.py:309
  1162.4 14.5 gather_fusion.7
  1185.1 8.8 convolution_bitcast_fusion
  1199.5 13.3 fusion
  1212.9 14.6 fusion.2
  1235.1 10.0 collective-permute-done.24
  1253.9 7.9 collective-permute-done.25
  1296.4 8.8 bitcast_convert_fusion.2
  1305.2 8.7 bitcast_convert_fusion.3
  1319.1 91.4 %reduce-scatter.21.cloned.1.call-done = bf16[128,2048]{1,0:T(8,128)(2,1)} async-done(((bf16[1024,2048]{1,0:T(8,128)(2,1)}), bf16[128,2048]{1,0:T(8,128)(2,1)}) %reduce-scatter.21.cloned.1.call-update) | async-done | bytes 524304 | tf_op jit(solution)/shard_map/reduce_scatter | solution.py:376
  1410.6 13.8 bitcast_convert_fusion
  1424.7 13.8 bitcast_convert_fusion.1
  1438.5 37.6 %reduce-scatter.43.cloned.1.call-done = bf16[128,16]{1,0:T(8,128)(2,1)} async-done(((bf16[1024,16]{1,0:T(8,128)(2,1)}), bf16[128,16]{1,0:T(8,128)(2,1)}) %reduce-scatter.43.cloned.1.call-update) | async-done | bytes 4112
  1477.0 64.1 %reduce-scatter.39.cloned.1.call-done = bf16[128,2]{1,0:T(8,128)(2,1)} async-done(((bf16[1024,2]{1,0:T(8,128)(2,1)}), bf16[128,2]{1,0:T(8,128)(2,1)}) %reduce-scatter.39.cloned.1.call-update) | async-done | bytes 528
  1541.9 64.1 %reduce-scatter.41.cloned.1.call-done = bf16[128,16]{1,0:T(8,128)(2,1)} async-done(((bf16[1024,16]{1,0:T(8,128)(2,1)}), bf16[128,16]{1,0:T(8,128)(2,1)}) %reduce-scatter.41.cloned.1.call-update) | async-done | bytes 4112
  1608.1 62.8 %reduce-scatter.37.cloned.1.call-done = bf16[128,2]{1,0:T(8,128)(2,1)} async-done(((bf16[1024,2]{1,0:T(8,128)(2,1)}), bf16[128,2]{1,0:T(8,128)(2,1)}) %reduce-scatter.37.cloned.1.call-update) | async-done | bytes 528
  1678.8 83.8 %reduce-scatter.35.cloned.1.call-done = bf16[4,64,1024]{2,1,0:T(8,128)(2,1)} async-done(((bf16[4,512,1024]{2,1,0:T(8,128)(2,1)}), bf16[4,64,1024]{2,1,0:T(8,128)(2,1)}) %reduce-scatter.35.cloned.1.call-update) | async-done | bytes 524304 | tf_op jit(solution)/shard_map/reduce_scatter | solution.py:388
  1762.6 92.4 %reduce-scatter.33.cloned.1.call-done = bf16[4,64,1024]{2,1,0:T(8,128)(2,1)} async-done(((bf16[4,512,1024]{2,1,0:T(8,128)(2,1)}), bf16[4,64,1024]{2,1,0:T(8,128)(2,1)}) %reduce-scatter.33.cloned.1.call-update) | async-done | bytes 524304 | tf_op jit(solution)/shard_map/reduce_scatter | solution.py:388
  1855.1 7.2 add_multiply_fusion.1
  1862.3 37.9 %all-reduce.12.cloned.1.call-done = (bf16[1,128,2048]{2,1,0:T(8,128)(2,1)}, bf16[1,128,2048]{2,1,0:T(8,128)(2,1)}, bf16[1,128,1024]{2,1,0:T(8,128)(2,1)}, bf16[1,128,1024]{2,1,0:T(8,128)(2,1)}) async-done(((bf16[1,128,2048]{2,1,0:T(8,128)(2,1)}, bf16[1,128,2048]{2,1,0:T(8,128)(2,1)}, bf16[1,128,1024]{2,1,0:T(8,128)(2,1)}, bf16[1,128,1024]{2,1,0:T(8,128)(2,1)}), (bf16[1,128,2048]{2,1,0:T(8,128)(2,1)}, ...) | async-done | bytes 1572880 | tf_op jit(solution)/shard_map/psum | solution.py:394
  1908.5 143.2 %reduce-scatter.31.cloned.1.call-done = bf16[4,128,1024]{2,1,0:T(8,128)(2,1)} async-done(((bf16[4,1024,1024]{2,1,0:T(8,128)(2,1)}), bf16[4,128,1024]{2,1,0:T(8,128)(2,1)}) %reduce-scatter.31.cloned.1.call-update) | async-done | bytes 1048592 | tf_op jit(solution)/shard_map/reduce_scatter | solution.py:385
  2051.7 150.6 %reduce-scatter.29.cloned.1.call-done = bf16[4,128,1024]{2,1,0:T(8,128)(2,1)} async-done(((bf16[4,1024,1024]{2,1,0:T(8,128)(2,1)}), bf16[4,128,1024]{2,1,0:T(8,128)(2,1)}) %reduce-scatter.29.cloned.1.call-update) | async-done | bytes 1048592 | tf_op jit(solution)/shard_map/reduce_scatter | solution.py:385
  2202.3 10.8 add_multiply_fusion
  (551 shorter events, 424.0 us)
Async XLA Ops:
  7.2 79.0 %all-gather.21.cloned.1.call-start = ((), (), s32[]{:S(2)}) async-start(), calls=%async_computation.28 | async-start | bytes 4718592 | tf_op jit(solution)/shard_map/all_gather | solution.py:144
  10.2 173.9 %all-gather.23.cloned.1.call-start = ((), (), s32[]{:S(2)}) async-start(), calls=%async_computation.29 | async-start | bytes 2359296 | tf_op jit(solution)/shard_map/all_gather | solution.py:145
  11.1 266.5 %all-gather.25.cloned.1.call-start = ((), (), s32[]{:S(2)}) async-start(), calls=%async_computation.30 | async-start | bytes 9437184 | tf_op jit(solution)/shard_map/all_gather | solution.py:147
  15.4 335.9 %all-gather.27.cloned.1.call-start = ((), (), s32[]{:S(2)}) async-start(), calls=%async_computation.31 | async-start | bytes 4718592 | tf_op jit(solution)/shard_map/all_gather | solution.py:148
  17.3 427.0 %all-gather.29.cloned.1.call-start = ((), (), s32[]{:S(2)}) async-start(), calls=%async_computation.32 | async-start | bytes 4718592 | tf_op jit(solution)/shard_map/all_gather | solution.py:144
  18.0 394.8 %copy-start.70 = (s32[256,8]{0,1:T(8,128)}, s32[256,8]{0,1:T(8,128)S(1)}, u32[]{:S(2)}) copy-start(s32[256,8]{0,1:T(8,128)S(1)} %get-tuple-element.110) | copy-start | bytes 24580
  89.8 10.7 collective-permute-start
  92.6 14.2 collective-permute-start.4
  100.6 16.6 collective-permute-start.1
  106.8 32.2 %collective-permute-start.5 = (bf16[256,512]{1,0:T(8,128)(2,1)S(1)}, bf16[256,512]{1,0:T(8,128)(2,1)S(1)}, u32[]{:S(2)}, u32[]{:S(2)}) collective-permute-start(bf16[256,512]{1,0:T(8,128)(2,1)S(1)} %collective-permute-done.4), channel_id=1, source_target_pairs={{0,1},{1,2},{2,3},{3,4},{4,5},{5,6},{6,7},{8,9},{9,10},{10,11},{11... | collective-permute-start | bytes 786440 | tf_op jit(solution)/shard_map/ppermute | solution.py:30
  117.2 27.8 %collective-permute-start.2 = (bf16[256,512]{1,0:T(8,128)(2,1)S(1)}, bf16[256,512]{1,0:T(8,128)(2,1)S(1)}, u32[]{:S(2)}, u32[]{:S(2)}) collective-permute-start(bf16[256,512]{1,0:T(8,128)(2,1)S(1)} %collective-permute-done.1), channel_id=1, source_target_pairs={{0,1},{1,2},{2,3},{3,4},{4,5},{5,6},{6,7},{8,9},{9,10},{10,11},{11... | collective-permute-start | bytes 786440 | tf_op jit(solution)/shard_map/ppermute | solution.py:30
  139.0 9.6 collective-permute-start.6
  145.0 10.8 collective-permute-start.3
  148.6 11.1 collective-permute-start.7
  186.9 257.0 %copy-start.5 = (f32[256,1024]{1,0:T(8,128)}, f32[256,1024]{1,0:T(8,128)S(1)}, u32[]{:S(2)}) copy-start(f32[256,1024]{1,0:T(8,128)S(1)} %get-tuple-element.126) | copy-start | bytes 3145732
  196.6 64.5 %all-to-all-start = ((bf16[4,4,160,1024]{3,2,1,0:T(8,128)(2,1)}), bf16[4,4,160,1024]{3,2,1,0:T(8,128)(2,1)}, u32[]{:S(2)}, u32[]{:S(2)}) async-start(bf16[4,4,160,1024]{3,2,1,0:T(8,128)(2,1)} %bitcast.430), calls=%async_computation | async-start | bytes 10485760 | tf_op jit(solution)/shard_map/all_to_all | solution.py:214
  201.7 343.3 %all-gather.31.cloned.1.call-start = ((), (), s32[]{:S(2)}) async-start(), calls=%async_computation.33 | async-start | bytes 2359296 | tf_op jit(solution)/shard_map/all_gather | solution.py:145
  202.2 444.2 %all-gather.33.cloned.1.call-start = ((), (), s32[]{:S(2)}) async-start(), calls=%async_computation.34 | async-start | bytes 9437184 | tf_op jit(solution)/shard_map/all_gather | solution.py:147
  360.4 64.6 %all-to-all-start.1 = ((bf16[4,4,160,1024]{3,2,1,0:T(8,128)(2,1)}), bf16[4,4,160,1024]{3,2,1,0:T(8,128)(2,1)}, u32[]{:S(2)}, u32[]{:S(2)}) async-start(bf16[4,4,160,1024]{3,2,1,0:T(8,128)(2,1)} %copy.195), calls=%async_computation.1 | async-start | bytes 10485760 | tf_op jit(solution)/shard_map/all_to_all | solution.py:216
  448.5 13.3 collective-permute-start.8
  451.0 22.0 collective-permute-start.12
  461.7 18.4 collective-permute-start.9
  473.0 14.6 collective-permute-start.13
  480.1 15.9 collective-permute-start.10
  487.5 15.1 collective-permute-start.14
  496.0 16.5 collective-permute-start.11
  502.7 19.1 collective-permute-start.15
  557.0 84.4 %all-to-all-start.2 = ((bf16[4,4,160,1024]{3,2,1,0:T(8,128)(2,1)}), bf16[4,4,160,1024]{3,2,1,0:T(8,128)(2,1)}, u32[]{:S(2)}, u32[]{:S(2)}) async-start(bf16[4,4,160,1024]{3,2,1,0:T(8,128)(2,1)} %bitcast.429), calls=%async_computation.2 | async-start | bytes 10485760 | tf_op jit(solution)/shard_map/all_to_all | solution.py:214
  562.2 138.8 %all-gather.35.cloned.1.call-start = ((), (), s32[]{:S(2)}) async-start(), calls=%async_computation.35 | async-start | bytes 4718592 | tf_op jit(solution)/shard_map/all_gather | solution.py:148
  641.4 64.5 %all-to-all-start.4 = ((bf16[4,4,160,1024]{3,2,1,0:T(8,128)(2,1)}), bf16[4,4,160,1024]{3,2,1,0:T(8,128)(2,1)}, u32[]{:S(2)}, u32[]{:S(2)}) async-start(bf16[4,4,160,1024]{3,2,1,0:T(8,128)(2,1)} %bitcast.432), calls=%async_computation.4 | async-start | bytes 10485760 | tf_op jit(solution)/shard_map/all_to_all | solution.py:291
  736.0 64.9 %all-to-all-start.5 = ((bf16[4,4,160,1024]{3,2,1,0:T(8,128)(2,1)}), bf16[4,4,160,1024]{3,2,1,0:T(8,128)(2,1)}, u32[]{:S(2)}, u32[]{:S(2)}) async-start(bf16[4,4,160,1024]{3,2,1,0:T(8,128)(2,1)} %copy.208), calls=%async_computation.5 | async-start | bytes 10485760 | tf_op jit(solution)/shard_map/all_to_all | solution.py:309
  800.9 64.5 %all-to-all-start.3 = ((bf16[4,4,160,1024]{3,2,1,0:T(8,128)(2,1)}), bf16[4,4,160,1024]{3,2,1,0:T(8,128)(2,1)}, u32[]{:S(2)}, u32[]{:S(2)}) async-start(bf16[4,4,160,1024]{3,2,1,0:T(8,128)(2,1)} %copy.205), calls=%async_computation.3 | async-start | bytes 10485760 | tf_op jit(solution)/shard_map/all_to_all | solution.py:216
  806.0 508.1 %reduce-scatter.27.cloned.1.call-start = ((), (), s32[]{:S(2)}) async-start(), calls=%async_computation.23 | async-start | bytes 2359296 | tf_op jit(solution)/shard_map/reduce_scatter | solution.py:379
  914.1 22.2 %collective-permute-start.20 = (bf16[256,512]{0,1:T(8,128)(2,1)S(1)}, bf16[256,512]{0,1:T(8,128)(2,1)S(1)}, u32[]{:S(2)}, u32[]{:S(2)}) collective-permute-start(bf16[256,512]{0,1:T(8,128)(2,1)S(1)} %bitcast.475), channel_id=1, source_target_pairs={{1,0},{2,1},{3,2},{4,3},{5,4},{6,5},{7,6},{9,8},{10,9},{11,10},{12... | collective-permute-start | bytes 786440 | tf_op jit(solution)/shard_map/ppermute | solution.py:30
  933.8 11.8 collective-permute-start.16
  937.2 13.6 collective-permute-start.21
  946.3 9.9 collective-permute-start.17
  951.8 13.0 collective-permute-start.22
  957.5 9.6 collective-permute-start.18
  965.7 10.9 collective-permute-start.23
  967.8 11.7 collective-permute-start.19
  1003.0 64.7 %all-to-all-start.6 = ((bf16[4,4,160,1024]{3,2,1,0:T(8,128)(2,1)}), bf16[4,4,160,1024]{3,2,1,0:T(8,128)(2,1)}, u32[]{:S(2)}, u32[]{:S(2)}) async-start(bf16[4,4,160,1024]{3,2,1,0:T(8,128)(2,1)} %bitcast.431), calls=%async_computation.6 | async-start | bytes 10485760 | tf_op jit(solution)/shard_map/all_to_all | solution.py:291
  1008.3 305.8 %reduce-scatter.23.cloned.1.call-start = ((), (), s32[]{:S(2)}) async-start(), calls=%async_computation.21 | async-start | bytes 4718592 | tf_op jit(solution)/shard_map/reduce_scatter | solution.py:376
  1097.8 64.7 %all-to-all-start.7 = ((bf16[4,4,160,1024]{3,2,1,0:T(8,128)(2,1)}), bf16[4,4,160,1024]{3,2,1,0:T(8,128)(2,1)}, u32[]{:S(2)}, u32[]{:S(2)}) async-start(bf16[4,4,160,1024]{3,2,1,0:T(8,128)(2,1)} %copy.217), calls=%async_computation.7 | async-start | bytes 10485760 | tf_op jit(solution)/shard_map/all_to_all | solution.py:309
  1103.0 216.0 %reduce-scatter.25.cloned.1.call-start = ((), (), s32[]{:S(2)}) async-start(), calls=%async_computation.22 | async-start | bytes 2359296 | tf_op jit(solution)/shard_map/reduce_scatter | solution.py:379
  1196.1 36.6 %collective-permute-start.28 = (bf16[256,512]{0,1:T(8,128)(2,1)}, bf16[256,512]{0,1:T(8,128)(2,1)}, u32[]{:S(2)}, u32[]{:S(2)}) collective-permute-start(bf16[256,512]{0,1:T(8,128)(2,1)} %bitcast.124), channel_id=1, source_target_pairs={{1,0},{2,1},{3,2},{4,3},{5,4},{6,5},{7,6},{9,8},{10,9},{11,10},{12... | collective-permute-start | bytes 786440 | tf_op jit(solution)/shard_map/ppermute | solution.py:30
  1212.8 197.7 %reduce-scatter.21.cloned.1.call-start = ((), (), s32[]{:S(2)}) async-start(), calls=%async_computation.20 | async-start | bytes 4718592 | tf_op jit(solution)/shard_map/reduce_scatter | solution.py:376
  1230.8 14.4 collective-permute-start.24
  1233.8 18.7 collective-permute-start.29
  1245.3 16.5 collective-permute-start.25
  1252.6 14.8 collective-permute-start.30
  1261.9 11.2 collective-permute-start.26
  1267.5 11.5 collective-permute-start.31
  1273.2 10.5 collective-permute-start.27
  1287.9 188.2 %reduce-scatter.43.cloned.1.call-start = ((), (), s32[]{:S(2)}) async-start(), calls=%async_computation.39 | async-start | bytes 294912
  1289.1 252.0 %reduce-scatter.39.cloned.1.call-start = ((), (), s32[]{:S(2)}) async-start(), calls=%async_computation.37 | async-start | bytes 294912
  1290.1 315.9 %reduce-scatter.41.cloned.1.call-start = ((), (), s32[]{:S(2)}) async-start(), calls=%async_computation.38 | async-start | bytes 294912
  1291.2 379.6 %reduce-scatter.37.cloned.1.call-start = ((), (), s32[]{:S(2)}) async-start(), calls=%async_computation.36 | async-start | bytes 294912
  1296.1 466.5 %reduce-scatter.35.cloned.1.call-start = ((), (), s32[]{:S(2)}) async-start(), calls=%async_computation.27 | async-start | bytes 4718592 | tf_op jit(solution)/shard_map/reduce_scatter | solution.py:388
  1305.2 549.9 %reduce-scatter.33.cloned.1.call-start = ((), (), s32[]{:S(2)}) async-start(), calls=%async_computation.26 | async-start | bytes 4718592 | tf_op jit(solution)/shard_map/reduce_scatter | solution.py:388
  1314.0 586.2 %all-reduce.12.cloned.1.call-start = ((), (), s32[]{:S(2)}) async-start(), calls=%async_computation.40 | async-start | bytes 3145728 | tf_op jit(solution)/shard_map/psum | solution.py:394
  1410.5 641.1 %reduce-scatter.31.cloned.1.call-start = ((), (), s32[]{:S(2)}) async-start(), calls=%async_computation.25 | async-start | bytes 9437184 | tf_op jit(solution)/shard_map/reduce_scatter | solution.py:385
  1424.4 777.9 %reduce-scatter.29.cloned.1.call-start = ((), (), s32[]{:S(2)}) async-start(), calls=%async_computation.24 | async-start | bytes 9437184 | tf_op jit(solution)/shard_map/reduce_scatter | solution.py:385
  1438.5 239.7 %copy-start.75 = (f32[2,128,16]{1,2,0:T(8,128)S(1)}, f32[2,128,16]{1,2,0:T(8,128)}, u32[]{:S(2)}) copy-start(f32[2,128,16]{1,2,0:T(8,128)} %param.35) | copy-start | bytes 49156
  (106 other events, 3047.3 us)
Sparse Core Ops, SparseCore 0:
  10.7 75.4 all-gather.20
  89.0 60.6 all-gather.22
  152.4 125.1 all-gather.24
  280.2 70.9 all-gather.26
  353.8 71.8 all-gather.28
  428.3 58.3 all-gather.30
  489.4 137.2 all-gather.32
  629.5 71.4 all-gather.34
  971.4 73.5 reduce-scatter.26
  1049.1 87.1 reduce-scatter.22
  1213.0 106.0 reduce-scatter.24
  1323.1 87.3 reduce-scatter.20
  1414.4 61.7 reduce-scatter.42
  1479.9 61.0 reduce-scatter.38
  1544.8 61.0 reduce-scatter.40
  1609.7 61.0 reduce-scatter.36
  1674.9 87.7 reduce-scatter.34
  1766.7 88.3 reduce-scatter.32
  1857.6 42.5 all-reduce.11
  1903.7 147.8 reduce-scatter.30
  2055.3 146.9 reduce-scatter.28
where the time goes:
time: 2230 us; the launch traced here: 2220 us
  waiting for transfers between devices  1350 us (61%)
  matrix products  242 us (11%)
  local copies, waits for them, and re-layouts  219 us (10%)
  starting transfers between devices  149 us (7%)
  other arithmetic  125 us (6%)
  blocking collectives  118 us (5%)
    reduce_scatter x2, waiting for transfers between devices, on_device(): lax.psum_scatter(d_w_in.astype(jnp.bfloat16), 'shard', scatter_dimension=...  294 us
    unnamed x25, waiting for transfers between devices  231 us
    reduce_scatter x2, waiting for transfers between devices, on_device(): lax.psum_scatter(d_w_down.astype(jnp.bfloat16), 'shard', scatter_dimensio...  176 us
    all_to_all x2, waiting for transfers between devices, on_device(): lax.all_to_all(d_items, 'expert', split_axis=0, concat_axis=0, tiled=True)  106 us
    ppermute x32, starting transfers between devices, shifted(): return lax.ppermute(block, axis, route)  106 us
    all_gather x2, waiting for transfers between devices, on_device(): lax.all_gather(pieces[5], 'shard', axis=1, tiled=True)  99.4 us
    ppermute x32, waiting for transfers between devices, shifted(): return lax.ppermute(block, axis, route)  92.3 us
    reduce_scatter x2, waiting for transfers between devices, on_device(): lax.psum_scatter(d_w_qkv.astype(jnp.bfloat16), 'shard', scatter_dimension...  91.5 us
  transfers between devices with their start and end apart: 61, of which 43 were waited for; matrix products, arithmetic and copies ran while one was open for 21% of the time, Pallas kernels for 0%

commit v1 on v0

v1 whole, which is shorter than its diff:
```python
import functools

import jax
import jax.numpy as jnp
from jax import lax
from jax.experimental import pallas as pl
from jax.experimental.pallas import tpu as pltpu
from jax.sharding import PartitionSpec as P

HEADS = 16
KV_HEADS = 8
HEAD = 64
TOP = 8
LAYERS = 2
WINDOW = 1024
SPAN = 8

norm_eps = 1e-05
masked_score = -1e30
beta_one = 0.9
beta_two = 0.95
adam_eps = 1e-08
learn_rate = 0.05
decay_rate = 0.1
adam_step = 10.0

F32 = jnp.float32
BF16 = jnp.bfloat16
MESH = pl.DeviceIdType.MESH
VMEM_LIMIT = 60 * 1024 * 1024


def rms_scale(values, gain_row):
    return (
        values * lax.rsqrt(jnp.mean(values * values, axis=-1, keepdims=True) + norm_eps) * gain_row
    )


def inner_rows(left_side, right_side):
    return lax.dot_general(
        left_side, right_side, (((0,), (0,)), ((), ())), preferred_element_type=F32
    )


def outer_cols(left_side, right_side):
    return lax.dot_general(
        left_side, right_side, (((1,), (1,)), ((), ())), preferred_element_type=F32
    )


def adam_update(weight, gradient, first_moment, second_moment):
    new_first = beta_one * first_moment + (1.0 - beta_one) * gradient
    new_second = beta_two * second_moment + (1.0 - beta_two) * gradient * gradient
    corr_first = new_first / (1.0 - beta_one**adam_step)
    corr_second = new_second / (1.0 - beta_two**adam_step)
    weight_step = -learn_rate * (
        corr_first / (jnp.sqrt(corr_second) + adam_eps) + decay_rate * weight
    )
    return [gradient, new_first, new_second, weight_step]


def greet(axis, count):
    me = lax.axis_index(axis)
    barrier = pltpu.get_barrier_semaphore()
    for d in range(1, count):
        pl.semaphore_signal(
            barrier, inc=1, device_id={axis: lax.rem(me + d, count)}, device_id_type=MESH
        )
    pl.semaphore_wait(barrier, count - 1)
    return me


def spread_kernel(count, x_ref, o_ref, send_sem, recv_sem):
    me = greet("expert", count)
    copies = []
    for d in range(1, count):
        copy = pltpu.make_async_remote_copy(
            src_ref=x_ref,
            dst_ref=o_ref.at[me],
            send_sem=send_sem.at[d - 1],
            recv_sem=recv_sem.at[d - 1],
            device_id={"expert": lax.rem(me + d, count)},
            device_id_type=MESH,
        )
        copy.start()
        copies.append(copy)
    o_ref[me] = x_ref[...]
    for copy in copies:
        copy.wait()


def spread(rows, count):
    return pl.pallas_call(
        functools.partial(spread_kernel, count),
        out_shape=jax.ShapeDtypeStruct((count,) + rows.shape, rows.dtype),
        in_specs=[pl.BlockSpec(memory_space=pltpu.VMEM)],
        out_specs=pl.BlockSpec(memory_space=pltpu.VMEM),
        scratch_shapes=[
            pltpu.SemaphoreType.DMA((count - 1,)),
            pltpu.SemaphoreType.DMA((count - 1,)),
        ],
        compiler_params=pltpu.CompilerParams(
            collective_id=1, has_side_effects=True, vmem_limit_bytes=VMEM_LIMIT
        ),
        name="spread",
    )(rows)


def collect_kernel(count, p_ref, o_ref, held, send_sem, recv_sem):
    me = greet("expert", count)
    copies = []
    for d in range(1, count):
        peer = lax.rem(me + d, count)
        copy = pltpu.make_async_remote_copy(
            src_ref=p_ref.at[peer],
            dst_ref=held.at[d - 1],
            send_sem=send_sem.at[d - 1],
            recv_sem=recv_sem.at[d - 1],
            device_id={"expert": peer},
            device_id_type=MESH,
        )
        copy.start()
        copies.append(copy)
    total = p_ref[me].astype(F32)
    for d, copy in enumerate(copies):
        copy.wait()
        total = total + held[d].astype(F32)
    o_ref[...] = total


def collect(parts):
    count, rows, width = parts.shape
    return pl.pallas_call(
        functools.partial(collect_kernel, count),
        out_shape=jax.ShapeDtypeStruct((rows, width), F32),
        in_specs=[pl.BlockSpec(memory_space=pltpu.VMEM)],
        out_specs=pl.BlockSpec(memory_space=pltpu.VMEM),
        scratch_shapes=[
            pltpu.VMEM((count - 1, rows, width), parts.dtype),
            pltpu.SemaphoreType.DMA((count - 1,)),
            pltpu.SemaphoreType.DMA((count - 1,)),
        ],
        compiler_params=pltpu.CompilerParams(
            collective_id=2, has_side_effects=True, vmem_limit_bytes=VMEM_LIMIT
        ),
        name="collect",
    )(parts)


def ring_shard(place, count):
    back = lax.div(place, count // 2)
    return (1 - back) * 2 * place + back * (2 * (count - 1 - place) + 1)


def ring_place(shard, count):
    odd, pair = lax.rem(shard, 2), lax.div(shard, 2)
    return (1 - odd) * pair + odd * (count - 1 - pair)


def signal(barrier, where):
    pl.semaphore_signal(barrier, inc=1, device_id=where, device_id_type=MESH)


def gather_dense_kernel(
    n, rows, x_ref, o_ref, ring_send, ring_recv, pair_send, pair_recv, own_sem
):
    e, s = lax.axis_index("expert"), lax.axis_index("shard")
    core = lax.rem(e, 2)
    partner = e + 1 - 2 * core
    p = ring_place(s, n)
    ways = (ring_shard(lax.rem(p + 1, n), n), ring_shard(lax.rem(p + n - 1, n), n))
    barrier = pltpu.get_barrier_semaphore()
    signal(barrier, {"expert": partner})
    signal(barrier, {"shard": ways[0]})
    signal(barrier, {"shard": ways[1]})
    pl.semaphore_wait(barrier, 3)
    quarter = rows // 4

    def part(side, way):
        return pl.ds(pl.multiple_of(side * 2 * quarter + way * quarter, quarter), quarter)

    def block(way, k):
        return ring_shard(lax.rem(p + (n - k if way == 0 else k), n), n)

    def ring_copy(way, k, src):
        return pltpu.make_async_remote_copy(
            src_ref=src,
            dst_ref=o_ref.at[block(way, k), part(core, way)],
            send_sem=ring_send.at[way, k],
            recv_sem=ring_recv.at[way, k],
            device_id={"shard": ways[way]},
            device_id_type=MESH,
        )

    def pair_copy(way, k, side):
        there = o_ref.at[block(way, k), part(side, way)]
        return pltpu.make_async_remote_copy(
            src_ref=there,
            dst_ref=there,
            send_sem=pair_send.at[way, k - 1],
            recv_sem=pair_recv.at[way, k - 1],
            device_id={"expert": partner},
            device_id_type=MESH,
        )

    for way in range(2):
        ring_copy(way, 0, x_ref.at[part(core, way)]).start()
    own = pltpu.make_async_copy(x_ref, o_ref.at[s], own_sem)
    own.start()

    def step(k, carry):
        for way in range(2):
            came = o_ref.at[block(way, k), part(core, way)]
            pltpu.make_async_remote_copy(
                src_ref=came,
                dst_ref=came,
                send_sem=ring_send.at[way, k - 1],
                recv_sem=ring_recv.at[way, k - 1],
                device_id={"shard": ways[way]},
                device_id_type=MESH,
            ).wait_recv()

            @pl.when(k < n - 1)
            def _():
                ring_copy(way, k, came).start()

            pair_copy(way, k, core).start()
        return carry

    lax.fori_loop(1, n, step, 0)

    def finish(k, carry):
        for way in range(2):
            ring_copy(way, k - 1, x_ref.at[part(core, way)]).wait_send()
            pair_copy(way, k, core).wait_send()
            pair_copy(way, k, 1 - core).wait_recv()
        return carry

    lax.fori_loop(1, n, finish, 0)
    own.wait()


def gather_dense(piece, n):
    rows, columns = piece.shape
    dma = pltpu.SemaphoreType.DMA
    return pl.pallas_call(
        functools.partial(gather_dense_kernel, n, rows),
        out_shape=jax.ShapeDtypeStruct((n, rows, columns), piece.dtype),
        in_specs=[pl.BlockSpec(memory_space=pltpu.VMEM)],
        out_specs=pl.BlockSpec(memory_space=pl.ANY),
        scratch_shapes=[
            dma((2, n - 1)), dma((2, n - 1)), dma((2, n - 1)), dma((2, n - 1)), dma,
        ],
        compiler_params=pltpu.CompilerParams(
            collective_id=3, has_side_effects=True, vmem_limit_bytes=VMEM_LIMIT
        ),
        name="gather_dense",
    )(piece)


def reduce_dense_kernel(
    n, owners, rows, g_ref, o_ref, paired, came, going, crossed, last_in,
    pair_send, pair_recv, ring_send, ring_recv, cross_send, cross_recv, last_send, last_recv,
):
    e, s = lax.axis_index("expert"), lax.axis_index("shard")
    core, x = lax.rem(e, 2), lax.div(e, 2)
    partner = e + 1 - 2 * core
    columns = owners // 2
    p = ring_place(s, n)
    ways = (ring_shard(lax.rem(p + 1, n), n), ring_shard(lax.rem(p + n - 1, n), n))
    barrier = pltpu.get_barrier_semaphore()
    signal(barrier, {"expert": partner})
    signal(barrier, {"shard": ways[0]})
    signal(barrier, {"shard": ways[1]})
    for d in range(1, columns):
        signal(barrier, {"expert": lax.rem(e + 2 * d, owners)})
    pl.semaphore_wait(barrier, 3 + columns - 1)
    half, quarter = rows // 2, rows // 4

    def mine(way):
        return pl.ds(pl.multiple_of(core * half + way * quarter, quarter), quarter)

    def block(way, k):
        return ring_shard(lax.rem(p + (2 * n - 1 - k if way == 0 else k + 1), n), n)

    def pair_copy(k):
        b = block(0, k)
        return pltpu.make_async_remote_copy(
            src_ref=g_ref.at[b, pl.ds(pl.multiple_of((1 - core) * half, half), half)],
            dst_ref=paired.at[b],
            send_sem=pair_send.at[b],
            recv_sem=pair_recv.at[b],
            device_id={"expert": partner},
            device_id_type=MESH,
        )

    def ring_copy(way, k):
        return pltpu.make_async_remote_copy(
            src_ref=going.at[way, k],
            dst_ref=came.at[way, k],
            send_sem=ring_send.at[way, k],
            recv_sem=ring_recv.at[way, k],
            device_id={"shard": ways[way]},
            device_id_type=MESH,
        )

    def own(way, b):
        return g_ref[b, mine(way), :].astype(F32) + paired[
            b, way * quarter : (way + 1) * quarter, :
        ].astype(F32)

    order = []
    for k in range(n):
        for place in (k, n - 2 - k):
            place = place % n
            if place not in order:
                order.append(place)
    for k in order:
        pair_copy(k).start()
    for k in order:
        pair_copy(k).wait_recv()
    for way in range(2):
        going[way, 0] = own(way, block(way, 0)).astype(BF16)
        ring_copy(way, 0).start()

    def step(k, carry):
        for way in range(2):
            ring_copy(way, k - 1).wait_recv()
            going[way, k] = (
                came[way, k - 1].astype(F32) + own(way, block(way, k))
            ).astype(BF16)
            ring_copy(way, k).start()
        return carry

    lax.fori_loop(1, n - 1, step, 0)
    for way in range(2):
        ring_copy(way, n - 2).wait_recv()
        crossed[x, way * quarter : (way + 1) * quarter, :] = (
            came[way, n - 2].astype(F32) + own(way, s)
        ).astype(BF16)

    def cross_copy(d):
        return pltpu.make_async_remote_copy(
            src_ref=crossed.at[x],
            dst_ref=crossed.at[x],
            send_sem=cross_send.at[d - 1],
            recv_sem=cross_recv.at[d - 1],
            device_id={"expert": lax.rem(e + 2 * d, owners)},
            device_id_type=MESH,
        )

    for d in range(1, columns):
        cross_copy(d).start()
    for d in range(1, columns):
        cross_copy(d).wait()
    total = crossed[0].astype(F32)
    for d in range(1, columns):
        total = total + crossed[d].astype(F32)
    here = pl.ds(pl.multiple_of(core * half, half), half)
    o_ref[here, :] = total.astype(BF16)
    last = pltpu.make_async_remote_copy(
        src_ref=o_ref.at[here],
        dst_ref=last_in,
        send_sem=last_send,
        recv_sem=last_recv,
        device_id={"expert": partner},
        device_id_type=MESH,
    )
    last.start()
    for k in order:
        pair_copy(k).wait_send()

    def finish(k, carry):
        for way in range(2):
            ring_copy(way, k).wait_send()
        return carry

    lax.fori_loop(0, n - 1, finish, 0)
    last.wait()
    o_ref[pl.ds(pl.multiple_of((1 - core) * half, half), half), :] = last_in[...]


def reduce_dense(grads, n, owners):
    rows, columns = grads.shape[1:]
    dma = pltpu.SemaphoreType.DMA
    across = owners // 2
    return pl.pallas_call(
        functools.partial(reduce_dense_kernel, n, owners, rows),
        out_shape=jax.ShapeDtypeStruct((rows, columns), BF16),
        in_specs=[pl.BlockSpec(memory_space=pltpu.VMEM)],
        out_specs=pl.BlockSpec(memory_space=pltpu.VMEM),
        scratch_shapes=[
            pltpu.VMEM((n, rows // 2, columns), BF16),
            pltpu.VMEM((2, n - 1, rows // 4, columns), BF16),
            pltpu.VMEM((2, n - 1, rows // 4, columns), BF16),
            pltpu.VMEM((across, rows // 2, columns), BF16),
            pltpu.VMEM((rows // 2, columns), BF16),
            dma((n,)), dma((n,)), dma((2, n - 1)), dma((2, n - 1)),
            dma((across - 1,)), dma((across - 1,)), dma, dma,
        ],
        compiler_params=pltpu.CompilerParams(
            collective_id=4, has_side_effects=True, vmem_limit_bytes=VMEM_LIMIT
        ),
        name="reduce_dense",
    )(grads)


def halo_links(n, s):
    odd = lax.rem(s, 2)
    return odd, s + 1 - 2 * odd, s + 2 < n, s >= 2


def halo_barrier(s, odd, mate, ahead, behind, sends_back):
    barrier = pltpu.get_barrier_semaphore()
    even = odd == 0
    to_ahead, to_behind = (ahead, behind) if not sends_back else (behind, ahead)
    step = -2 if not sends_back else 2
    mate_copies = (odd == 1) | behind if not sends_back else even | behind
    to_mate = even | behind if not sends_back else (odd == 1) | behind

    @pl.when(to_behind)
    def _():
        signal(barrier, {"shard": s + step})

    @pl.when(mate_copies)
    def _():
        signal(barrier, {"shard": mate})

    @pl.when(to_ahead & to_mate)
    def _():
        pl.semaphore_wait(barrier, 2)

    @pl.when(to_ahead != to_mate)
    def _():
        pl.semaphore_wait(barrier, 1)


def halo_kernel(n, rows, cuts, kv_ref, o_ref, sends, recvs, own_sem):
    s = lax.axis_index("shard")
    odd, mate, ahead, behind = halo_links(n, s)
    even = odd == 0
    size = rows // cuts

    def copy(kind, cut, src, slot, where):
        return pltpu.make_async_remote_copy(
            src_ref=src.at[pl.ds(cut * size, size)],
            dst_ref=o_ref.at[slot, pl.ds(cut * size, size)],
            send_sem=sends.at[kind, cut],
            recv_sem=recvs.at[kind, cut],
            device_id={"shard": where},
            device_id_type=MESH,
        )

    halo_barrier(s, odd, mate, ahead, behind, False)
    from_odd = (o_ref.at[2], o_ref.at[0])
    from_even = (kv_ref, o_ref.at[2])
    for cut in range(cuts):

        @pl.when(ahead)
        def _():
            copy(0, cut, kv_ref, 2, s + 2).start()

        @pl.when(even)
        def _():
            copy(2, cut, kv_ref, 3, mate).start()

    o_ref[4] = kv_ref[...]
    for slot in range(4):

        @pl.when(s < 4 - slot)
        def _():
            o_ref[slot] = jnp.zeros_like(o_ref[slot])

    for cut in range(cuts):

        @pl.when(behind)
        def _():
            copy(0, cut, kv_ref, 2, s).wait_recv()

        @pl.when(behind & ahead)
        def _():
            copy(1, cut, o_ref.at[2], 0, s + 2).start()

        @pl.when(behind & (odd == 1))
        def _():
            copy(2, cut, from_odd[0], 3, mate).start()

        @pl.when(behind & even)
        def _():
            copy(3, cut, from_even[1], 1, mate).start()

    for cut in range(cuts):

        @pl.when(s >= 4)
        def _():
            copy(1, cut, o_ref.at[2], 0, s).wait_recv()

        @pl.when((s >= 4) & (odd == 1))
        def _():
            copy(3, cut, from_odd[1], 1, mate).start()

    for cut in range(cuts):

        @pl.when(s >= 1)
        def _():
            copy(2, cut, kv_ref, 3, mate).wait_recv()

        @pl.when(s >= 3)
        def _():
            copy(3, cut, kv_ref, 1, mate).wait_recv()

        @pl.when(ahead)
        def _():
            copy(0, cut, kv_ref, 2, s).wait_send()

        @pl.when(behind & ahead)
        def _():
            copy(1, cut, kv_ref, 0, s).wait_send()

        @pl.when(even | behind)
        def _():
            copy(2, cut, kv_ref, 3, mate).wait_send()

        @pl.when((even & behind) | ((odd == 1) & (s >= 4)))
        def _():
            copy(3, cut, kv_ref, 1, mate).wait_send()


def halo(kv, n, slots):
    rows, columns = kv.shape
    dma = pltpu.SemaphoreType.DMA
    cuts = 2
    return pl.pallas_call(
        functools.partial(halo_kernel, n, rows, cuts),
        out_shape=jax.ShapeDtypeStruct((slots, rows, columns), kv.dtype),
        in_specs=[pl.BlockSpec(memory_space=pltpu.VMEM)],
        out_specs=pl.BlockSpec(memory_space=pltpu.VMEM),
        scratch_shapes=[dma((4, cuts)), dma((4, cuts)), dma],
        compiler_params=pltpu.CompilerParams(
            collective_id=5, has_side_effects=True, vmem_limit_bytes=VMEM_LIMIT
        ),
        name="halo",
    )(kv)


def halo_back_kernel(n, rows, cuts, g_ref, o_ref, own, came, sends, recvs):
    s = lax.axis_index("shard")
    odd, mate, ahead, behind = halo_links(n, s)
    even = odd == 0
    size = rows // cuts

    def copy(kind, cut, src, where):
        return pltpu.make_async_remote_copy(
            src_ref=src.at[pl.ds(cut * size, size)],
            dst_ref=came.at[kind, pl.ds(cut * size, size)],
            send_sem=sends.at[kind, cut],
            recv_sem=recvs.at[kind, cut],
            device_id={"shard": where},
            device_id_type=MESH,
        )

    def there(ref, cut, value=None):
        here = pl.ds(cut * size, size)
        return ref[here, :].astype(F32)

    halo_barrier(s, odd, mate, ahead, behind, True)
    for cut in range(cuts):

        @pl.when(s >= 3)
        def _():
            copy(3, cut, g_ref.at[1], mate).start()

        @pl.when(s >= 1)
        def _():
            copy(2, cut, g_ref.at[3], mate).start()

    for cut in range(cuts):
        here = pl.ds(cut * size, size)

        @pl.when((odd == 1) & (s >= 4))
        def _():
            copy(3, cut, g_ref.at[1], mate).wait_recv()
            own[0, here, :] = (there(g_ref.at[0], cut) + there(came.at[3], cut)).astype(BF16)

        @pl.when((odd == 1) & (s >= 4))
        def _():
            copy(1, cut, own.at[0], s - 2).start()

        @pl.when(even & (s >= 4))
        def _():
            copy(1, cut, g_ref.at[0], s - 2).start()

    for cut in range(cuts):
        here = pl.ds(cut * size, size)

        @pl.when((odd == 1) & behind)
        def _():
            copy(2, cut, g_ref.at[3], mate).wait_recv()
            own[1, here, :] = (there(g_ref.at[2], cut) + there(came.at[2], cut)).astype(BF16)

        @pl.when(even & behind)
        def _():
            copy(3, cut, g_ref.at[1], mate).wait_recv()
            own[1, here, :] = (there(g_ref.at[2], cut) + there(came.at[3], cut)).astype(BF16)

        @pl.when(behind & ahead)
        def _():
            copy(1, cut, g_ref.at[0], s).wait_recv()
            own[1, here, :] = (there(own.at[1], cut) + there(came.at[1], cut)).astype(BF16)

        @pl.when(behind)
        def _():
            copy(0, cut, own.at[1], s - 2).start()

    for cut in range(cuts):
        here = pl.ds(cut * size, size)
        o_ref[here, :] = there(g_ref.at[4], cut)

        @pl.when(even)
        def _():
            copy(2, cut, g_ref.at[3], mate).wait_recv()
            o_ref[here, :] += there(came.at[2], cut)

        @pl.when(ahead)
        def _():
            copy(0, cut, own.at[1], s).wait_recv()
            o_ref[here, :] += there(came.at[0], cut)

        @pl.when(s >= 3)
        def _():
            copy(3, cut, g_ref.at[1], mate).wait_send()

        @pl.when(s >= 1)
        def _():
            copy(2, cut, g_ref.at[3], mate).wait_send()

        @pl.when(s >= 4)
        def _():
            copy(1, cut, g_ref.at[0], mate).wait_send()

        @pl.when(behind)
        def _():
            copy(0, cut, own.at[1], mate).wait_send()


def halo_back(grads, n):
    slots, rows, columns = grads.shape
    dma = pltpu.SemaphoreType.DMA
    cuts = 2
    return pl.pallas_call(
        functools.partial(halo_back_kernel, n, rows, cuts),
        out_shape=jax.ShapeDtypeStruct((rows, columns), F32),
        in_specs=[pl.BlockSpec(memory_space=pltpu.VMEM)],
        out_specs=pl.BlockSpec(memory_space=pltpu.VMEM),
        scratch_shapes=[
            pltpu.VMEM((3, rows, columns), BF16),
            pltpu.VMEM((4, rows, columns), BF16),
            dma((4, cuts)),
            dma((4, cuts)),
        ],
        compiler_params=pltpu.CompilerParams(
            collective_id=6, has_side_effects=True, vmem_limit_bytes=VMEM_LIMIT
        ),
        name="halo_back",
    )(grads)


def column_of(extra, index, experts_total):
    lanes = lax.broadcasted_iota(jnp.int32, extra.shape, 1)
    hit = (lanes == index) | (lanes == index + experts_total)
    return jnp.sum(jnp.where(hit, extra.astype(F32), 0.0), axis=1, keepdims=True)


def ffn_forward_kernel(
    tile, width, in_rows, experts_total, first_ref, x_ref, w_ref, part_ref, gate_up_ref, acc
):
    e = pl.program_id(0)
    w_in = w_ref[:, 0, :in_rows, :].reshape(width, w_ref.shape[-1])
    w_down = w_ref[:, 0, in_rows:, :].reshape(-1, width)
    half = w_in.shape[1] // 2
    index = first_ref[0] + e
    count = x_ref.shape[0] // tile
    for t in range(count):
        rows = pl.ds(t * tile, tile)
        gate_up = jnp.dot(x_ref[rows, :width], w_in, preferred_element_type=F32)
        gate, up = gate_up[:, :half], gate_up[:, half:]
        gate_up_ref[0, rows, :] = gate_up.astype(BF16)
        weight = column_of(x_ref[rows, width:], index, experts_total)
        hidden = (gate * jax.nn.sigmoid(gate) * up * weight).astype(BF16)
        out = jnp.dot(hidden, w_down, preferred_element_type=F32)

        @pl.when(e == 0)
        def _():
            acc[rows, :] = out

        @pl.when(e > 0)
        def _():
            acc[rows, :] += out

        @pl.when(e == pl.num_programs(0) - 1)
        def _():
            part_ref[rows, :] = acc[rows, :].astype(BF16)


def ffn_forward(first, x_all, w_all, experts_total, in_rows):
    shards, local, piece, inner = w_all.shape
    tokens, wide = x_all.shape
    width = in_rows * shards
    return pl.pallas_call(
        functools.partial(ffn_forward_kernel, 256, width, in_rows, experts_total),
        grid_spec=pltpu.PrefetchScalarGridSpec(
            num_scalar_prefetch=1,
            grid=(local,),
            in_specs=[
                pl.BlockSpec((tokens, wide), lambda e, f: (0, 0)),
                pl.BlockSpec((shards, 1, piece, inner), lambda e, f: (0, e, 0, 0)),
            ],
            out_specs=[
                pl.BlockSpec((tokens, width), lambda e, f: (0, 0)),
                pl.BlockSpec((1, tokens, inner), lambda e, f: (e, 0, 0)),
            ],
            scratch_shapes=[pltpu.VMEM((tokens, width), F32)],
        ),
        out_shape=[
            jax.ShapeDtypeStruct((tokens, width), BF16),
            jax.ShapeDtypeStruct((local, tokens, inner), BF16),
        ],
        compiler_params=pltpu.CompilerParams(vmem_limit_bytes=VMEM_LIMIT),
        cost_estimate=pl.CostEstimate(
            flops=2 * local * tokens * width * (inner + inner // 2),
            bytes_accessed=2 * (w_all.size + local * tokens * inner + 2 * tokens * wide),
            transcendentals=0,
        ),
        name="ffn_forward",
    )(first, x_all, w_all)


def ffn_backward_kernel(
    tile,
    width,
    in_rows,
    experts_total,
    first_ref,
    x_ref,
    g_ref,
    gate_up_ref,
    w_ref,
    router_ref,
    part_ref,
    grad_ref,
    router_grad_ref,
    acc,
    d_gate_up,
    hidden_all,
    d_logits,
):
    e = pl.program_id(0)
    inner = w_ref.shape[-1]
    w_in = w_ref[:, 0, :in_rows, :].reshape(width, inner)
    w_down = w_ref[:, 0, in_rows:, :].reshape(-1, width)
    half = inner // 2
    index = first_ref[0] + e
    tokens = x_ref.shape[0]
    last = pl.num_programs(0) - 1
    for t in range(tokens // tile):
        rows = pl.ds(t * tile, tile)
        d_plain = outer_cols(g_ref[rows, :width], w_down)
        gate = gate_up_ref[0, rows, :half].astype(F32)
        up = gate_up_ref[0, rows, half:].astype(F32)
        weight = column_of(x_ref[rows, width:], index, experts_total)
        mean_d = column_of(g_ref[rows, width:], 0, 1)
        sig = jax.nn.sigmoid(gate)
        silu = gate * sig
        hidden = silu * up
        d_weight = jnp.sum(hidden * d_plain, axis=1, keepdims=True)
        d_hidden = d_plain * weight
        hidden_all[rows, :] = (hidden * weight).astype(BF16)
        d_gate_up[rows, :half] = (d_hidden * up * sig * (1.0 + gate * (1.0 - sig))).astype(BF16)
        d_gate_up[rows, half:] = (d_hidden * silu).astype(BF16)
        lanes = lax.broadcasted_iota(jnp.int32, (tile, d_logits.shape[1]), 1)
        d_logit = jnp.where(lanes == e, weight * (d_weight - mean_d), 0.0).astype(BF16)
        out = outer_cols(d_gate_up[rows, :], w_in)

        @pl.when(e == 0)
        def _():
            acc[rows, :] = out
            d_logits[rows, :] = d_logit

        @pl.when(e > 0)
        def _():
            acc[rows, :] += out
            d_logits[rows, :] += d_logit

    x = x_ref[:, :width]
    grad_ref[:, 0, :in_rows, :] = (
        inner_rows(x, d_gate_up[...]).astype(BF16).reshape(-1, in_rows, inner)
    )
    grad_ref[:, 0, in_rows:, :] = (
        inner_rows(hidden_all[...], g_ref[:, :width])
        .astype(BF16)
        .reshape(-1, w_ref.shape[2] - in_rows, width)
    )

    @pl.when(e == last)
    def _():
        for t in range(tokens // tile):
            rows = pl.ds(t * tile, tile)
            out = acc[rows, :] + jnp.dot(
                d_logits[rows, :], router_ref[...], preferred_element_type=F32
            )
            part_ref[rows, :] = out.astype(BF16)
        router_grad_ref[...] = inner_rows(x, d_logits[...])


def ffn_backward(first, x_all, g_all, gate_up, w_all, router_rows, experts_total, in_rows):
    shards, local, piece, inner = w_all.shape
    tokens, wide = x_all.shape
    width = in_rows * shards
    lanes = router_rows.shape[0]
    return pl.pallas_call(
        functools.partial(ffn_backward_kernel, 256, width, in_rows, experts_total),
        grid_spec=pltpu.PrefetchScalarGridSpec(
            num_scalar_prefetch=1,
            grid=(local,),
            in_specs=[
                pl.BlockSpec((tokens, wide), lambda e, f: (0, 0)),
                pl.BlockSpec((tokens, g_all.shape[1]), lambda e, f: (0, 0)),
                pl.BlockSpec((1, tokens, inner), lambda e, f: (e, 0, 0)),
                pl.BlockSpec((shards, 1, piece, inner), lambda e, f: (0, e, 0, 0)),
                pl.BlockSpec((lanes, width), lambda e, f: (0, 0)),
            ],
            out_specs=[
                pl.BlockSpec((tokens, width), lambda e, f: (0, 0)),
                pl.BlockSpec((shards, 1, piece, inner), lambda e, f: (0, e, 0, 0)),
                pl.BlockSpec((width, lanes), lambda e, f: (0, 0)),
            ],
            scratch_shapes=[
                pltpu.VMEM((tokens, width), F32),
                pltpu.VMEM((tokens, inner), BF16),
                pltpu.VMEM((tokens, inner // 2), BF16),
                pltpu.VMEM((tokens, lanes), BF16),
            ],
        ),
        out_shape=[
            jax.ShapeDtypeStruct((tokens, width), BF16),
            jax.ShapeDtypeStruct(w_all.shape, BF16),
            jax.ShapeDtypeStruct((width, lanes), F32),
        ],
        compiler_params=pltpu.CompilerParams(vmem_limit_bytes=VMEM_LIMIT),
        cost_estimate=pl.CostEstimate(
            flops=4 * local * tokens * width * (inner + inner // 2),
            bytes_accessed=2 * (2 * w_all.size + local * tokens * inner + 4 * tokens * wide),
            transcendentals=0,
        ),
        name="ffn_backward",
    )(first, x_all, g_all, gate_up, w_all, router_rows)


def on_device(
    hidden_in,
    cotangent,
    doc_lengths,
    routes,
    gains,
    gains_first,
    gains_second,
    w_qkv,
    w_qkv_first,
    w_qkv_second,
    w_out,
    w_out_first,
    w_out_second,
    router,
    router_first,
    router_second,
    w_in,
    w_in_first,
    w_in_second,
    w_down,
    w_down_first,
    w_down_second,
):
    tok_rows, width = hidden_in.shape
    owners = lax.axis_size("expert")
    shards = lax.axis_size("shard")
    local_experts = w_in.shape[1]
    in_rows = w_in.shape[2]
    experts_total = local_experts * owners
    seq_len = tok_rows * SPAN
    hop_count = min(-(-WINDOW // tok_rows), SPAN - 1)
    key_count = (hop_count + 1) * tok_rows
    q_width = HEADS * HEAD
    kv_width = KV_HEADS * HEAD
    qkv_width = q_width + 2 * kv_width
    groups = HEADS // KV_HEADS
    score_scale = HEAD ** (-0.5)
    extra = -(-2 * experts_total // 128) * 128
    my_owner = lax.axis_index("expert")
    first_expert = my_owner * local_experts
    first_array = first_expert.astype(jnp.int32).reshape(1)
    row_start = (my_owner * shards + lax.axis_index("shard")) * tok_rows
    my_seq = row_start // seq_len
    doc_ends = jnp.cumsum(lax.dynamic_slice_in_dim(doc_lengths, my_seq, 1, 0)[0])
    query_rows = row_start + jnp.arange(tok_rows, dtype=jnp.int32)
    key_rows = row_start - hop_count * tok_rows + jnp.arange(key_count, dtype=jnp.int32)
    query_docs = jnp.sum(
        (query_rows[:, None] % seq_len >= doc_ends[None, :]).astype(jnp.int32), axis=1
    )
    key_docs = jnp.sum((key_rows[:, None] % seq_len >= doc_ends[None, :]).astype(jnp.int32), axis=1)
    distance = query_rows[:, None] - key_rows[None, :]
    allowed = (
        (query_rows[:, None] // seq_len == key_rows[None, :] // seq_len)
        & (query_docs[:, None] == key_docs[None, :])
        & (distance >= 0)
        & (distance < WINDOW)
    )
    expert_ids = jnp.arange(experts_total, dtype=jnp.int32)
    side = 128

    def dense_piece():
        rows = w_qkv.shape[1]
        parts = []
        for layer_no in range(LAYERS):
            parts += [w_qkv[layer_no].astype(BF16), w_out[layer_no].astype(BF16)]
        for layer_no in range(LAYERS):
            parts += [router[layer_no].astype(BF16), gains[layer_no].T.astype(BF16)]
        parts.append(jnp.zeros((rows, side - LAYERS * (experts_total + 2)), BF16))
        return jnp.concatenate(parts, 1)

    def expert_piece(layer_no):
        return jnp.concatenate(
            [w_in[layer_no].astype(BF16), w_down[layer_no].astype(BF16)], 1
        )

    layer_columns = qkv_width + width
    dense = gather_dense(dense_piece(), shards).reshape(width, -1)
    expert_full = []
    for layer_no in range(LAYERS):
        expert_full.append(lax.all_gather(expert_piece(layer_no), "shard", axis=0, tiled=False))

    kept_layers = []
    stream = hidden_in
    for layer_no in range(LAYERS):
        at = layer_no * layer_columns
        w_qkv_full = dense[:, at : at + qkv_width]
        w_out_full = dense[:, at + qkv_width : at + layer_columns]
        at = LAYERS * layer_columns + layer_no * (experts_total + 2)
        small = dense[:, at : at + experts_total + 2]
        router_full = small[:, :experts_total]
        gain_pair = small[:, experts_total : experts_total + 2].astype(F32).T
        normed_one = rms_scale(stream, gain_pair[0]).astype(BF16)
        qkv_rows = jnp.dot(normed_one, w_qkv_full, preferred_element_type=F32).astype(BF16)
        queries = qkv_rows[:, :q_width].reshape(tok_rows, KV_HEADS, groups, HEAD)
        ext = halo(qkv_rows[:, q_width:], shards, hop_count + 1).reshape(key_count, 2 * kv_width)
        ext_keys = ext[:, :kv_width].reshape(key_count, KV_HEADS, HEAD)
        ext_values = ext[:, kv_width:].reshape(key_count, KV_HEADS, HEAD)
        scores = (
            jnp.einsum("tngd,snd->ngts", queries, ext_keys, preferred_element_type=F32)
            * score_scale
        )
        masked = jnp.where(allowed, scores, masked_score)
        row_top = jnp.max(masked, axis=-1, keepdims=True)
        log_total = row_top + jnp.log(jnp.sum(jnp.exp(masked - row_top), axis=-1, keepdims=True))
        prob_rows = jnp.exp(masked - log_total).astype(BF16)
        attended = (
            jnp.einsum("ngts,snd->tngd", prob_rows, ext_values, preferred_element_type=F32)
            .astype(BF16)
            .reshape(tok_rows, q_width)
        )
        mixed = stream + jnp.dot(attended, w_out_full, preferred_element_type=F32)
        normed_two = rms_scale(mixed, gain_pair[1]).astype(BF16)
        logits = jnp.dot(normed_two, router_full, preferred_element_type=F32)
        named = jnp.any(routes[layer_no][:, :, None] == expert_ids[None, None, :], axis=1)
        top_logit = jnp.max(jnp.where(named, logits, -jnp.inf), axis=1, keepdims=True)
        powers = jnp.where(named, jnp.exp(jnp.where(named, logits - top_logit, 0.0)), 0.0)
        weights = powers / jnp.sum(powers, axis=1, keepdims=True)
        high = weights.astype(BF16)
        low = (weights - high.astype(F32)).astype(BF16)
        wide_rows = jnp.concatenate(
            [normed_two, high, low, jnp.zeros((tok_rows, extra - 2 * experts_total), BF16)], 1
        )
        x_all = spread(wide_rows, owners).reshape(owners * tok_rows, width + extra)
        partial, gate_up = ffn_forward(
            first_array, x_all, expert_full[layer_no], experts_total, in_rows
        )
        moe_out = collect(partial.reshape(owners, tok_rows, width))
        kept_layers.append(
            (
                stream, normed_one, queries, ext_keys, ext_values, log_total, attended, mixed,
                x_all, gate_up, moe_out, w_qkv_full, w_out_full, router_full, gain_pair,
            )
        )
        stream = mixed + moe_out
    grad_stream = cotangent
    collected = [None] * LAYERS
    dense_parts = [None] * LAYERS
    small_parts = [None] * LAYERS
    for layer_no in reversed(range(LAYERS)):
        (
            layer_input, normed_one, queries, ext_keys, ext_values, log_total, attended, mixed,
            x_all, gate_up, moe_out, w_qkv_full, w_out_full, router_full, gain_pair,
        ) = kept_layers[layer_no]
        mean_d = jnp.sum(grad_stream * moe_out, axis=1, keepdims=True)
        high = mean_d.astype(BF16)
        low = (mean_d - high.astype(F32)).astype(BF16)
        wide_rows = jnp.concatenate(
            [grad_stream.astype(BF16), high, low, jnp.zeros((tok_rows, extra - 2), BF16)], 1
        )
        g_all = spread(wide_rows, owners).reshape(owners * tok_rows, width + extra)
        router_rows = jnp.concatenate(
            [
                lax.dynamic_slice_in_dim(router_full, first_expert, local_experts, 1).T,
                jnp.zeros((side - local_experts, width), BF16),
            ],
            0,
        )
        d_partial, d_experts, d_router_local = ffn_backward(
            first_array, x_all, g_all, gate_up, expert_full[layer_no], router_rows,
            experts_total, in_rows,
        )
        d_experts = lax.psum_scatter(d_experts, "shard", scatter_dimension=0, tiled=True)[0]
        d_normed_two = collect(d_partial.reshape(owners, tok_rows, width))
        _, norm_back = jax.vjp(rms_scale, mixed, gain_pair[1])
        d_mixed_norm, d_gain_two = norm_back(d_normed_two)
        grad_mixed = grad_stream + d_mixed_norm
        d_att = grad_mixed.astype(BF16)
        d_w_out = inner_rows(attended, d_att)
        d_attended = (
            outer_cols(d_att, w_out_full).astype(BF16).reshape(tok_rows, KV_HEADS, groups, HEAD)
        )
        scores = (
            jnp.einsum("tngd,snd->ngts", queries, ext_keys, preferred_element_type=F32)
            * score_scale
        )
        prob_rows = jnp.exp(jnp.where(allowed, scores, masked_score) - log_total)
        d_probs = jnp.einsum("tngd,snd->ngts", d_attended, ext_values, preferred_element_type=F32)
        d_scores = (
            prob_rows * (d_probs - jnp.sum(prob_rows * d_probs, axis=-1, keepdims=True))
        ).astype(BF16)
        d_queries = (
            jnp.einsum("ngts,snd->tngd", d_scores, ext_keys, preferred_element_type=F32)
            * score_scale
        )
        d_keys = (
            jnp.einsum("ngts,tngd->snd", d_scores, queries, preferred_element_type=F32)
            * score_scale
        )
        d_values = jnp.einsum(
            "ngts,tngd->snd", prob_rows.astype(BF16), d_attended, preferred_element_type=F32
        )
        blocks = jnp.concatenate(
            [d_keys.reshape(key_count, kv_width), d_values.reshape(key_count, kv_width)], 1
        ).reshape(hop_count + 1, tok_rows, 2 * kv_width)
        carried = halo_back(blocks.astype(BF16), shards)
        d_qkv = jnp.concatenate([d_queries.reshape(tok_rows, q_width), carried], 1).astype(BF16)
        d_w_qkv = inner_rows(normed_one, d_qkv)
        d_normed_one = outer_cols(d_qkv, w_qkv_full)
        _, norm_back = jax.vjp(rms_scale, layer_input, gain_pair[0])
        d_input_norm, d_gain_one = norm_back(d_normed_one)
        grad_stream = grad_mixed + d_input_norm
        lanes = jnp.arange(experts_total, dtype=jnp.int32)
        d_router = jnp.where(
            (lanes >= first_expert) & (lanes < first_expert + local_experts),
            jnp.tile(d_router_local[:, :local_experts], (1, owners)),
            0.0,
        )
        dense_parts[layer_no] = [d_w_qkv.astype(BF16), d_w_out.astype(BF16)]
        small_parts[layer_no] = [
            d_router.astype(BF16),
            jnp.stack([d_gain_one, d_gain_two], 1).astype(BF16),
        ]
        collected[layer_no] = (
            d_experts[:, :in_rows, :].astype(F32),
            d_experts[:, in_rows:, :].astype(F32),
        )
    parts = sum(dense_parts, []) + sum(small_parts, [])
    parts.append(jnp.zeros((width, side - LAYERS * (experts_total + 2)), BF16))
    d_dense = jnp.concatenate(parts, 1).reshape(shards, width // shards, -1)
    d_dense = reduce_dense(d_dense, shards, owners).astype(F32)
    for layer_no in range(LAYERS):
        at = layer_no * layer_columns
        d_main = d_dense[:, at : at + layer_columns]
        at = LAYERS * layer_columns + layer_no * (experts_total + 2)
        small = d_dense[:, at : at + experts_total + 2]
        collected[layer_no] = (
            small[:, experts_total:].T,
            d_main[:, :qkv_width],
            d_main[:, qkv_width:],
            small[:, :experts_total],
        ) + collected[layer_no]
    stacked = [
        jnp.stack([collected[layer_no][member] for layer_no in range(LAYERS)], 0)
        for member in range(6)
    ]
    results = [stream, grad_stream]
    results.extend(adam_update(gains, stacked[0], gains_first, gains_second))
    results.extend(adam_update(w_qkv, stacked[1], w_qkv_first, w_qkv_second))
    results.extend(adam_update(w_out, stacked[2], w_out_first, w_out_second))
    results.extend(adam_update(router, stacked[3], router_first, router_second))
    results.extend(adam_update(w_in, stacked[4], w_in_first, w_in_second))
    results.extend(adam_update(w_down, stacked[5], w_down_first, w_down_second))
    return tuple(results)


def solution(mesh):
    return jax.shard_map(
        on_device,
        mesh=mesh,
        in_specs=(
            P(("expert", "shard"), None),
            P(("expert", "shard"), None),
            P(),
            P(None, ("expert", "shard"), None),
            P(None, None, "shard"),
            P(None, None, "shard"),
            P(None, None, "shard"),
            P(None, "shard", None),
            P(None, "shard", None),
            P(None, "shard", None),
            P(None, "shard", None),
            P(None, "shard", None),
            P(None, "shard", None),
            P(None, "shard", None),
            P(None, "shard", None),
            P(None, "shard", None),
            P(None, "expert", "shard", None),
            P(None, "expert", "shard", None),
            P(None, "expert", "shard", None),
            P(None, "expert", "shard", None),
            P(None, "expert", "shard", None),
            P(None, "expert", "shard", None),
        ),
        out_specs=(
            P(("expert", "shard"), None),
            P(("expert", "shard"), None),
            P(None, None, "shard"),
            P(None, None, "shard"),
            P(None, None, "shard"),
            P(None, None, "shard"),
            P(None, "shard", None),
            P(None, "shard", None),
            P(None, "shard", None),
            P(None, "shard", None),
            P(None, "shard", None),
            P(None, "shard", None),
            P(None, "shard", None),
            P(None, "shard", None),
            P(None, "shard", None),
            P(None, "shard", None),
            P(None, "shard", None),
            P(None, "shard", None),
            P(None, "expert", "shard", None),
            P(None, "expert", "shard", None),
            P(None, "expert", "shard", None),
            P(None, "expert", "shard", None),
            P(None, "expert", "shard", None),
            P(None, "expert", "shard", None),
            P(None, "expert", "shard", None),
            P(None, "expert", "shard", None),
        ),
        check_vma=False,
    )
```

time: 2230 us -> 1250 us (0.56)
  waiting for transfers between devices: 1350 us -> 0.13 us
  Pallas kernels: 0 us -> 893 us
  starting transfers between devices: 149 us -> 0.16 us
  blocking collectives: 118 us -> 0 us
  matrix products: 242 us -> 128 us
  local copies, waits for them, and re-layouts: 219 us -> 117 us
  other arithmetic: 125 us -> 92.7 us
    pallas_call x0 -> x18, Pallas kernels: none -> 893 us  [the longest x1 175 us: gather_dense(): pl.pallas_call(functools.partial(gather_dense_kernel, n, rows), out_shape...]
    reduce_scatter x8 -> x2, waiting for transfers between devices: 566 us -> 0.02 us  [on_device(): lax.psum_scatter(d_experts, 'shard', scatter_dimension=0, tiled=True)[0]]
    all_to_all x8 -> x0, waiting for transfers between devices: 276 us -> none  [the longest x2 106 us: on_device(): lax.all_to_all(d_items, 'expert', split_axis=0, concat_axis=0, tiled=True)]
    unnamed x25 -> x4, waiting for transfers between devices: 231 us -> 0.07 us
    all_gather x8 -> x2, waiting for transfers between devices: 146 us -> 0.04 us  [on_device(): lax.all_gather(expert_piece(layer_no), 'shard', axis=0, tiled=False)]
    dot_general x26 -> x14, matrix products: 182 us -> 64.2 us  [the longest x2 20.7 us: on_device(): jnp.einsum('ngts,tngd->snd', prob_rows.astype(BF16), d_attended, preferre...]
    all_gather x4 -> x0, blocking collectives: 112 us -> none  [the longest x2 70.3 us: on_device(): lax.all_gather(pieces[3], 'shard', axis=0, tiled=True)]
    ppermute x32 -> x0, starting transfers between devices: 106 us -> none  [shifted(): return lax.ppermute(block, axis, route)]
  transfers between devices with their start and end apart: 61 -> 4, of which waited for: 43 -> 0; matrix products, arithmetic and copies ran while one was open for 21% -> 23% of each run, Pallas kernels for 0% -> 62%
where the time goes in v1:
time: 1250 us
  Pallas kernels  893 us (71%)
  matrix products  128 us (10%)
  local copies, waits for them, and re-layouts  117 us (9%)
  other arithmetic  92.7 us (7%)
  between operations  15.6 us (1%)
    pallas_call x1, Pallas kernels, gather_dense(): pl.pallas_call(functools.partial(gather_dense_kernel, n, rows), out_shape...  175 us
    pallas_call x2, Pallas kernels, halo_back(): pl.pallas_call(functools.partial(halo_back_kernel, n, rows, cuts), out_sh...  155 us
    pallas_call x4, Pallas kernels, spread(): pl.pallas_call(functools.partial(spread_kernel, count), out_shape=jax.Sha...  118 us
    pallas_call x1, Pallas kernels, reduce_dense(): pl.pallas_call(functools.partial(reduce_dense_kernel, n, owners, rows), o...  115 us
    pallas_call x4, Pallas kernels, collect(): pl.pallas_call(functools.partial(collect_kernel, count), out_shape=jax.Sh...  111 us
    pallas_call x2, Pallas kernels, ffn_backward(): pl.pallas_call(functools.partial(ffn_backward_kernel, 256, width, in_rows...  88.3 us
    pallas_call x2, Pallas kernels, halo(): pl.pallas_call(functools.partial(halo_kernel, n, rows, cuts), out_shape=j...  83.1 us
    pallas_call x2, Pallas kernels, ffn_forward(): pl.pallas_call(functools.partial(ffn_forward_kernel, 256, width, in_rows,...  46.8 us
  transfers between devices with their start and end apart: 4, of which 0 were waited for; matrix products, arithmetic and copies ran while one was open for 23% of the time, Pallas kernels for 62%

profile of v1, /device:TPU:0, one launch (start us, length us, event | category | flops | bytes accessed | tf_op | source)
XLA Modules:
  0.0 1246.6 jit_solution(14563012176630036677)
XLA Ops:
  12.0 2.6 pad_maximum_fusion.4
  20.2 175.0 %gather_dense.1 = bf16[8,128,6272]{2,1,0:T(8,128)(2,1)} custom-call(bf16[128,6272]{1,0:T(8,128)(2,1)} %concatenate.57.x_ref), custom_call_target="tpu_custom_call" | custom-call | tf_op jit(solution)/shard_map/gather_dense/pallas_call | solution.py:246
  200.6 3.5 fusion.37
  206.0 25.8 %halo.2 = bf16[5,256,1024]{2,1,0:T(8,128)(2,1)} custom-call(bf16[256,1024]{1,0:T(8,128)(2,1)} %get-tuple-element.161.kv_ref), custom_call_target="tpu_custom_call" | custom-call | tf_op jit(solution)/shard_map/halo/pallas_call | solution.py:533
  237.8 4.7 fusion.127
  242.6 3.1 exponential_reduce_fusion.1
  245.7 3.9 copy-done.2
  249.6 5.5 fusion.63
  255.1 2.9 multiply_reduce_fusion.12
  261.4 29.9 %spread.4 = bf16[4,256,1152]{2,1,0:T(8,128)(2,1)} custom-call(bf16[256,1152]{1,0:T(8,128)(2,1)} %concatenate.58.x_ref), custom_call_target="tpu_custom_call" | custom-call | tf_op jit(solution)/shard_map/spread/pallas_call | solution.py:93
  291.4 23.4 %ffn_forward.2 = (bf16[1024,1024]{1,0:T(8,128)(2,1)}, bf16[4,1024,1024]{2,1,0:T(8,128)(2,1)}) custom-call(s32[1]{0:T(128)} %bitcast.26.first_ref, bf16[1024,1152]{1,0:T(8,128)(2,1)} %bitcast.269, bf16[8,4,192,1024]{3,2,1,0:T(8,128)(2,1)} %bitcast.321), custom_call_target="tpu_custom_call" | custom-call | flops 12884901888 | bytes 25690112 | tf_op jit(solution)/shard_map/ffn_forward/pallas_call | solution.py:709
  314.7 28.0 %collect.4 = f32[256,1024]{1,0:T(8,128)} custom-call(bf16[4,256,1024]{2,1,0:T(8,128)(2,1)} %bitcast.277), custom_call_target="tpu_custom_call" | custom-call | tf_op jit(solution)/shard_map/collect/pallas_call | solution.py:133
  344.3 3.9 fusion.40
  350.1 57.3 %halo.3 = bf16[5,256,1024]{2,1,0:T(8,128)(2,1)} custom-call(bf16[256,1024]{1,0:T(8,128)(2,1)} %get-tuple-element.159.kv_ref), custom_call_target="tpu_custom_call" | custom-call | tf_op jit(solution)/shard_map/halo/pallas_call | solution.py:533
  412.3 4.7 fusion.128
  417.0 3.1 exponential_reduce_fusion
  420.1 3.9 copy-done.3
  424.0 5.5 fusion.66
  429.5 2.9 multiply_reduce_fusion.10
  435.4 29.3 %spread.5 = bf16[4,256,1152]{2,1,0:T(8,128)(2,1)} custom-call(bf16[256,1152]{1,0:T(8,128)(2,1)} %concatenate.60.x_ref), custom_call_target="tpu_custom_call" | custom-call | tf_op jit(solution)/shard_map/spread/pallas_call | solution.py:93
  464.7 23.4 %ffn_forward.3 = (bf16[1024,1024]{1,0:T(8,128)(2,1)}, bf16[4,1024,1024]{2,1,0:T(8,128)(2,1)}) custom-call(s32[1]{0:T(128)} %bitcast.26.first_ref, bf16[1024,1152]{1,0:T(8,128)(2,1)} %bitcast.271, bf16[8,4,192,1024]{3,2,1,0:T(8,128)(2,1)} %bitcast.323), custom_call_target="tpu_custom_call" | custom-call | flops 12884901888 | bytes 25690112 | tf_op jit(solution)/shard_map/ffn_forward/pallas_call | solution.py:709
  488.1 27.7 %collect.5 = f32[256,1024]{1,0:T(8,128)} custom-call(bf16[4,256,1024]{2,1,0:T(8,128)(2,1)} %bitcast.278), custom_call_target="tpu_custom_call" | custom-call | tf_op jit(solution)/shard_map/collect/pallas_call | solution.py:133
  518.8 30.2 %spread.6 = bf16[4,256,1152]{2,1,0:T(8,128)(2,1)} custom-call(bf16[256,1152]{1,0:T(8,128)(2,1)} %concatenate.62.x_ref), custom_call_target="tpu_custom_call" | custom-call | tf_op jit(solution)/shard_map/spread/pallas_call | solution.py:93
  549.0 44.2 %ffn_backward.2 = (bf16[1024,1024]{1,0:T(8,128)(2,1)}, bf16[8,4,192,1024]{3,2,1,0:T(8,128)(2,1)}, f32[1024,128]{1,0:T(8,128)}) custom-call(s32[1]{0:T(128)} %bitcast.26.first_ref, bf16[1024,1152]{1,0:T(8,128)(2,1)} %bitcast.272, bf16[1024,1152]{1,0:T(8,128)(2,1)} %bitcast.273, bf16[4,1024,1024]{2,1,0:T(8,128)(2,1)} %get-tuple-element.38.gate_up_ref, ...), custom_call_target="tpu_custom_call" | custom-call | flops 25769803776 | bytes 42991616 | tf_op jit(solution)/shard_map/ffn_backward/pallas_call | solution.py:820
  595.2 27.7 %collect.6 = f32[256,1024]{1,0:T(8,128)} custom-call(bf16[4,256,1024]{2,1,0:T(8,128)(2,1)} %bitcast.276), custom_call_target="tpu_custom_call" | custom-call | tf_op jit(solution)/shard_map/collect/pallas_call | solution.py:133
  626.0 2.7 fusion.72
  629.0 10.3 fusion.34
  639.3 4.1 concatenate.65
  643.4 4.0 copy.299
  647.5 14.0 %fusion.3 = (f32[8,2,256]{2,1,0:T(2,128)S(1)}, f32[8,1280,256,2]{2,1,3,0:T(8,128)}) fusion(f32[8,2,256,1280]{2,3,1,0:T(8,128)} %copy-done.3, f32[8,2,256]{2,1,0:T(2,128)S(1)} %bitcast.289, bf16[1280,8,64,1]{0,2,3,1:T(8,128)(2,1)S(1)} %bitcast.252, bf16[256,8,2,64]{0,3,2,1:T(8,128)(2,1)S(1)} %bitcast.260), kind=kOutput, calls=%fused_computation.7 | convolution fusion | flops 686813184 | bytes 43810816 | tf_op jit(solution)/shard_map/tngd,snd->ngts/dot_general | solution.py:1036
  661.4 14.5 %fusion.5 = bf16[8,2,256,1280]{2,3,1,0:T(8,128)(2,1)S(1)} fusion(f32[8,1280,256,2]{2,1,3,0:T(8,128)} %get-tuple-element.195, f32[8,2,256,1280]{2,3,1,0:T(8,128)} %copy-done.3, f32[8,2,256]{2,1,0:T(2,128)S(1)} %get-tuple-element.194, f32[8,2,256]{2,1,0:T(2,128)S(1)} %bitcast.290), kind=kLoop, calls=%fused_computation.9 | loop fusion | flops 20971520 | bytes 52461568 | tf_op jit(solution)/shard_map/convert_element_type | solution.py:1039
  677.8 2.0 copy-done.4
  680.9 7.3 fusion.30
  688.2 2.4 concatenate.64
  690.6 4.2 copy.298
  694.8 3.2 pad_maximum_fusion.g_ref
  698.0 97.6 %halo_back.2 = f32[256,1024]{1,0:T(8,128)} custom-call(bf16[5,256,1024]{2,1,0:T(8,128)(2,1)} %pad_maximum_fusion.g_ref), custom_call_target="tpu_custom_call" | custom-call | tf_op jit(solution)/shard_map/halo_back/pallas_call | solution.py:650
  796.9 3.9 multiply_reduce_fusion.1
  803.1 29.0 %spread.7 = bf16[4,256,1152]{2,1,0:T(8,128)(2,1)} custom-call(bf16[256,1152]{1,0:T(8,128)(2,1)} %concatenate.68.x_ref), custom_call_target="tpu_custom_call" | custom-call | tf_op jit(solution)/shard_map/spread/pallas_call | solution.py:93
  832.1 44.1 %ffn_backward.3 = (bf16[1024,1024]{1,0:T(8,128)(2,1)}, bf16[8,4,192,1024]{3,2,1,0:T(8,128)(2,1)}, f32[1024,128]{1,0:T(8,128)}) custom-call(s32[1]{0:T(128)} %bitcast.26.first_ref, bf16[1024,1152]{1,0:T(8,128)(2,1)} %bitcast.270, bf16[1024,1152]{1,0:T(8,128)(2,1)} %bitcast.274, bf16[4,1024,1024]{2,1,0:T(8,128)(2,1)} %get-tuple-element.40.gate_up_ref, ...), custom_call_target="tpu_custom_call" | custom-call | flops 25769803776 | bytes 42991616 | tf_op jit(solution)/shard_map/ffn_backward/pallas_call | solution.py:820
  879.2 28.0 %collect.7 = f32[256,1024]{1,0:T(8,128)} custom-call(bf16[4,256,1024]{2,1,0:T(8,128)(2,1)} %bitcast.275), custom_call_target="tpu_custom_call" | custom-call | tf_op jit(solution)/shard_map/collect/pallas_call | solution.py:133
  913.4 2.3 fusion.69
  915.9 10.4 fusion.31
  926.4 4.1 concatenate.71
  930.5 4.1 copy.309
  934.6 13.7 %fusion = (f32[8,2,256]{2,1,0:T(2,128)S(1)}, f32[8,1280,256,2]{2,1,3,0:T(8,128)}) fusion(f32[8,2,256,1280]{2,3,1,0:T(8,128)} %copy-done.2, f32[8,2,256]{2,1,0:T(2,128)S(1)} %bitcast.285, bf16[1280,8,64,1]{0,2,3,1:T(8,128)(2,1)S(1)} %bitcast.250, bf16[256,8,2,64]{0,3,2,1:T(8,128)(2,1)S(1)} %bitcast.262), kind=kOutput, calls=%fused_computation.2 | convolution fusion | flops 686813184 | bytes 43810816 | tf_op jit(solution)/shard_map/tngd,snd->ngts/dot_general | solution.py:1036
  948.3 15.0 %fusion.2 = bf16[8,2,256,1280]{2,3,1,0:T(8,128)(2,1)S(1)} fusion(f32[8,1280,256,2]{2,1,3,0:T(8,128)} %get-tuple-element.198, f32[8,2,256,1280]{2,3,1,0:T(8,128)} %copy-done.2, f32[8,2,256]{2,1,0:T(2,128)S(1)} %get-tuple-element.197, f32[8,2,256]{2,1,0:T(2,128)S(1)} %bitcast.286), kind=kLoop, calls=%fused_computation.4 | loop fusion | flops 20971520 | bytes 52461568 | tf_op jit(solution)/shard_map/convert_element_type | solution.py:1039
  965.2 2.1 copy-done.5
  968.3 7.3 fusion.29
  975.6 2.4 concatenate.70
  978.0 4.2 copy.308
  982.2 3.2 pad_maximum_fusion.1.g_ref
  985.4 57.3 %halo_back.3 = f32[256,1024]{1,0:T(8,128)} custom-call(bf16[5,256,1024]{2,1,0:T(8,128)(2,1)} %pad_maximum_fusion.1.g_ref), custom_call_target="tpu_custom_call" | custom-call | tf_op jit(solution)/shard_map/halo_back/pallas_call | solution.py:650
  1044.1 4.7 multiply_reduce_fusion.3
  1052.0 2.0 convolution_convert_fusion.3
  1054.1 3.4 convolution_convert_fusion
  1057.5 3.4 convolution_convert_fusion.1
  1060.9 22.1 %concatenate.74 = bf16[1024,6272]{1,0:T(8,128)(2,1)} concatenate(bf16[1024,2048]{1,0:T(8,128)(2,1)} %convolution_convert_fusion.1, bf16[1024,1024]{1,0:T(8,128)(2,1)} %convolution_convert_fusion.3, bf16[1024,2048]{1,0:T(8,128)(2,1)} %convolution_convert_fusion, bf16[1024,1024]{1,0:T(8,128)(2,1)} %convolution_convert_fusion.2, bf16[1024,16]{1,0:T(8,128)(2,1)} %get-tuple-element.181, ...), dimensions={1} | concatenate | bytes 25690112 | tf_op jit(solution)/shard_map/concatenate | solution.py:1078
  1083.0 115.5 %reduce_dense.1 = bf16[128,6272]{1,0:T(8,128)(2,1)} custom-call(bf16[8,128,6272]{2,1,0:T(8,128)(2,1)} %bitcast.232), custom_call_target="tpu_custom_call" | custom-call | tf_op jit(solution)/shard_map/reduce_dense/pallas_call | solution.py:387
  1205.9 2.6 fusion.78
  1208.6 2.5 add_multiply_fusion.3
  1214.4 4.0 add_multiply_fusion.2
  1224.3 6.6 add_multiply_fusion.1
  1232.5 7.4 add_multiply_fusion
  (326 shorter events, 87.4 us)
Async XLA Ops:
  7.2 7.4 copy-start
  7.2 284.1 %all-gather.5.cloned.1.call-start = ((), (), s32[]{:S(2)}) async-start(), calls=%async_computation.4 | async-start | bytes 14155776 | tf_op jit(solution)/shard_map/all_gather | solution.py:939
  11.9 4.5 copy-start.86
  11.9 4.6 copy-start.73
  11.9 452.8 %all-gather.7.cloned.1.call-start = ((), (), s32[]{:S(2)}) async-start(), calls=%async_computation.5 | async-start | bytes 14155776 | tf_op jit(solution)/shard_map/all_gather | solution.py:939
  12.0 5.9 copy-start.32
  14.6 1203.8 %reduce-scatter.5.cloned.1.call-start = ((), (), s32[]{:S(2)}) async-start(), calls=%async_computation.3 | async-start | bytes 14155776 | tf_op jit(solution)/shard_map/reduce_scatter | solution.py:1021
  195.2 4.6 copy-start.8
  200.6 57.9 %copy-start.71 = (f32[1,1024]{1,0:T(1,128)}, f32[1,1024]{1,0:T(1,128)S(1)}, u32[]{:S(2)}) copy-start(f32[1,1024]{1,0:T(1,128)S(1)} %get-tuple-element.178) | copy-start | bytes 12292
  237.8 4.7 copy-start.34
  242.6 7.0 copy-start.2
  245.7 9.4 copy-start.63
  255.1 4.9 copy-start.66
  257.9 84.8 %copy-start.6 = (f32[256,1024]{1,0:T(8,128)}, f32[256,1024]{1,0:T(8,128)S(1)}, u32[]{:S(2)}) copy-start(f32[256,1024]{1,0:T(8,128)S(1)} %get-tuple-element.185) | copy-start | bytes 3145732
  258.0 33.3 %copy-start.80 = (f32[256]{0:T(256)}, f32[256]{0:T(256)S(1)}, u32[]{:S(2)}) copy-start(f32[256]{0:T(256)S(1)} %fusion.99) | copy-start | bytes 3076
  260.4 54.4 %copy-start.61 = (bf16[256,96]{1,0:T(8,128)(2,1)}, bf16[256,96]{1,0:T(8,128)(2,1)S(1)}, u32[]{:S(2)}) copy-start(bf16[256,96]{1,0:T(8,128)(2,1)S(1)} %broadcast.331) | copy-start | bytes 147460
  344.2 3.9 copy-start.10
  417.0 7.0 copy-start.3
  429.5 4.5 copy-start.65
  488.1 27.7 %copy-start.41 = (f32[256,1024]{1,0:T(8,128)S(1)}, f32[256,1024]{1,0:T(8,128)}, u32[]{:S(2)}) copy-start(f32[256,1024]{1,0:T(8,128)} %param.23) | copy-start | bytes 3145732
  593.2 628.5 %reduce-scatter.3.cloned.1.call-start = ((), (), s32[]{:S(2)}) async-start(), calls=%async_computation.2 | async-start | bytes 14155776 | tf_op jit(solution)/shard_map/reduce_scatter | solution.py:1021
  595.2 29.4 %copy-start.24 = (f32[256,1024]{1,0:T(8,128)S(1)}, f32[256,1024]{1,0:T(8,128)}, u32[]{:S(2)}) copy-start(f32[256,1024]{1,0:T(8,128)} %collect.5) | copy-start | bytes 3145732
  626.0 174.8 %copy-start.27 = (f32[256,1024]{1,0:T(8,128)}, f32[256,1024]{1,0:T(8,128)S(1)}, u32[]{:S(2)}) copy-start(f32[256,1024]{1,0:T(8,128)S(1)} %get-tuple-element.152) | copy-start | bytes 3145732
  639.3 8.2 copy-start.19
  661.4 14.5 %copy-start.13 = (bf16[1280,512]{0,1:T(8,128)(2,1)S(1)}, bf16[1280,512]{0,1:T(8,128)(2,1)}, u32[]{:S(2)}) copy-start(bf16[1280,512]{0,1:T(8,128)(2,1)} %copy.284) | copy-start | bytes 3932164
  675.9 3.9 copy-start.4
  675.9 4.9 copy-start.21
  690.6 4.2 copy-start.35
  697.9 98.9 %copy-start.11 = (f32[256,1024]{1,0:T(8,128)S(1)}, f32[256,1024]{1,0:T(8,128)}, u32[]{:S(2)}) copy-start(f32[256,1024]{1,0:T(8,128)} %copy-done.10) | copy-start | bytes 3145732
  697.9 98.9 %copy-start.47 = (bf16[256,1024]{1,0:T(8,128)(2,1)S(1)}, bf16[256,1024]{1,0:T(8,128)(2,1)}, u32[]{:S(2)}) copy-start(bf16[256,1024]{1,0:T(8,128)(2,1)} %copy.300) | copy-start | bytes 1572868
  796.9 3.9 copy-start.45
  796.9 4.0 copy-start.29
  801.3 30.8 %copy-start.30 = (f32[256,1024]{1,0:T(8,128)}, f32[256,1024]{1,0:T(8,128)S(1)}, u32[]{:S(2)}) copy-start(f32[256,1024]{1,0:T(8,128)S(1)} %get-tuple-element.131) | copy-start | bytes 3145732
  876.2 31.0 %copy-start.7 = (f32[256,1024]{1,0:T(8,128)S(1)}, f32[256,1024]{1,0:T(8,128)}, u32[]{:S(2)}) copy-start(f32[256,1024]{1,0:T(8,128)} %copy-done.6) | copy-start | bytes 3145732
  876.2 31.0 %copy-start.72 = (f32[1,1024]{1,0:T(1,128)S(1)}, f32[1,1024]{1,0:T(1,128)}, u32[]{:S(2)}) copy-start(f32[1,1024]{1,0:T(1,128)} %copy-done.71) | copy-start | bytes 12292
  876.2 31.0 %copy-start.81 = (f32[256]{0:T(256)S(1)}, f32[256]{0:T(256)}, u32[]{:S(2)}) copy-start(f32[256]{0:T(256)} %copy-done.80) | copy-start | bytes 3076
  879.2 30.6 %copy-start.70 = (f32[1024,128]{1,0:T(8,128)S(1)}, f32[1024,128]{1,0:T(8,128)}, u32[]{:S(2)}) copy-start(f32[1024,128]{1,0:T(8,128)} %get-tuple-element.42) | copy-start | bytes 1572868
  879.2 31.6 %copy-start.85 = (f32[256]{0:T(256)S(1)}, f32[256]{0:T(256)}, u32[]{:S(2)}) copy-start(f32[256]{0:T(256)} %copy-done.84) | copy-start | bytes 3076
  926.4 8.2 copy-start.18
  948.3 15.0 %copy-start.12 = (bf16[1280,512]{0,1:T(8,128)(2,1)S(1)}, bf16[1280,512]{0,1:T(8,128)(2,1)}, u32[]{:S(2)}) copy-start(bf16[1280,512]{0,1:T(8,128)(2,1)} %copy.276) | copy-start | bytes 3932164
  963.3 4.0 copy-start.5
  963.3 5.0 copy-start.20
  978.0 4.2 copy-start.36
  985.4 58.6 %copy-start.9 = (f32[256,1024]{1,0:T(8,128)S(1)}, f32[256,1024]{1,0:T(8,128)}, u32[]{:S(2)}) copy-start(f32[256,1024]{1,0:T(8,128)} %param.22) | copy-start | bytes 3145732
  985.4 58.6 %copy-start.49 = (bf16[256,1024]{1,0:T(8,128)(2,1)S(1)}, bf16[256,1024]{1,0:T(8,128)(2,1)}, u32[]{:S(2)}) copy-start(bf16[256,1024]{1,0:T(8,128)(2,1)} %copy.310) | copy-start | bytes 1572868
  985.4 58.6 %copy-start.68 = (f32[1,1024]{1,0:T(1,128)S(1)}, f32[1,1024]{1,0:T(1,128)}, u32[]{:S(2)}) copy-start(f32[1,1024]{1,0:T(1,128)} %copy-done.67) | copy-start | bytes 12292
  985.4 58.6 %copy-start.76 = (f32[256]{0:T(256)S(1)}, f32[256]{0:T(256)}, u32[]{:S(2)}) copy-start(f32[256]{0:T(256)} %copy-done.75) | copy-start | bytes 3076
  1044.1 5.0 copy-start.54
  1044.1 5.0 copy-start.55
  1044.1 5.9 copy-start.28
  1044.1 5.9 copy-start.38
  1198.5 4.8 copy-start.83
  1198.5 4.8 copy-start.87
  1198.5 4.8 copy-start.88
  1198.5 4.8 copy-start.89
  1198.5 5.4 copy-start.74
  1198.5 5.4 copy-start.78
  1198.6 5.4 copy-start.79
  1208.6 4.1 copy-start.52
  1220.2 4.0 copy-start.31
  1224.3 6.7 copy-start.15
  1224.3 6.7 copy-start.39
  1224.3 8.2 copy-start.40
  1232.5 7.4 copy-start.1
  (30 other events, 71.9 us)
Sparse Core Ops, SparseCore 0:
  12.0 240.9 all-gather.4
  255.8 188.3 all-gather.6
  593.3 281.7 reduce-scatter.4
  878.6 238.7 reduce-scatter.2

commit v2 on v1

--- a/solution.py
+++ b/solution.py
@@ -59,45 +59,76 @@
     return [gradient, new_first, new_second, weight_step]
 
 
-def greet(axis, count):
-    me = lax.axis_index(axis)
+def signal(barrier, where):
+    pl.semaphore_signal(barrier, inc=1, device_id=where, device_id_type=MESH)
+
+
+def greet_chips(owners):
+    e = lax.axis_index("expert")
+    partner = e + 1 - 2 * lax.rem(e, 2)
     barrier = pltpu.get_barrier_semaphore()
-    for d in range(1, count):
-        pl.semaphore_signal(
-            barrier, inc=1, device_id={axis: lax.rem(me + d, count)}, device_id_type=MESH
-        )
-    pl.semaphore_wait(barrier, count - 1)
-    return me
-
-
-def spread_kernel(count, x_ref, o_ref, send_sem, recv_sem):
-    me = greet("expert", count)
-    copies = []
-    for d in range(1, count):
-        copy = pltpu.make_async_remote_copy(
-            src_ref=x_ref,
-            dst_ref=o_ref.at[me],
-            send_sem=send_sem.at[d - 1],
-            recv_sem=recv_sem.at[d - 1],
-            device_id={"expert": lax.rem(me + d, count)},
+    signal(barrier, {"expert": partner})
+    for d in range(1, owners // 2):
+        signal(barrier, {"expert": lax.rem(e + 2 * d, owners)})
+    pl.semaphore_wait(barrier, owners // 2)
+    return e, partner
+
+
+def spread_kernel(owners, cuts, x_ref, o_ref, pair_send, pair_recv, far_send, far_recv):
+    e, partner = greet_chips(owners)
+    chips = owners // 2
+    size = x_ref.shape[0] // cuts
+
+    def pair_copy(d, cut):
+        rows = pl.ds(cut * size, size)
+        there = o_ref.at[lax.rem(e + owners - 2 * d, owners), rows]
+        return pltpu.make_async_remote_copy(
+            src_ref=x_ref.at[rows] if d == 0 else there,
+            dst_ref=there,
+            send_sem=pair_send.at[d, cut],
+            recv_sem=pair_recv.at[d, cut],
+            device_id={"expert": partner},
             device_id_type=MESH,
         )
-        copy.start()
-        copies.append(copy)
-    o_ref[me] = x_ref[...]
-    for copy in copies:
-        copy.wait()
-
-
-def spread(rows, count):
+
+    def far_copy(d, cut):
+        rows = pl.ds(cut * size, size)
+        return pltpu.make_async_remote_copy(
+            src_ref=x_ref.at[rows],
+            dst_ref=o_ref.at[e, rows],
+            send_sem=far_send.at[d - 1, cut],
+            recv_sem=far_recv.at[d - 1, cut],
+            device_id={"expert": lax.rem(e + 2 * d, owners)},
+            device_id_type=MESH,
+        )
+
+    for cut in range(cuts):
+        for d in range(1, chips):
+            far_copy(d, cut).start()
+    for cut in range(cuts):
+        pair_copy(0, cut).start()
+    o_ref[e] = x_ref[...]
+    for cut in range(cuts):
+        for d in range(1, chips):
+            far_copy(d, cut).wait_recv()
+            pair_copy(d, cut).start()
+    for cut in range(cuts):
+        for d in range(chips):
+            pair_copy(d, cut).wait()
+        for d in range(1, chips):
+            far_copy(d, cut).wait_send()
+
+
+def spread(rows, owners):
+    dma = pltpu.SemaphoreType.DMA
+    chips, cuts = owners // 2, 4
     return pl.pallas_call(
-        functools.partial(spread_kernel, count),
-        out_shape=jax.ShapeDtypeStruct((count,) + rows.shape, rows.dtype),
+        functools.partial(spread_kernel, owners, cuts),
+        out_shape=jax.ShapeDtypeStruct((owners,) + rows.shape, rows.dtype),
         in_specs=[pl.BlockSpec(memory_space=pltpu.VMEM)],
         out_specs=pl.BlockSpec(memory_space=pltpu.VMEM),
         scratch_shapes=[
-            pltpu.SemaphoreType.DMA((count - 1,)),
-            pltpu.SemaphoreType.DMA((count - 1,)),
+            dma((chips, cuts)), dma((chips, cuts)), dma((chips - 1, cuts)), dma((chips - 1, cuts)),
         ],
         compiler_params=pltpu.CompilerParams(
             collective_id=1, has_side_effects=True, vmem_limit_bytes=VMEM_LIMIT
@@ -106,39 +137,78 @@
     )(rows)
 
 
-def collect_kernel(count, p_ref, o_ref, held, send_sem, recv_sem):
-    me = greet("expert", count)
-    copies = []
-    for d in range(1, count):
-        peer = lax.rem(me + d, count)
-        copy = pltpu.make_async_remote_copy(
-            src_ref=p_ref.at[peer],
-            dst_ref=held.at[d - 1],
-            send_sem=send_sem.at[d - 1],
-            recv_sem=recv_sem.at[d - 1],
-            device_id={"expert": peer},
+def collect_kernel(
+    owners, cuts, p_ref, o_ref, paired, going, came, pair_send, pair_recv, far_send, far_recv
+):
+    e, partner = greet_chips(owners)
+    chips = owners // 2
+    size = o_ref.shape[0] // cuts
+
+    def pair_copy(d, cut):
+        rows = pl.ds(cut * size, size)
+        return pltpu.make_async_remote_copy(
+            src_ref=p_ref.at[lax.rem(partner + 2 * d, owners), rows],
+            dst_ref=paired.at[d, rows],
+            send_sem=pair_send.at[d, cut],
+            recv_sem=pair_recv.at[d, cut],
+            device_id={"expert": partner},
             device_id_type=MESH,
         )
-        copy.start()
-        copies.append(copy)
-    total = p_ref[me].astype(F32)
-    for d, copy in enumerate(copies):
-        copy.wait()
-        total = total + held[d].astype(F32)
-    o_ref[...] = total
+
+    def far_copy(d, cut):
+        rows = pl.ds(cut * size, size)
+        return pltpu.make_async_remote_copy(
+            src_ref=going.at[d - 1, rows],
+            dst_ref=came.at[d - 1, rows],
+            send_sem=far_send.at[d - 1, cut],
+            recv_sem=far_recv.at[d - 1, cut],
+            device_id={"expert": lax.rem(e + 2 * d, owners)},
+            device_id_type=MESH,
+        )
+
+    for cut in range(cuts):
+        for d in range(1, chips):
+            pair_copy(d, cut).start()
+    for cut in range(cuts):
+        pair_copy(0, cut).start()
+    for cut in range(cuts):
+        rows = pl.ds(cut * size, size)
+        for d in range(1, chips):
+            pair_copy(d, cut).wait_recv()
+            going[d - 1, rows, :] = (
+                p_ref[lax.rem(e + 2 * d, owners), rows, :].astype(F32)
+                + paired[d, rows, :].astype(F32)
+            ).astype(BF16)
+            far_copy(d, cut).start()
+    for cut in range(cuts):
+        rows = pl.ds(cut * size, size)
+        pair_copy(0, cut).wait_recv()
+        total = p_ref[e, rows, :].astype(F32) + paired[0, rows, :].astype(F32)
+        for d in range(1, chips):
+            far_copy(d, cut).wait_recv()
+            total = total + came[d - 1, rows, :].astype(F32)
+        o_ref[rows, :] = total
+    for cut in range(cuts):
+        for d in range(chips):
+            pair_copy(d, cut).wait_send()
+        for d in range(1, chips):
+            far_copy(d, cut).wait_send()
 
 
 def collect(parts):
-    count, rows, width = parts.shape
+    owners, rows, width = parts.shape
+    dma = pltpu.SemaphoreType.DMA
+    chips, cuts = owners // 2, 4
     return pl.pallas_call(
-        functools.partial(collect_kernel, count),
+        functools.partial(collect_kernel, owners, cuts),
         out_shape=jax.ShapeDtypeStruct((rows, width), F32),
         in_specs=[pl.BlockSpec(memory_space=pltpu.VMEM)],
         out_specs=pl.BlockSpec(memory_space=pltpu.VMEM),
         scratch_shapes=[
-            pltpu.VMEM((count - 1, rows, width), parts.dtype),
-            pltpu.SemaphoreType.DMA((count - 1,)),
-            pltpu.SemaphoreType.DMA((count - 1,)),
+            pltpu.VMEM((chips, rows, width), parts.dtype),
+            pltpu.VMEM((chips - 1, rows, width), parts.dtype),
+            pltpu.VMEM((chips - 1, rows, width), parts.dtype),
+            dma((chips, cuts)), dma((chips, cuts)), dma((chips - 1, cuts)), dma((chips - 1, cuts)),
         ],
         compiler_params=pltpu.CompilerParams(
             collective_id=2, has_side_effects=True, vmem_limit_bytes=VMEM_LIMIT
@@ -155,10 +225,6 @@
 def ring_place(shard, count):
     odd, pair = lax.rem(shard, 2), lax.div(shard, 2)
     return (1 - odd) * pair + odd * (count - 1 - pair)
-
-
-def signal(barrier, where):
-    pl.semaphore_signal(barrier, inc=1, device_id=where, device_id_type=MESH)
 
 
 def gather_dense_kernel(
@@ -259,9 +325,13 @@
 
 
 def reduce_dense_kernel(
-    n, owners, rows, g_ref, o_ref, paired, came, going, crossed, last_in,
-    pair_send, pair_recv, ring_send, ring_recv, cross_send, cross_recv, last_send, last_recv,
+    n, owners, rows, places, *refs,
 ):
+    g_refs = refs[: len(places)]
+    (
+        o_ref, paired, came, going, crossed, last_in, pair_send, pair_recv, ring_send,
+        ring_recv, cross_send, cross_recv, last_send, last_recv,
+    ) = refs[len(places) :]
     e, s = lax.axis_index("expert"), lax.axis_index("shard")
     core, x = lax.rem(e, 2), lax.div(e, 2)
     partner = e + 1 - 2 * core
@@ -283,13 +353,14 @@
     def block(way, k):
         return ring_shard(lax.rem(p + (2 * n - 1 - k if way == 0 else k + 1), n), n)
 
-    def pair_copy(k):
+    def pair_copy(k, i):
         b = block(0, k)
+        at, wide = places[i]
         return pltpu.make_async_remote_copy(
-            src_ref=g_ref.at[b, pl.ds(pl.multiple_of((1 - core) * half, half), half)],
-            dst_ref=paired.at[b],
-            send_sem=pair_send.at[b],
-            recv_sem=pair_recv.at[b],
+            src_ref=g_refs[i].at[b, pl.ds(pl.multiple_of((1 - core) * half, half), half)],
+            dst_ref=paired.at[b, :, pl.ds(at, wide)],
+            send_sem=pair_send.at[i, b],
+            recv_sem=pair_recv.at[i, b],
             device_id={"expert": partner},
             device_id_type=MESH,
         )
@@ -304,10 +375,14 @@
             device_id_type=MESH,
         )
 
-    def own(way, b):
-        return g_ref[b, mine(way), :].astype(F32) + paired[
-            b, way * quarter : (way + 1) * quarter, :
-        ].astype(F32)
+    def put(target, way, b, more=None):
+        for g_ref, (at, wide) in zip(g_refs, places):
+            total = g_ref[b, mine(way), :].astype(F32) + paired[
+                b, way * quarter : (way + 1) * quarter, at : at + wide
+            ].astype(F32)
+            if more is not None:
+                total = total + more[:, at : at + wide].astype(F32)
+            target[:, at : at + wide] = total.astype(BF16)
 
     order = []
     for k in range(n):
@@ -315,29 +390,33 @@
             place = place % n
             if place not in order:
                 order.append(place)
+    every = range(len(places))
     for k in order:
-        pair_copy(k).start()
-    for k in order:
-        pair_copy(k).wait_recv()
+        for i in every:
+            pair_copy(k, i).start()
+    for k in order[:2]:
+        for i in every:
+            pair_copy(k, i).wait_recv()
     for way in range(2):
-        going[way, 0] = own(way, block(way, 0)).astype(BF16)
+        put(going.at[way, 0], way, block(way, 0))
         ring_copy(way, 0).start()
+    for k in order[2:]:
+        for i in every:
+            pair_copy(k, i).wait_recv()
 
     def step(k, carry):
         for way in range(2):
             ring_copy(way, k - 1).wait_recv()
-            going[way, k] = (
-                came[way, k - 1].astype(F32) + own(way, block(way, k))
-            ).astype(BF16)
+            put(going.at[way, k], way, block(way, k), came.at[way, k - 1])
             ring_copy(way, k).start()
         return carry
 
     lax.fori_loop(1, n - 1, step, 0)
     for way in range(2):
         ring_copy(way, n - 2).wait_recv()
-        crossed[x, way * quarter : (way + 1) * quarter, :] = (
-            came[way, n - 2].astype(F32) + own(way, s)
-        ).astype(BF16)
+        put(
+            crossed.at[x, pl.ds(way * quarter, quarter)], way, s, came.at[way, n - 2]
+        )
 
     def cross_copy(d):
         return pltpu.make_async_remote_copy(
@@ -368,7 +447,8 @@
     )
     last.start()
     for k in order:
-        pair_copy(k).wait_send()
+        for i in every:
+            pair_copy(k, i).wait_send()
 
     def finish(k, carry):
         for way in range(2):
@@ -381,13 +461,17 @@
 
 
 def reduce_dense(grads, n, owners):
-    rows, columns = grads.shape[1:]
+    rows = grads[0].shape[1]
+    places, columns = [], 0
+    for grad in grads:
+        places.append((columns, grad.shape[2]))
+        columns += grad.shape[2]
     dma = pltpu.SemaphoreType.DMA
     across = owners // 2
     return pl.pallas_call(
-        functools.partial(reduce_dense_kernel, n, owners, rows),
+        functools.partial(reduce_dense_kernel, n, owners, rows, tuple(places)),
         out_shape=jax.ShapeDtypeStruct((rows, columns), BF16),
-        in_specs=[pl.BlockSpec(memory_space=pltpu.VMEM)],
+        in_specs=[pl.BlockSpec(memory_space=pltpu.VMEM)] * len(places),
         out_specs=pl.BlockSpec(memory_space=pltpu.VMEM),
         scratch_shapes=[
             pltpu.VMEM((n, rows // 2, columns), BF16),
@@ -395,14 +479,14 @@
             pltpu.VMEM((2, n - 1, rows // 4, columns), BF16),
             pltpu.VMEM((across, rows // 2, columns), BF16),
             pltpu.VMEM((rows // 2, columns), BF16),
-            dma((n,)), dma((n,)), dma((2, n - 1)), dma((2, n - 1)),
+            dma((len(places), n)), dma((len(places), n)), dma((2, n - 1)), dma((2, n - 1)),
             dma((across - 1,)), dma((across - 1,)), dma, dma,
         ],
         compiler_params=pltpu.CompilerParams(
             collective_id=4, has_side_effects=True, vmem_limit_bytes=VMEM_LIMIT
         ),
         name="reduce_dense",
-    )(grads)
+    )(*grads)
 
 
 def halo_links(n, s):
@@ -917,15 +1001,18 @@
     expert_ids = jnp.arange(experts_total, dtype=jnp.int32)
     side = 128
 
-    def dense_piece():
+    def dense_piece(layer_no):
         rows = w_qkv.shape[1]
-        parts = []
-        for layer_no in range(LAYERS):
-            parts += [w_qkv[layer_no].astype(BF16), w_out[layer_no].astype(BF16)]
-        for layer_no in range(LAYERS):
-            parts += [router[layer_no].astype(BF16), gains[layer_no].T.astype(BF16)]
-        parts.append(jnp.zeros((rows, side - LAYERS * (experts_total + 2)), BF16))
-        return jnp.concatenate(parts, 1)
+        return jnp.concatenate(
+            [
+                w_qkv[layer_no].astype(BF16),
+                w_out[layer_no].astype(BF16),
+                router[layer_no].astype(BF16),
+                gains[layer_no].T.astype(BF16),
+                jnp.zeros((rows, side - experts_total - 2), BF16),
+            ],
+            1,
+        )
 
     def expert_piece(layer_no):
         return jnp.concatenate(
@@ -933,19 +1020,19 @@
         )
 
     layer_columns = qkv_width + width
-    dense = gather_dense(dense_piece(), shards).reshape(width, -1)
+    dense = gather_dense(dense_piece(0), shards)
     expert_full = []
     for layer_no in range(LAYERS):
-        expert_full.append(lax.all_gather(expert_piece(layer_no), "shard", axis=0, tiled=False))
+        piece, dense = lax.optimization_barrier((expert_piece(layer_no), dense))
+        expert_full.append(lax.all_gather(piece, "shard", axis=0, tiled=False))
 
     kept_layers = []
     stream = hidden_in
     for layer_no in range(LAYERS):
-        at = layer_no * layer_columns
-        w_qkv_full = dense[:, at : at + qkv_width]
-        w_out_full = dense[:, at + qkv_width : at + layer_columns]
-        at = LAYERS * layer_columns + layer_no * (experts_total + 2)
-        small = dense[:, at : at + experts_total + 2]
+        dense = dense.reshape(width, -1)
+        w_qkv_full = dense[:, :qkv_width]
+        w_out_full = dense[:, qkv_width:layer_columns]
+        small = dense[:, layer_columns:]
         router_full = small[:, :experts_total]
         gain_pair = small[:, experts_total : experts_total + 2].astype(F32).T
         normed_one = rms_scale(stream, gain_pair[0]).astype(BF16)
@@ -980,6 +1067,10 @@
             [normed_two, high, low, jnp.zeros((tok_rows, extra - 2 * experts_total), BF16)], 1
         )
         x_all = spread(wide_rows, owners).reshape(owners * tok_rows, width + extra)
+        if layer_no + 1 < LAYERS:
+            piece, x_all = lax.optimization_barrier((dense_piece(layer_no + 1), x_all))
+            dense = gather_dense(piece, shards)
+            dense, x_all = lax.optimization_barrier((dense, x_all))
         partial, gate_up = ffn_forward(
             first_array, x_all, expert_full[layer_no], experts_total, in_rows
         )
@@ -1073,9 +1164,10 @@
             d_experts[:, :in_rows, :].astype(F32),
             d_experts[:, in_rows:, :].astype(F32),
         )
-    parts = sum(dense_parts, []) + sum(small_parts, [])
-    parts.append(jnp.zeros((width, side - LAYERS * (experts_total + 2)), BF16))
-    d_dense = jnp.concatenate(parts, 1).reshape(shards, width // shards, -1)
+    small = sum(small_parts, [])
+    small.append(jnp.zeros((width, side - LAYERS * (experts_total + 2)), BF16))
+    parts = sum(dense_parts, []) + [jnp.concatenate(small, 1)]
+    d_dense = [part.reshape(shards, width // shards, -1) for part in parts]
     d_dense = reduce_dense(d_dense, shards, owners).astype(F32)
     for layer_no in range(LAYERS):
         at = layer_no * layer_columns

time: 1250 us -> 1190 us (0.952)
  Pallas kernels: 893 us -> 775 us
  waiting for transfers between devices: 0.13 us -> 72.4 us
    all_gather x2, waiting for transfers between devices: 0.04 us -> 71.6 us  [on_device(): expert_full.append(lax.all_gather(piece, 'shard', axis=0, tiled=False))]
    pallas_call x2, Pallas kernels: 155 us -> 94.7 us  [halo_back(): pl.pallas_call(functools.partial(halo_back_kernel, n, rows, cuts), out_sh...]
    pallas_call x9, Pallas kernels: 345 us -> 301 us  [the longest x1 153 us: reduce_dense(): pl.pallas_call(functools.partial(reduce_dense_kernel, n, owners, rows, tu...]
    pallas_call x2, Pallas kernels: 83.1 us -> 51.1 us  [halo(): pl.pallas_call(functools.partial(halo_kernel, n, rows, cuts), out_shape=j...]
    concatenate x2 -> x3, local copies, waits for them, and re-layouts: 24 us -> 5.59 us  [the longest x2 2.99 us: dense_piece(): jnp.concatenate([w_qkv[layer_no].astype(BF16), w_out[layer_no].astype(BF1...]
    pallas_call x1 -> x2, Pallas kernels: 175 us -> 192 us  [gather_dense(): pl.pallas_call(functools.partial(gather_dense_kernel, n, rows), out_shape...]
    unnamed x187 -> x192, local copies, waits for them, and re-layouts: 24.5 us -> 27.8 us
  transfers between devices with their start and end apart: 4 -> 4, of which waited for: 0 -> 1; matrix products, arithmetic and copies ran while one was open for 23% -> 23% of each run, Pallas kernels for 62% -> 52%
where the time goes in v2:
time: 1190 us
  Pallas kernels  775 us (65%)
  matrix products  129 us (11%)
  local copies, waits for them, and re-layouts  106 us (9%)
  other arithmetic  90.5 us (8%)
  waiting for transfers between devices  72.4 us (6%)
  between operations  15.6 us (1%)
    pallas_call x2, Pallas kernels, gather_dense(): pl.pallas_call(functools.partial(gather_dense_kernel, n, rows), out_shape...  192 us
    pallas_call x1, Pallas kernels, reduce_dense(): pl.pallas_call(functools.partial(reduce_dense_kernel, n, owners, rows, tu...  153 us
    pallas_call x2, Pallas kernels, halo_back(): pl.pallas_call(functools.partial(halo_back_kernel, n, rows, cuts), out_sh...  94.7 us
    pallas_call x2, Pallas kernels, ffn_backward(): pl.pallas_call(functools.partial(ffn_backward_kernel, 256, width, in_rows...  88.4 us
    pallas_call x4, Pallas kernels, spread(): pl.pallas_call(functools.partial(spread_kernel, owners, cuts), out_shape=...  74.1 us
    pallas_call x4, Pallas kernels, collect(): pl.pallas_call(functools.partial(collect_kernel, owners, cuts), out_shape...  73.9 us
    all_gather x2, waiting for transfers between devices, on_device(): expert_full.append(lax.all_gather(piece, 'shard', axis=0, tiled=False))  71.6 us
    pallas_call x2, Pallas kernels, halo(): pl.pallas_call(functools.partial(halo_kernel, n, rows, cuts), out_shape=j...  51.1 us
  transfers between devices with their start and end apart: 4, of which 1 were waited for; matrix products, arithmetic and copies ran while one was open for 23% of the time, Pallas kernels for 52%

profile of v2, /device:TPU:0, one launch (start us, length us, event | category | flops | bytes accessed | tf_op | source)
XLA Modules:
  0.0 1188.8 jit_solution(13589344266073301858)
XLA Ops:
  19.0 50.4 %gather_dense.2 = bf16[8,128,3200]{2,1,0:T(8,128)(2,1)} custom-call(bf16[128,3200]{1,0:T(8,128)(2,1)} %concatenate.67.x_ref), custom_call_target="tpu_custom_call" | custom-call | tf_op jit(solution)/shard_map/gather_dense/pallas_call | solution.py:312
  69.4 2.2 pad_maximum_fusion.3
  76.2 3.5 fusion.37
  81.6 28.5 %halo.2 = bf16[5,256,1024]{2,1,0:T(8,128)(2,1)} custom-call(bf16[256,1024]{1,0:T(8,128)(2,1)} %get-tuple-element.173.kv_ref), custom_call_target="tpu_custom_call" | custom-call | tf_op jit(solution)/shard_map/halo/pallas_call | solution.py:617
  116.1 4.7 fusion.126
  120.8 3.1 exponential_reduce_fusion.1
  123.9 3.9 copy-done.2
  127.8 5.5 fusion.63
  133.3 2.8 multiply_reduce_fusion.12
  139.5 19.2 %spread.4 = bf16[4,256,1152]{2,1,0:T(8,128)(2,1)} custom-call(bf16[256,1152]{1,0:T(8,128)(2,1)} %concatenate.69.x_ref), custom_call_target="tpu_custom_call" | custom-call | tf_op jit(solution)/shard_map/spread/pallas_call | solution.py:125
  159.8 141.4 %gather_dense.3 = bf16[8,128,3200]{2,1,0:T(8,128)(2,1)} custom-call(bf16[128,3200]{1,0:T(8,128)(2,1)} %concatenate.68.x_ref), custom_call_target="tpu_custom_call" | custom-call | tf_op jit(solution)/shard_map/gather_dense/pallas_call | solution.py:312
  304.6 24.4 %ffn_forward.2 = (bf16[1024,1024]{1,0:T(8,128)(2,1)}, bf16[4,1024,1024]{2,1,0:T(8,128)(2,1)}) custom-call(s32[1]{0:T(128)} %bitcast.25.first_ref, bf16[1024,1152]{1,0:T(8,128)(2,1)} %bitcast.290, bf16[8,4,192,1024]{3,2,1,0:T(8,128)(2,1)} %bitcast.346), custom_call_target="tpu_custom_call" | custom-call | flops 12884901888 | bytes 25690112 | tf_op jit(solution)/shard_map/ffn_forward/pallas_call | solution.py:793
  329.0 18.5 %collect.4 = f32[256,1024]{1,0:T(8,128)} custom-call(bf16[4,256,1024]{2,1,0:T(8,128)(2,1)} %bitcast.298), custom_call_target="tpu_custom_call" | custom-call | tf_op jit(solution)/shard_map/collect/pallas_call | solution.py:202
  349.1 3.9 fusion.40
  354.8 22.6 %halo.3 = bf16[5,256,1024]{2,1,0:T(8,128)(2,1)} custom-call(bf16[256,1024]{1,0:T(8,128)(2,1)} %get-tuple-element.169.kv_ref), custom_call_target="tpu_custom_call" | custom-call | tf_op jit(solution)/shard_map/halo/pallas_call | solution.py:617
  382.2 4.7 fusion.127
  386.9 3.1 exponential_reduce_fusion
  390.0 3.9 copy-done.3
  393.9 5.5 fusion.66
  399.4 2.8 multiply_reduce_fusion.10
  405.2 18.4 %spread.5 = bf16[4,256,1152]{2,1,0:T(8,128)(2,1)} custom-call(bf16[256,1152]{1,0:T(8,128)(2,1)} %concatenate.70.x_ref), custom_call_target="tpu_custom_call" | custom-call | tf_op jit(solution)/shard_map/spread/pallas_call | solution.py:125
  423.5 71.6 %all-gather.7.cloned.1.call-done = bf16[32,192,1024]{2,1,0:T(8,128)(2,1)} async-done(((bf16[4,192,1024]{2,1,0:T(8,128)(2,1)}), bf16[32,192,1024]{2,1,0:T(8,128)(2,1)}) %all-gather.7.cloned.1.call-update) | async-done | bytes 12582928 | tf_op jit(solution)/shard_map/all_gather | solution.py:1027
  495.2 23.4 %ffn_forward.3 = (bf16[1024,1024]{1,0:T(8,128)(2,1)}, bf16[4,1024,1024]{2,1,0:T(8,128)(2,1)}) custom-call(s32[1]{0:T(128)} %bitcast.25.first_ref, bf16[1024,1152]{1,0:T(8,128)(2,1)} %bitcast.292, bf16[8,4,192,1024]{3,2,1,0:T(8,128)(2,1)} %bitcast.348), custom_call_target="tpu_custom_call" | custom-call | flops 12884901888 | bytes 25690112 | tf_op jit(solution)/shard_map/ffn_forward/pallas_call | solution.py:793
  518.5 18.4 %collect.5 = f32[256,1024]{1,0:T(8,128)} custom-call(bf16[4,256,1024]{2,1,0:T(8,128)(2,1)} %bitcast.299), custom_call_target="tpu_custom_call" | custom-call | tf_op jit(solution)/shard_map/collect/pallas_call | solution.py:202
  539.9 18.8 %spread.6 = bf16[4,256,1152]{2,1,0:T(8,128)(2,1)} custom-call(bf16[256,1152]{1,0:T(8,128)(2,1)} %concatenate.71.x_ref), custom_call_target="tpu_custom_call" | custom-call | tf_op jit(solution)/shard_map/spread/pallas_call | solution.py:125
  558.7 44.4 %ffn_backward.2 = (bf16[1024,1024]{1,0:T(8,128)(2,1)}, bf16[8,4,192,1024]{3,2,1,0:T(8,128)(2,1)}, f32[1024,128]{1,0:T(8,128)}) custom-call(s32[1]{0:T(128)} %bitcast.25.first_ref, bf16[1024,1152]{1,0:T(8,128)(2,1)} %bitcast.293, bf16[1024,1152]{1,0:T(8,128)(2,1)} %bitcast.294, bf16[4,1024,1024]{2,1,0:T(8,128)(2,1)} %get-tuple-element.54.gate_up_ref, ...), custom_call_target="tpu_custom_call" | custom-call | flops 25769803776 | bytes 42991616 | tf_op jit(solution)/shard_map/ffn_backward/pallas_call | solution.py:904
  605.2 18.5 %collect.6 = f32[256,1024]{1,0:T(8,128)} custom-call(bf16[4,256,1024]{2,1,0:T(8,128)(2,1)} %bitcast.297), custom_call_target="tpu_custom_call" | custom-call | tf_op jit(solution)/shard_map/collect/pallas_call | solution.py:202
  626.8 2.8 fusion.72
  629.8 10.2 fusion.34
  640.1 4.1 concatenate.74
  644.2 4.1 copy.296
  648.3 13.8 %fusion.3 = (f32[8,2,256]{2,1,0:T(2,128)S(1)}, f32[8,1280,256,2]{2,1,3,0:T(8,128)}) fusion(f32[8,2,256,1280]{2,3,1,0:T(8,128)} %copy-done.3, f32[8,2,256]{2,1,0:T(2,128)S(1)} %bitcast.310, bf16[1280,8,64,1]{0,2,3,1:T(8,128)(2,1)S(1)} %bitcast.271, bf16[256,8,2,64]{0,3,2,1:T(8,128)(2,1)S(1)} %bitcast.281), kind=kOutput, calls=%fused_computation.7 | convolution fusion | flops 686813184 | bytes 43810816 | tf_op jit(solution)/shard_map/tngd,snd->ngts/dot_general | solution.py:1127
  662.1 14.9 %fusion.5 = bf16[8,2,256,1280]{2,3,1,0:T(8,128)(2,1)S(1)} fusion(f32[8,1280,256,2]{2,1,3,0:T(8,128)} %get-tuple-element.207, f32[8,2,256,1280]{2,3,1,0:T(8,128)} %copy-done.3, f32[8,2,256]{2,1,0:T(2,128)S(1)} %get-tuple-element.206, f32[8,2,256]{2,1,0:T(2,128)S(1)} %bitcast.311), kind=kLoop, calls=%fused_computation.9 | loop fusion | flops 20971520 | bytes 52461568 | tf_op jit(solution)/shard_map/convert_element_type | solution.py:1130
  681.9 7.3 fusion.30
  689.2 2.4 concatenate.73
  691.6 4.2 copy.295
  695.8 3.2 pad_maximum_fusion.g_ref
  699.0 39.1 %halo_back.2 = f32[256,1024]{1,0:T(8,128)} custom-call(bf16[5,256,1024]{2,1,0:T(8,128)(2,1)} %pad_maximum_fusion.g_ref), custom_call_target="tpu_custom_call" | custom-call | tf_op jit(solution)/shard_map/halo_back/pallas_call | solution.py:734
  739.5 3.9 multiply_reduce_fusion.1
  745.7 17.8 %spread.7 = bf16[4,256,1152]{2,1,0:T(8,128)(2,1)} custom-call(bf16[256,1152]{1,0:T(8,128)(2,1)} %concatenate.77.x_ref), custom_call_target="tpu_custom_call" | custom-call | tf_op jit(solution)/shard_map/spread/pallas_call | solution.py:125
  763.5 44.0 %ffn_backward.3 = (bf16[1024,1024]{1,0:T(8,128)(2,1)}, bf16[8,4,192,1024]{3,2,1,0:T(8,128)(2,1)}, f32[1024,128]{1,0:T(8,128)}) custom-call(s32[1]{0:T(128)} %bitcast.25.first_ref, bf16[1024,1152]{1,0:T(8,128)(2,1)} %bitcast.291, bf16[1024,1152]{1,0:T(8,128)(2,1)} %bitcast.295, bf16[4,1024,1024]{2,1,0:T(8,128)(2,1)} %get-tuple-element.56.gate_up_ref, ...), custom_call_target="tpu_custom_call" | custom-call | flops 25769803776 | bytes 42991616 | tf_op jit(solution)/shard_map/ffn_backward/pallas_call | solution.py:904
  810.5 18.6 %collect.7 = f32[256,1024]{1,0:T(8,128)} custom-call(bf16[4,256,1024]{2,1,0:T(8,128)(2,1)} %bitcast.296), custom_call_target="tpu_custom_call" | custom-call | tf_op jit(solution)/shard_map/collect/pallas_call | solution.py:202
  836.3 3.0 fusion.69
  839.5 10.3 fusion.31
  849.8 4.1 concatenate.80
  853.9 4.0 copy.306
  858.0 13.4 %fusion = (f32[8,2,256]{2,1,0:T(2,128)S(1)}, f32[8,1280,256,2]{2,1,3,0:T(8,128)}) fusion(f32[8,2,256,1280]{2,3,1,0:T(8,128)} %copy-done.2, f32[8,2,256]{2,1,0:T(2,128)S(1)} %bitcast.306, bf16[1280,8,64,1]{0,2,3,1:T(8,128)(2,1)S(1)} %bitcast.269, bf16[256,8,2,64]{0,3,2,1:T(8,128)(2,1)S(1)} %bitcast.283), kind=kOutput, calls=%fused_computation.2 | convolution fusion | flops 686813184 | bytes 43810816 | tf_op jit(solution)/shard_map/tngd,snd->ngts/dot_general | solution.py:1127
  871.3 14.8 %fusion.2 = bf16[8,2,256,1280]{2,3,1,0:T(8,128)(2,1)S(1)} fusion(f32[8,1280,256,2]{2,1,3,0:T(8,128)} %get-tuple-element.210, f32[8,2,256,1280]{2,3,1,0:T(8,128)} %copy-done.2, f32[8,2,256]{2,1,0:T(2,128)S(1)} %get-tuple-element.209, f32[8,2,256]{2,1,0:T(2,128)S(1)} %bitcast.307), kind=kLoop, calls=%fused_computation.4 | loop fusion | flops 20971520 | bytes 52461568 | tf_op jit(solution)/shard_map/convert_element_type | solution.py:1130
  891.2 7.6 fusion.29
  898.8 2.4 concatenate.79
  901.2 4.2 copy.305
  905.4 3.2 pad_maximum_fusion.1.g_ref
  908.6 55.6 %halo_back.3 = f32[256,1024]{1,0:T(8,128)} custom-call(bf16[5,256,1024]{2,1,0:T(8,128)(2,1)} %pad_maximum_fusion.1.g_ref), custom_call_target="tpu_custom_call" | custom-call | tf_op jit(solution)/shard_map/halo_back/pallas_call | solution.py:734
  965.6 4.8 multiply_reduce_fusion.3
  972.9 2.6 concatenate.83.refs_4_
  975.6 3.5 convolution_convert_fusion.2
  981.1 3.4 convolution_convert_fusion
  984.5 3.4 convolution_convert_fusion.1
  987.9 152.7 %reduce_dense.1 = bf16[128,6272]{1,0:T(8,128)(2,1)} custom-call(bf16[8,128,2048]{2,1,0:T(8,128)(2,1)} %bitcast.249, bf16[8,128,1024]{2,1,0:T(8,128)(2,1)} %bitcast.279, bf16[8,128,2048]{2,1,0:T(8,128)(2,1)} %bitcast.248, bf16[8,128,1024]{2,1,0:T(8,128)(2,1)} %bitcast.278, bf16[8,128,128]{2,1,0:T(8,128)(2,1)} %concatenate.83.refs_4_), custom_call_target="tpu_custom_call" | custom-call | tf_op jit(solution)/shard_map/reduce_dense/pallas_call | solution.py:471
  1148.0 2.6 fusion.78
  1150.7 2.5 add_multiply_fusion.3
  1156.4 4.0 add_multiply_fusion.2
  1166.4 6.6 add_multiply_fusion.1
  1174.6 7.4 add_multiply_fusion
  (333 shorter events, 98.6 us)
Async XLA Ops:
  7.2 65.2 %copy-start = (s32[4,4]{1,0:T(4,128)S(1)}, s32[4,4]{1,0:T(4,128)}, u32[]{:S(2)}) copy-start(s32[4,4]{1,0:T(4,128)} %param.24) | copy-start | bytes 196
  7.2 5.1 copy-start.32
  7.2 297.3 %all-gather.5.cloned.1.call-start = ((), (), s32[]{:S(2)}) async-start(), calls=%async_computation.4 | async-start | bytes 14155776 | tf_op jit(solution)/shard_map/all_gather | solution.py:1027
  17.0 52.4 %copy-start.68 = (bf16[128,110]{1,0:T(8,128)(2,1)}, bf16[128,110]{1,0:T(8,128)(2,1)S(1)}, u32[]{:S(2)}) copy-start(bf16[128,110]{1,0:T(8,128)(2,1)S(1)} %broadcast.344) | copy-start | bytes 84484
  71.6 423.6 %all-gather.7.cloned.1.call-start = ((), (), s32[]{:S(2)}) async-start(), calls=%async_computation.5 | async-start | bytes 14155776 | tf_op jit(solution)/shard_map/all_gather | solution.py:1027
  72.4 1088.0 %reduce-scatter.5.cloned.1.call-start = ((), (), s32[]{:S(2)}) async-start(), calls=%async_computation.3 | async-start | bytes 14155776 | tf_op jit(solution)/shard_map/reduce_scatter | solution.py:1112
  76.2 60.1 %copy-start.75 = (f32[1,1024]{1,0:T(1,128)}, f32[1,1024]{1,0:T(1,128)S(1)}, u32[]{:S(2)}) copy-start(f32[1,1024]{1,0:T(1,128)S(1)} %get-tuple-element.190) | copy-start | bytes 12292
  116.1 4.8 copy-start.34
  120.8 7.0 copy-start.2
  123.9 9.4 copy-start.64
  133.3 4.8 copy-start.67
  136.2 211.4 %copy-start.6 = (f32[256,1024]{1,0:T(8,128)}, f32[256,1024]{1,0:T(8,128)S(1)}, u32[]{:S(2)}) copy-start(f32[256,1024]{1,0:T(8,128)S(1)} %get-tuple-element.197) | copy-start | bytes 3145732
  136.2 22.5 %copy-start.83 = (f32[256]{0:T(256)}, f32[256]{0:T(256)S(1)}, u32[]{:S(2)}) copy-start(f32[256]{0:T(256)S(1)} %fusion.99) | copy-start | bytes 3076
  138.0 20.7 %copy-start.53 = (bf16[128,2048]{1,0:T(8,128)(2,1)S(1)}, bf16[128,2048]{1,0:T(8,128)(2,1)}, u32[]{:S(2)}) copy-start(bf16[128,2048]{1,0:T(8,128)(2,1)} %get-tuple-element.170) | copy-start | bytes 1572868
  138.0 20.7 %copy-start.58 = (bf16[128,1024]{1,0:T(8,128)(2,1)S(1)}, bf16[128,1024]{1,0:T(8,128)(2,1)}, u32[]{:S(2)}) copy-start(bf16[128,1024]{1,0:T(8,128)(2,1)} %get-tuple-element.176) | copy-start | bytes 786436
  138.0 20.7 %copy-start.69 = (bf16[128,110]{1,0:T(8,128)(2,1)S(1)}, bf16[128,110]{1,0:T(8,128)(2,1)}, u32[]{:S(2)}) copy-start(bf16[128,110]{1,0:T(8,128)(2,1)} %copy-done.68) | copy-start | bytes 84484
  138.0 20.7 %copy-start.73 = (bf16[128,2]{1,0:T(8,128)(2,1)S(1)}, bf16[128,2]{1,0:T(8,128)(2,1)}, u32[]{:S(2)}) copy-start(bf16[128,2]{1,0:T(8,128)(2,1)} %get-tuple-element.182) | copy-start | bytes 1540
  138.0 20.7 %copy-start.74 = (bf16[128,16]{1,0:T(8,128)(2,1)S(1)}, bf16[128,16]{1,0:T(8,128)(2,1)}, u32[]{:S(2)}) copy-start(bf16[128,16]{1,0:T(8,128)(2,1)} %get-tuple-element.184) | copy-start | bytes 12292
  138.5 21.3 %copy-start.62 = (bf16[256,96]{1,0:T(8,128)(2,1)}, bf16[256,96]{1,0:T(8,128)(2,1)S(1)}, u32[]{:S(2)}) copy-start(bf16[256,96]{1,0:T(8,128)(2,1)S(1)} %broadcast.348) | copy-start | bytes 147460
  386.9 7.0 copy-start.3
  399.4 4.4 copy-start.66
  518.5 18.4 %copy-start.40 = (f32[256,1024]{1,0:T(8,128)S(1)}, f32[256,1024]{1,0:T(8,128)}, u32[]{:S(2)}) copy-start(f32[256,1024]{1,0:T(8,128)} %param.23) | copy-start | bytes 3145732
  603.1 560.6 %reduce-scatter.3.cloned.1.call-start = ((), (), s32[]{:S(2)}) async-start(), calls=%async_computation.2 | async-start | bytes 14155776 | tf_op jit(solution)/shard_map/reduce_scatter | solution.py:1112
  605.2 20.2 %copy-start.24 = (f32[256,1024]{1,0:T(8,128)S(1)}, f32[256,1024]{1,0:T(8,128)}, u32[]{:S(2)}) copy-start(f32[256,1024]{1,0:T(8,128)} %collect.5) | copy-start | bytes 3145732
  626.8 116.6 %copy-start.27 = (f32[256,1024]{1,0:T(8,128)}, f32[256,1024]{1,0:T(8,128)S(1)}, u32[]{:S(2)}) copy-start(f32[256,1024]{1,0:T(8,128)S(1)} %get-tuple-element.164) | copy-start | bytes 3145732
  640.1 8.2 copy-start.19
  662.0 14.9 %copy-start.13 = (bf16[1280,512]{0,1:T(8,128)(2,1)S(1)}, bf16[1280,512]{0,1:T(8,128)(2,1)}, u32[]{:S(2)}) copy-start(bf16[1280,512]{0,1:T(8,128)(2,1)} %copy.281) | copy-start | bytes 3932164
  677.0 4.9 copy-start.21
  691.6 4.2 copy-start.35
  699.0 40.4 %copy-start.11 = (f32[256,1024]{1,0:T(8,128)S(1)}, f32[256,1024]{1,0:T(8,128)}, u32[]{:S(2)}) copy-start(f32[256,1024]{1,0:T(8,128)} %copy-done.10) | copy-start | bytes 3145732
  699.0 40.5 %copy-start.48 = (bf16[256,1024]{1,0:T(8,128)(2,1)S(1)}, bf16[256,1024]{1,0:T(8,128)(2,1)}, u32[]{:S(2)}) copy-start(bf16[256,1024]{1,0:T(8,128)(2,1)} %copy.297) | copy-start | bytes 1572868
  743.9 19.6 %copy-start.29 = (f32[256,1024]{1,0:T(8,128)}, f32[256,1024]{1,0:T(8,128)S(1)}, u32[]{:S(2)}) copy-start(f32[256,1024]{1,0:T(8,128)S(1)} %get-tuple-element.147) | copy-start | bytes 3145732
  807.5 21.6 %copy-start.7 = (f32[256,1024]{1,0:T(8,128)S(1)}, f32[256,1024]{1,0:T(8,128)}, u32[]{:S(2)}) copy-start(f32[256,1024]{1,0:T(8,128)} %copy-done.6) | copy-start | bytes 3145732
  807.5 21.6 %copy-start.76 = (f32[1,1024]{1,0:T(1,128)S(1)}, f32[1,1024]{1,0:T(1,128)}, u32[]{:S(2)}) copy-start(f32[1,1024]{1,0:T(1,128)} %copy-done.75) | copy-start | bytes 12292
  807.5 21.6 %copy-start.84 = (f32[256]{0:T(256)S(1)}, f32[256]{0:T(256)}, u32[]{:S(2)}) copy-start(f32[256]{0:T(256)} %copy-done.83) | copy-start | bytes 3076
  810.5 23.3 %copy-start.88 = (f32[256]{0:T(256)S(1)}, f32[256]{0:T(256)}, u32[]{:S(2)}) copy-start(f32[256]{0:T(256)} %copy-done.87) | copy-start | bytes 3076
  829.1 4.7 copy-start.25
  849.8 8.2 copy-start.18
  871.3 14.8 %copy-start.12 = (bf16[1280,512]{0,1:T(8,128)(2,1)S(1)}, bf16[1280,512]{0,1:T(8,128)(2,1)}, u32[]{:S(2)}) copy-start(bf16[1280,512]{0,1:T(8,128)(2,1)} %copy.272) | copy-start | bytes 3932164
  886.2 4.0 copy-start.5
  886.2 5.0 copy-start.20
  901.2 4.2 copy-start.36
  908.6 56.9 %copy-start.9 = (f32[256,1024]{1,0:T(8,128)S(1)}, f32[256,1024]{1,0:T(8,128)}, u32[]{:S(2)}) copy-start(f32[256,1024]{1,0:T(8,128)} %param.22) | copy-start | bytes 3145732
  908.6 56.9 %copy-start.50 = (bf16[256,1024]{1,0:T(8,128)(2,1)S(1)}, bf16[256,1024]{1,0:T(8,128)(2,1)}, u32[]{:S(2)}) copy-start(bf16[256,1024]{1,0:T(8,128)(2,1)} %copy.307) | copy-start | bytes 1572868
  908.6 56.9 %copy-start.71 = (f32[1,1024]{1,0:T(1,128)S(1)}, f32[1,1024]{1,0:T(1,128)}, u32[]{:S(2)}) copy-start(f32[1,1024]{1,0:T(1,128)} %copy-done.70) | copy-start | bytes 12292
  908.6 56.9 %copy-start.79 = (f32[256]{0:T(256)S(1)}, f32[256]{0:T(256)}, u32[]{:S(2)}) copy-start(f32[256]{0:T(256)} %copy-done.78) | copy-start | bytes 3076
  965.5 4.9 copy-start.46
  965.6 5.7 copy-start.56
  965.6 5.7 copy-start.57
  965.6 7.4 copy-start.59
  972.9 6.1 copy-start.23
  1140.6 4.8 copy-start.86
  1140.6 4.8 copy-start.89
  1140.6 4.8 copy-start.90
  1140.6 4.8 copy-start.91
  1140.6 5.4 copy-start.77
  1140.6 5.4 copy-start.81
  1140.6 5.4 copy-start.82
  1150.7 4.1 copy-start.55
  1162.3 4.0 copy-start.31
  1166.3 6.7 copy-start.15
  1166.4 6.7 copy-start.38
  1166.4 8.2 copy-start.39
  1174.6 7.4 copy-start.1
  (32 other events, 80.5 us)
Sparse Core Ops, SparseCore 0:
  71.7 221.8 all-gather.4
  296.4 198.7 all-gather.6
  603.2 224.2 reduce-scatter.4
  830.9 245.9 reduce-scatter.2

commit v3 on v2

--- a/solution.py
+++ b/solution.py
@@ -119,7 +119,7 @@
             far_copy(d, cut).wait_send()
 
 
-def spread(rows, owners):
+def spread(rows, owners, collective):
     dma = pltpu.SemaphoreType.DMA
     chips, cuts = owners // 2, 4
     return pl.pallas_call(
@@ -131,7 +131,7 @@
             dma((chips, cuts)), dma((chips, cuts)), dma((chips - 1, cuts)), dma((chips - 1, cuts)),
         ],
         compiler_params=pltpu.CompilerParams(
-            collective_id=1, has_side_effects=True, vmem_limit_bytes=VMEM_LIMIT
+            collective_id=collective, has_side_effects=True, vmem_limit_bytes=VMEM_LIMIT
         ),
         name="spread",
     )(rows)
@@ -195,7 +195,7 @@
             far_copy(d, cut).wait_send()
 
 
-def collect(parts):
+def collect(parts, collective):
     owners, rows, width = parts.shape
     dma = pltpu.SemaphoreType.DMA
     chips, cuts = owners // 2, 4
@@ -211,7 +211,7 @@
             dma((chips, cuts)), dma((chips, cuts)), dma((chips - 1, cuts)), dma((chips - 1, cuts)),
         ],
         compiler_params=pltpu.CompilerParams(
-            collective_id=2, has_side_effects=True, vmem_limit_bytes=VMEM_LIMIT
+            collective_id=collective, has_side_effects=True, vmem_limit_bytes=VMEM_LIMIT
         ),
         name="collect",
     )(parts)
@@ -829,14 +829,12 @@
     g_ref,
     gate_up_ref,
     w_ref,
-    router_ref,
     part_ref,
     grad_ref,
-    router_grad_ref,
     acc,
     d_gate_up,
     hidden_all,
-    d_logits,
+    d_weights,
 ):
     e = pl.program_id(0)
     inner = w_ref.shape[-1]
@@ -848,11 +846,10 @@
     last = pl.num_programs(0) - 1
     for t in range(tokens // tile):
         rows = pl.ds(t * tile, tile)
-        d_plain = outer_cols(g_ref[rows, :width], w_down)
+        d_plain = outer_cols(g_ref[rows, :], w_down)
         gate = gate_up_ref[0, rows, :half].astype(F32)
         up = gate_up_ref[0, rows, half:].astype(F32)
         weight = column_of(x_ref[rows, width:], index, experts_total)
-        mean_d = column_of(g_ref[rows, width:], 0, 1)
         sig = jax.nn.sigmoid(gate)
         silu = gate * sig
         hidden = silu * up
@@ -861,46 +858,42 @@
         hidden_all[rows, :] = (hidden * weight).astype(BF16)
         d_gate_up[rows, :half] = (d_hidden * up * sig * (1.0 + gate * (1.0 - sig))).astype(BF16)
         d_gate_up[rows, half:] = (d_hidden * silu).astype(BF16)
-        lanes = lax.broadcasted_iota(jnp.int32, (tile, d_logits.shape[1]), 1)
-        d_logit = jnp.where(lanes == e, weight * (d_weight - mean_d), 0.0).astype(BF16)
+        lanes = lax.broadcasted_iota(jnp.int32, (tile, d_weights.shape[1]), 1)
+        high = d_weight.astype(BF16).astype(F32)
+        columns = jnp.where(
+            lanes == index, high, jnp.where(lanes == index + experts_total, d_weight - high, 0.0)
+        )
         out = outer_cols(d_gate_up[rows, :], w_in)
 
         @pl.when(e == 0)
         def _():
             acc[rows, :] = out
-            d_logits[rows, :] = d_logit
+            d_weights[rows, :] = columns
 
         @pl.when(e > 0)
         def _():
             acc[rows, :] += out
-            d_logits[rows, :] += d_logit
-
-    x = x_ref[:, :width]
+            d_weights[rows, :] += columns
+
+        @pl.when(e == last)
+        def _():
+            part_ref[rows, :width] = acc[rows, :].astype(BF16)
+            part_ref[rows, width:] = d_weights[rows, :].astype(BF16)
+
     grad_ref[:, 0, :in_rows, :] = (
-        inner_rows(x, d_gate_up[...]).astype(BF16).reshape(-1, in_rows, inner)
+        inner_rows(x_ref[:, :width], d_gate_up[...]).astype(BF16).reshape(-1, in_rows, inner)
     )
     grad_ref[:, 0, in_rows:, :] = (
-        inner_rows(hidden_all[...], g_ref[:, :width])
+        inner_rows(hidden_all[...], g_ref[...])
         .astype(BF16)
         .reshape(-1, w_ref.shape[2] - in_rows, width)
     )
 
-    @pl.when(e == last)
-    def _():
-        for t in range(tokens // tile):
-            rows = pl.ds(t * tile, tile)
-            out = acc[rows, :] + jnp.dot(
-                d_logits[rows, :], router_ref[...], preferred_element_type=F32
-            )
-            part_ref[rows, :] = out.astype(BF16)
-        router_grad_ref[...] = inner_rows(x, d_logits[...])
-
-
-def ffn_backward(first, x_all, g_all, gate_up, w_all, router_rows, experts_total, in_rows):
+
+def ffn_backward(first, x_all, g_all, gate_up, w_all, experts_total, in_rows):
     shards, local, piece, inner = w_all.shape
     tokens, wide = x_all.shape
     width = in_rows * shards
-    lanes = router_rows.shape[0]
     return pl.pallas_call(
         functools.partial(ffn_backward_kernel, 256, width, in_rows, experts_total),
         grid_spec=pltpu.PrefetchScalarGridSpec(
@@ -908,27 +901,24 @@
             grid=(local,),
             in_specs=[
                 pl.BlockSpec((tokens, wide), lambda e, f: (0, 0)),
-                pl.BlockSpec((tokens, g_all.shape[1]), lambda e, f: (0, 0)),
+                pl.BlockSpec((tokens, width), lambda e, f: (0, 0)),
                 pl.BlockSpec((1, tokens, inner), lambda e, f: (e, 0, 0)),
                 pl.BlockSpec((shards, 1, piece, inner), lambda e, f: (0, e, 0, 0)),
-                pl.BlockSpec((lanes, width), lambda e, f: (0, 0)),
             ],
             out_specs=[
-                pl.BlockSpec((tokens, width), lambda e, f: (0, 0)),
+                pl.BlockSpec((tokens, wide), lambda e, f: (0, 0)),
                 pl.BlockSpec((shards, 1, piece, inner), lambda e, f: (0, e, 0, 0)),
-                pl.BlockSpec((width, lanes), lambda e, f: (0, 0)),
             ],
             scratch_shapes=[
                 pltpu.VMEM((tokens, width), F32),
                 pltpu.VMEM((tokens, inner), BF16),
                 pltpu.VMEM((tokens, inner // 2), BF16),
-                pltpu.VMEM((tokens, lanes), BF16),
+                pltpu.VMEM((tokens, wide - width), F32),
             ],
         ),
         out_shape=[
-            jax.ShapeDtypeStruct((tokens, width), BF16),
+            jax.ShapeDtypeStruct((tokens, wide), BF16),
             jax.ShapeDtypeStruct(w_all.shape, BF16),
-            jax.ShapeDtypeStruct((width, lanes), F32),
         ],
         compiler_params=pltpu.CompilerParams(vmem_limit_bytes=VMEM_LIMIT),
         cost_estimate=pl.CostEstimate(
@@ -937,7 +927,7 @@
             transcendentals=0,
         ),
         name="ffn_backward",
-    )(first, x_all, g_all, gate_up, w_all, router_rows)
+    )(first, x_all, g_all, gate_up, w_all)
 
 
 def on_device(
@@ -1001,18 +991,15 @@
     expert_ids = jnp.arange(experts_total, dtype=jnp.int32)
     side = 128
 
-    def dense_piece(layer_no):
+    def dense_piece():
         rows = w_qkv.shape[1]
-        return jnp.concatenate(
-            [
-                w_qkv[layer_no].astype(BF16),
-                w_out[layer_no].astype(BF16),
-                router[layer_no].astype(BF16),
-                gains[layer_no].T.astype(BF16),
-                jnp.zeros((rows, side - experts_total - 2), BF16),
-            ],
-            1,
-        )
+        parts = []
+        for layer_no in range(LAYERS):
+            parts += [w_qkv[layer_no].astype(BF16), w_out[layer_no].astype(BF16)]
+        for layer_no in range(LAYERS):
+            parts += [router[layer_no].astype(BF16), gains[layer_no].T.astype(BF16)]
+        parts.append(jnp.zeros((rows, side - LAYERS * (experts_total + 2)), BF16))
+        return jnp.concatenate(parts, 1)
 
     def expert_piece(layer_no):
         return jnp.concatenate(
@@ -1020,19 +1007,21 @@
         )
 
     layer_columns = qkv_width + width
-    dense = gather_dense(dense_piece(0), shards)
     expert_full = []
     for layer_no in range(LAYERS):
-        piece, dense = lax.optimization_barrier((expert_piece(layer_no), dense))
-        expert_full.append(lax.all_gather(piece, "shard", axis=0, tiled=False))
+        expert_full.append(
+            lax.all_gather(expert_piece(layer_no), "shard", axis=0, tiled=False)
+        )
+    dense = gather_dense(dense_piece(), shards).reshape(width, -1)
 
     kept_layers = []
     stream = hidden_in
     for layer_no in range(LAYERS):
-        dense = dense.reshape(width, -1)
-        w_qkv_full = dense[:, :qkv_width]
-        w_out_full = dense[:, qkv_width:layer_columns]
-        small = dense[:, layer_columns:]
+        at = layer_no * layer_columns
+        w_qkv_full = dense[:, at : at + qkv_width]
+        w_out_full = dense[:, at + qkv_width : at + layer_columns]
+        at = LAYERS * layer_columns + layer_no * (experts_total + 2)
+        small = dense[:, at : at + experts_total + 2]
         router_full = small[:, :experts_total]
         gain_pair = small[:, experts_total : experts_total + 2].astype(F32).T
         normed_one = rms_scale(stream, gain_pair[0]).astype(BF16)
@@ -1066,19 +1055,25 @@
         wide_rows = jnp.concatenate(
             [normed_two, high, low, jnp.zeros((tok_rows, extra - 2 * experts_total), BF16)], 1
         )
-        x_all = spread(wide_rows, owners).reshape(owners * tok_rows, width + extra)
-        if layer_no + 1 < LAYERS:
-            piece, x_all = lax.optimization_barrier((dense_piece(layer_no + 1), x_all))
-            dense = gather_dense(piece, shards)
-            dense, x_all = lax.optimization_barrier((dense, x_all))
+        x_all = spread(wide_rows, owners, 1).reshape(owners * tok_rows, width + extra)
+        if layer_no + 1 == LAYERS:
+            g_rows, x_all = lax.optimization_barrier((cotangent.astype(BF16), x_all))
+            g_all = spread(g_rows, owners, 8).reshape(owners * tok_rows, width)
+            g_all, x_all = lax.optimization_barrier((g_all, x_all))
         partial, gate_up = ffn_forward(
             first_array, x_all, expert_full[layer_no], experts_total, in_rows
         )
-        moe_out = collect(partial.reshape(owners, tok_rows, width))
+        if layer_no + 1 == LAYERS:
+            d_partial, d_experts = ffn_backward(
+                first_array, x_all, g_all, gate_up, expert_full[layer_no], experts_total, in_rows
+            )
+            partial, d_partial = lax.optimization_barrier((partial, d_partial))
+        moe_out = collect(partial.reshape(owners, tok_rows, width), 2)
         kept_layers.append(
             (
                 stream, normed_one, queries, ext_keys, ext_values, log_total, attended, mixed,
-                x_all, gate_up, moe_out, w_qkv_full, w_out_full, router_full, gain_pair,
+                x_all, gate_up, normed_two, weights, w_qkv_full, w_out_full, router_full,
+                gain_pair,
             )
         )
         stream = mixed + moe_out
@@ -1089,28 +1084,24 @@
     for layer_no in reversed(range(LAYERS)):
         (
             layer_input, normed_one, queries, ext_keys, ext_values, log_total, attended, mixed,
-            x_all, gate_up, moe_out, w_qkv_full, w_out_full, router_full, gain_pair,
+            x_all, gate_up, normed_two, weights, w_qkv_full, w_out_full, router_full,
+            gain_pair,
         ) = kept_layers[layer_no]
-        mean_d = jnp.sum(grad_stream * moe_out, axis=1, keepdims=True)
-        high = mean_d.astype(BF16)
-        low = (mean_d - high.astype(F32)).astype(BF16)
-        wide_rows = jnp.concatenate(
-            [grad_stream.astype(BF16), high, low, jnp.zeros((tok_rows, extra - 2), BF16)], 1
-        )
-        g_all = spread(wide_rows, owners).reshape(owners * tok_rows, width + extra)
-        router_rows = jnp.concatenate(
-            [
-                lax.dynamic_slice_in_dim(router_full, first_expert, local_experts, 1).T,
-                jnp.zeros((side - local_experts, width), BF16),
-            ],
-            0,
-        )
-        d_partial, d_experts, d_router_local = ffn_backward(
-            first_array, x_all, g_all, gate_up, expert_full[layer_no], router_rows,
-            experts_total, in_rows,
-        )
+        if layer_no + 1 < LAYERS:
+            g_all = spread(grad_stream.astype(BF16), owners, 8).reshape(owners * tok_rows, width)
+            d_partial, d_experts = ffn_backward(
+                first_array, x_all, g_all, gate_up, expert_full[layer_no], experts_total, in_rows
+            )
         d_experts = lax.psum_scatter(d_experts, "shard", scatter_dimension=0, tiled=True)[0]
-        d_normed_two = collect(d_partial.reshape(owners, tok_rows, width))
+        d_all = collect(d_partial.reshape(owners, tok_rows, -1), 7)
+        d_weights = (
+            d_all[:, width : width + experts_total]
+            + d_all[:, width + experts_total : width + 2 * experts_total]
+        )
+        mean_d = jnp.sum(weights * d_weights, axis=1, keepdims=True)
+        d_logits = (weights * (d_weights - mean_d)).astype(BF16)
+        d_router = inner_rows(normed_two, d_logits)
+        d_normed_two = d_all[:, :width] + outer_cols(d_logits, router_full)
         _, norm_back = jax.vjp(rms_scale, mixed, gain_pair[1])
         d_mixed_norm, d_gain_two = norm_back(d_normed_two)
         grad_mixed = grad_stream + d_mixed_norm
@@ -1149,12 +1140,6 @@
         _, norm_back = jax.vjp(rms_scale, layer_input, gain_pair[0])
         d_input_norm, d_gain_one = norm_back(d_normed_one)
         grad_stream = grad_mixed + d_input_norm
-        lanes = jnp.arange(experts_total, dtype=jnp.int32)
-        d_router = jnp.where(
-            (lanes >= first_expert) & (lanes < first_expert + local_experts),
-            jnp.tile(d_router_local[:, :local_experts], (1, owners)),
-            0.0,
-        )
         dense_parts[layer_no] = [d_w_qkv.astype(BF16), d_w_out.astype(BF16)]
         small_parts[layer_no] = [
             d_router.astype(BF16),

time: 1190 us -> 1190 us (level)
  Pallas kernels: 775 us -> 849 us
  waiting for transfers between devices: 72.4 us -> 0.13 us
  local copies, waits for them, and re-layouts: 106 us -> 93.5 us
    all_gather x2, waiting for transfers between devices: 71.6 us -> 0.04 us  [on_device(): lax.all_gather(expert_piece(layer_no), 'shard', axis=0, tiled=False)]
    pallas_call x2, Pallas kernels: 94.7 us -> 165 us  [halo_back(): pl.pallas_call(functools.partial(halo_back_kernel, n, rows, cuts), out_sh...]
    pallas_call x2, Pallas kernels: 51.1 us -> 93.5 us  [halo(): pl.pallas_call(functools.partial(halo_kernel, n, rows, cuts), out_shape=j...]
    pallas_call x2 -> x1, Pallas kernels: 192 us -> 168 us  [gather_dense(): pl.pallas_call(functools.partial(gather_dense_kernel, n, rows), out_shape...]
    unnamed x192 -> x180, local copies, waits for them, and re-layouts: 27.8 us -> 24.5 us
  transfers between devices with their start and end apart: 4 -> 4, of which waited for: 1 -> 0; matrix products, arithmetic and copies ran while one was open for 23% -> 23% of each run, Pallas kernels for 52% -> 66%
where the time goes in v3:
time: 1190 us; the launch traced here: 1180 us
  Pallas kernels  849 us (71%)
  matrix products  133 us (11%)
  local copies, waits for them, and re-layouts  93.5 us (8%)
  other arithmetic  91.9 us (8%)
  between operations  15.4 us (1%)
    pallas_call x1, Pallas kernels, gather_dense(): pl.pallas_call(functools.partial(gather_dense_kernel, n, rows), out_shape...  168 us
    pallas_call x2, Pallas kernels, halo_back(): pl.pallas_call(functools.partial(halo_back_kernel, n, rows, cuts), out_sh...  165 us
    pallas_call x1, Pallas kernels, reduce_dense(): pl.pallas_call(functools.partial(reduce_dense_kernel, n, owners, rows, tu...  142 us
    pallas_call x2, Pallas kernels, halo(): pl.pallas_call(functools.partial(halo_kernel, n, rows, cuts), out_shape=j...  93.5 us
    pallas_call x2, Pallas kernels, ffn_backward(): pl.pallas_call(functools.partial(ffn_backward_kernel, 256, width, in_rows...  84.9 us
    pallas_call x4, Pallas kernels, collect(): pl.pallas_call(functools.partial(collect_kernel, owners, cuts), out_shape...  76.3 us
    pallas_call x4, Pallas kernels, spread(): pl.pallas_call(functools.partial(spread_kernel, owners, cuts), out_shape=...  71.7 us
    pallas_call x2, Pallas kernels, ffn_forward(): pl.pallas_call(functools.partial(ffn_forward_kernel, 256, width, in_rows,...  47.5 us
  transfers between devices with their start and end apart: 4, of which 0 were waited for; matrix products, arithmetic and copies ran while one was open for 23% of the time, Pallas kernels for 66%

profile of v3, /device:TPU:0, one launch (start us, length us, event | category | flops | bytes accessed | tf_op | source)
XLA Modules:
  0.0 1182.9 jit_solution(17169442753262392385)
XLA Ops:
  17.8 1.9 concatenate.45.x_ref
  19.8 167.8 %gather_dense.1 = bf16[8,128,6272]{2,1,0:T(8,128)(2,1)} custom-call(bf16[128,6272]{1,0:T(8,128)(2,1)} %concatenate.45.x_ref), custom_call_target="tpu_custom_call" | custom-call | tf_op jit(solution)/shard_map/gather_dense/pallas_call | solution.py:312
  190.1 3.6 fusion.37
  195.6 26.6 %halo.2 = bf16[5,256,1024]{2,1,0:T(8,128)(2,1)} custom-call(bf16[256,1024]{1,0:T(8,128)(2,1)} %get-tuple-element.171.kv_ref), custom_call_target="tpu_custom_call" | custom-call | tf_op jit(solution)/shard_map/halo/pallas_call | solution.py:617
  228.1 4.7 fusion.128
  232.9 3.1 exponential_reduce_fusion.1
  236.0 3.9 copy-done.2
  239.9 5.5 fusion.63
  245.4 2.9 multiply_reduce_fusion.10
  252.5 19.0 %spread.4 = bf16[4,256,1152]{2,1,0:T(8,128)(2,1)} custom-call(bf16[256,1152]{1,0:T(8,128)(2,1)} %concatenate.46.x_ref), custom_call_target="tpu_custom_call" | custom-call | tf_op jit(solution)/shard_map/spread/pallas_call | solution.py:125
  271.6 24.1 %ffn_forward.2 = (bf16[1024,1024]{1,0:T(8,128)(2,1)}, bf16[4,1024,1024]{2,1,0:T(8,128)(2,1)}) custom-call(s32[1]{0:T(128)} %bitcast.26.first_ref, bf16[1024,1152]{1,0:T(8,128)(2,1)} %bitcast.275, bf16[8,4,192,1024]{3,2,1,0:T(8,128)(2,1)} %bitcast.320), custom_call_target="tpu_custom_call" | custom-call | flops 12884901888 | bytes 25690112 | tf_op jit(solution)/shard_map/ffn_forward/pallas_call | solution.py:793
  295.7 18.3 %collect.4 = f32[256,1024]{1,0:T(8,128)} custom-call(bf16[4,256,1024]{2,1,0:T(8,128)(2,1)} %bitcast.284), custom_call_target="tpu_custom_call" | custom-call | tf_op jit(solution)/shard_map/collect/pallas_call | solution.py:202
  315.6 3.9 fusion.40
  321.3 66.9 %halo.3 = bf16[5,256,1024]{2,1,0:T(8,128)(2,1)} custom-call(bf16[256,1024]{1,0:T(8,128)(2,1)} %get-tuple-element.169.kv_ref), custom_call_target="tpu_custom_call" | custom-call | tf_op jit(solution)/shard_map/halo/pallas_call | solution.py:617
  393.1 4.7 fusion.129
  397.8 3.1 exponential_reduce_fusion
  400.8 4.3 copy-done.3
  405.2 5.5 fusion.66
  410.7 2.9 multiply_reduce_fusion.8
  416.8 18.6 %spread.5 = bf16[4,256,1152]{2,1,0:T(8,128)(2,1)} custom-call(bf16[256,1152]{1,0:T(8,128)(2,1)} %concatenate.48.x_ref), custom_call_target="tpu_custom_call" | custom-call | tf_op jit(solution)/shard_map/spread/pallas_call | solution.py:125
  435.4 17.7 %spread.6 = bf16[4,256,1024]{2,1,0:T(8,128)(2,1)} custom-call(bf16[256,1024]{1,0:T(8,128)(2,1)} %convert_element_type.207.x_ref), custom_call_target="tpu_custom_call" | custom-call | tf_op jit(solution)/shard_map/spread/pallas_call | solution.py:125
  453.2 23.4 %ffn_forward.3 = (bf16[1024,1024]{1,0:T(8,128)(2,1)}, bf16[4,1024,1024]{2,1,0:T(8,128)(2,1)}) custom-call(s32[1]{0:T(128)} %bitcast.26.first_ref, bf16[1024,1152]{1,0:T(8,128)(2,1)} %bitcast.279, bf16[8,4,192,1024]{3,2,1,0:T(8,128)(2,1)} %bitcast.322), custom_call_target="tpu_custom_call" | custom-call | flops 12884901888 | bytes 25690112 | tf_op jit(solution)/shard_map/ffn_forward/pallas_call | solution.py:793
  476.6 42.4 %ffn_backward.2 = (bf16[1024,1152]{1,0:T(8,128)(2,1)}, bf16[8,4,192,1024]{3,2,1,0:T(8,128)(2,1)}) custom-call(s32[1]{0:T(128)} %bitcast.26.first_ref, bf16[1024,1152]{1,0:T(8,128)(2,1)} %bitcast.280, bf16[1024,1024]{1,0:T(8,128)(2,1)} %bitcast.281, bf16[4,1024,1024]{2,1,0:T(8,128)(2,1)} %get-tuple-element.46.gate_up_ref, bf16[8,4,192,1024]{3,2,1,0:T(8,128)(2,1)} %bitcast.323), custom_call_target="tpu_custom_call" | custom-call | flops 25769803776 | bytes 42991616 | tf_op jit(solution)/shard_map/ffn_backward/pallas_call | solution.py:897
  519.1 18.4 %collect.5 = f32[256,1024]{1,0:T(8,128)} custom-call(bf16[4,256,1024]{2,1,0:T(8,128)(2,1)} %bitcast.283), custom_call_target="tpu_custom_call" | custom-call | tf_op jit(solution)/shard_map/collect/pallas_call | solution.py:202
  537.4 19.4 %collect.6 = f32[256,1152]{1,0:T(8,128)} custom-call(bf16[4,256,1152]{2,1,0:T(8,128)(2,1)} %bitcast.278), custom_call_target="tpu_custom_call" | custom-call | tf_op jit(solution)/shard_map/collect/pallas_call | solution.py:202
  562.6 2.7 fusion.72
  565.5 10.3 fusion.34
  575.8 4.1 concatenate.51
  580.0 4.0 copy.231
  584.0 14.0 %fusion.3 = (f32[8,2,256]{2,1,0:T(2,128)S(1)}, f32[8,1280,256,2]{2,1,3,0:T(8,128)}) fusion(f32[8,2,256,1280]{2,3,1,0:T(8,128)} %copy-done.3, f32[8,2,256]{2,1,0:T(2,128)S(1)} %bitcast.296, bf16[1280,8,64,1]{0,2,3,1:T(8,128)(2,1)S(1)} %bitcast.256, bf16[256,8,2,64]{0,3,2,1:T(8,128)(2,1)S(1)} %bitcast.266), kind=kOutput, calls=%fused_computation.7 | convolution fusion | flops 686813184 | bytes 43810816 | tf_op jit(solution)/shard_map/tngd,snd->ngts/dot_general | solution.py:1118
  598.0 14.6 %fusion.5 = bf16[8,2,256,1280]{2,3,1,0:T(8,128)(2,1)S(1)} fusion(f32[8,1280,256,2]{2,1,3,0:T(8,128)} %get-tuple-element.200, f32[8,2,256,1280]{2,3,1,0:T(8,128)} %copy-done.3, f32[8,2,256]{2,1,0:T(2,128)S(1)} %get-tuple-element.199, f32[8,2,256]{2,1,0:T(2,128)S(1)} %bitcast.297), kind=kLoop, calls=%fused_computation.9 | loop fusion | flops 20971520 | bytes 52461568 | tf_op jit(solution)/shard_map/convert_element_type | solution.py:1121
  614.5 2.0 copy-done.4
  617.5 7.3 fusion.30
  624.8 2.4 concatenate.50
  627.2 4.2 copy.230
  631.3 3.2 pad_maximum_fusion.g_ref
  634.5 107.3 %halo_back.2 = f32[256,1024]{1,0:T(8,128)} custom-call(bf16[5,256,1024]{2,1,0:T(8,128)(2,1)} %pad_maximum_fusion.g_ref), custom_call_target="tpu_custom_call" | custom-call | tf_op jit(solution)/shard_map/halo_back/pallas_call | solution.py:734
  743.2 3.9 multiply_reduce_fusion.1
  748.6 16.3 %spread.7 = bf16[4,256,1024]{2,1,0:T(8,128)(2,1)} custom-call(bf16[256,1024]{1,0:T(8,128)(2,1)} %get-tuple-element.138.x_ref), custom_call_target="tpu_custom_call" | custom-call | tf_op jit(solution)/shard_map/spread/pallas_call | solution.py:125
  764.9 42.5 %ffn_backward.3 = (bf16[1024,1152]{1,0:T(8,128)(2,1)}, bf16[8,4,192,1024]{3,2,1,0:T(8,128)(2,1)}) custom-call(s32[1]{0:T(128)} %bitcast.26.first_ref, bf16[1024,1152]{1,0:T(8,128)(2,1)} %bitcast.276, bf16[1024,1024]{1,0:T(8,128)(2,1)} %bitcast.282, bf16[4,1024,1024]{2,1,0:T(8,128)(2,1)} %get-tuple-element.50.gate_up_ref, bf16[8,4,192,1024]{3,2,1,0:T(8,128)(2,1)} %bitcast.321), custom_call_target="tpu_custom_call" | custom-call | flops 25769803776 | bytes 42991616 | tf_op jit(solution)/shard_map/ffn_backward/pallas_call | solution.py:897
  811.3 20.2 %collect.7 = f32[256,1152]{1,0:T(8,128)} custom-call(bf16[4,256,1152]{2,1,0:T(8,128)(2,1)} %bitcast.277), custom_call_target="tpu_custom_call" | custom-call | tf_op jit(solution)/shard_map/collect/pallas_call | solution.py:202
  840.1 2.4 fusion.69
  842.7 10.0 fusion.31
  852.7 4.4 concatenate.55
  857.2 4.1 copy.238
  861.3 13.5 %fusion = (f32[8,2,256]{2,1,0:T(2,128)S(1)}, f32[8,1280,256,2]{2,1,3,0:T(8,128)}) fusion(f32[8,2,256,1280]{2,3,1,0:T(8,128)} %copy-done.2, f32[8,2,256]{2,1,0:T(2,128)S(1)} %bitcast.292, bf16[1280,8,64,1]{0,2,3,1:T(8,128)(2,1)S(1)} %bitcast.254, bf16[256,8,2,64]{0,3,2,1:T(8,128)(2,1)S(1)} %bitcast.268), kind=kOutput, calls=%fused_computation.2 | convolution fusion | flops 686813184 | bytes 43810816 | tf_op jit(solution)/shard_map/tngd,snd->ngts/dot_general | solution.py:1118
  874.8 15.4 %fusion.2 = bf16[8,2,256,1280]{2,3,1,0:T(8,128)(2,1)S(1)} fusion(f32[8,1280,256,2]{2,1,3,0:T(8,128)} %get-tuple-element.204, f32[8,2,256,1280]{2,3,1,0:T(8,128)} %copy-done.2, f32[8,2,256]{2,1,0:T(2,128)S(1)} %get-tuple-element.203, f32[8,2,256]{2,1,0:T(2,128)S(1)} %bitcast.293), kind=kLoop, calls=%fused_computation.4 | loop fusion | flops 20971520 | bytes 52461568 | tf_op jit(solution)/shard_map/convert_element_type | solution.py:1121
  892.2 2.1 copy-done.5
  895.3 7.3 fusion.29
  902.6 2.4 concatenate.54
  904.9 4.2 copy.237
  909.1 3.2 pad_maximum_fusion.1.g_ref
  912.3 57.9 %halo_back.3 = f32[256,1024]{1,0:T(8,128)} custom-call(bf16[5,256,1024]{2,1,0:T(8,128)(2,1)} %pad_maximum_fusion.1.g_ref), custom_call_target="tpu_custom_call" | custom-call | tf_op jit(solution)/shard_map/halo_back/pallas_call | solution.py:734
  971.6 4.9 multiply_reduce_fusion.3
  978.1 2.7 concatenate.58
  980.8 3.2 convolution_convert_fusion.2
  984.0 2.0 convolution_convert_fusion.3
  986.1 3.4 convolution_convert_fusion
  989.5 3.6 convolution_convert_fusion.1
  993.1 141.9 %reduce_dense.1 = bf16[128,6272]{1,0:T(8,128)(2,1)} custom-call(bf16[8,128,2048]{2,1,0:T(8,128)(2,1)} %bitcast.248, bf16[8,128,1024]{2,1,0:T(8,128)(2,1)} %bitcast.264, bf16[8,128,2048]{2,1,0:T(8,128)(2,1)} %bitcast.247, bf16[8,128,1024]{2,1,0:T(8,128)(2,1)} %bitcast.263, bf16[8,128,128]{2,1,0:T(8,128)(2,1)} %bitcast.289), custom_call_target="tpu_custom_call" | custom-call | tf_op jit(solution)/shard_map/reduce_dense/pallas_call | solution.py:471
  1144.8 2.5 add_multiply_fusion.3
  1150.6 4.0 add_multiply_fusion.2
  1160.5 6.6 add_multiply_fusion.1
  1168.7 7.4 add_multiply_fusion
  (295 shorter events, 86.8 us)
Async XLA Ops:
  7.2 6.1 copy-start
  7.2 264.4 %all-gather.5.cloned.1.call-start = ((), (), s32[]{:S(2)}) async-start(), calls=%async_computation.4 | async-start | bytes 14155776 | tf_op jit(solution)/shard_map/all_gather | solution.py:1013
  11.9 441.2 %all-gather.7.cloned.1.call-start = ((), (), s32[]{:S(2)}) async-start(), calls=%async_computation.5 | async-start | bytes 14155776 | tf_op jit(solution)/shard_map/all_gather | solution.py:1013
  13.2 4.2 copy-start.32
  13.3 1141.3 %reduce-scatter.5.cloned.1.call-start = ((), (), s32[]{:S(2)}) async-start(), calls=%async_computation.3 | async-start | bytes 14155776 | tf_op jit(solution)/shard_map/reduce_scatter | solution.py:1095
  190.0 3.6 copy-start.73
  190.1 58.7 %copy-start.69 = (f32[1,1024]{1,0:T(1,128)}, f32[1,1024]{1,0:T(1,128)S(1)}, u32[]{:S(2)}) copy-start(f32[1,1024]{1,0:T(1,128)S(1)} %get-tuple-element.184) | copy-start | bytes 12292
  228.1 4.7 copy-start.34
  232.9 7.0 copy-start.2
  236.0 9.4 copy-start.63
  245.4 5.1 copy-start.66
  248.2 65.8 %copy-start.6 = (f32[256,1024]{1,0:T(8,128)}, f32[256,1024]{1,0:T(8,128)S(1)}, u32[]{:S(2)}) copy-start(f32[256,1024]{1,0:T(8,128)S(1)} %get-tuple-element.189) | copy-start | bytes 3145732
  248.3 23.3 %copy-start.78 = (f32[256]{0:T(256)}, f32[256]{0:T(256)S(1)}, u32[]{:S(2)}) copy-start(f32[256]{0:T(256)S(1)} %fusion.105) | copy-start | bytes 3076
  249.0 22.6 %copy-start.28 = (bf16[256,1024]{1,0:T(8,128)(2,1)}, bf16[256,1024]{1,0:T(8,128)(2,1)S(1)}, u32[]{:S(2)}) copy-start(bf16[256,1024]{1,0:T(8,128)(2,1)S(1)} %multiply_convert_fusion.2) | copy-start | bytes 1572868
  251.5 44.2 %copy-start.61 = (bf16[256,96]{1,0:T(8,128)(2,1)}, bf16[256,96]{1,0:T(8,128)(2,1)S(1)}, u32[]{:S(2)}) copy-start(bf16[256,96]{1,0:T(8,128)(2,1)S(1)} %broadcast.319) | copy-start | bytes 147460
  315.6 3.9 copy-start.10
  397.7 7.4 copy-start.3
  410.7 4.7 copy-start.65
  413.7 21.7 %copy-start.30 = (bf16[256,1024]{1,0:T(8,128)(2,1)}, bf16[256,1024]{1,0:T(8,128)(2,1)S(1)}, u32[]{:S(2)}) copy-start(bf16[256,1024]{1,0:T(8,128)(2,1)S(1)} %multiply_convert_fusion) | copy-start | bytes 1572868
  519.0 638.9 %reduce-scatter.3.cloned.1.call-start = ((), (), s32[]{:S(2)}) async-start(), calls=%async_computation.2 | async-start | bytes 14155776 | tf_op jit(solution)/shard_map/reduce_scatter | solution.py:1095
  556.9 4.4 copy-start.40
  556.9 4.4 copy-start.42
  562.6 184.6 %copy-start.22 = (f32[256,1024]{1,0:T(8,128)}, f32[256,1024]{1,0:T(8,128)S(1)}, u32[]{:S(2)}) copy-start(f32[256,1024]{1,0:T(8,128)S(1)} %get-tuple-element.164) | copy-start | bytes 3145732
  575.8 8.2 copy-start.19
  598.0 14.6 %copy-start.13 = (bf16[1280,512]{0,1:T(8,128)(2,1)S(1)}, bf16[1280,512]{0,1:T(8,128)(2,1)}, u32[]{:S(2)}) copy-start(bf16[1280,512]{0,1:T(8,128)(2,1)} %copy.220) | copy-start | bytes 3932164
  612.6 3.9 copy-start.4
  612.6 4.9 copy-start.21
  627.2 4.2 copy-start.35
  634.5 108.7 %copy-start.11 = (f32[256,1024]{1,0:T(8,128)S(1)}, f32[256,1024]{1,0:T(8,128)}, u32[]{:S(2)}) copy-start(f32[256,1024]{1,0:T(8,128)} %copy-done.10) | copy-start | bytes 3145732
  634.5 108.7 %copy-start.49 = (bf16[256,1024]{1,0:T(8,128)(2,1)S(1)}, bf16[256,1024]{1,0:T(8,128)(2,1)}, u32[]{:S(2)}) copy-start(bf16[256,1024]{1,0:T(8,128)(2,1)} %copy.232) | copy-start | bytes 1572868
  743.2 3.9 copy-start.45
  808.4 23.0 %copy-start.56 = (f32[256,16]{1,0:T(8,128)S(1)}, f32[256,16]{1,0:T(8,128)}, u32[]{:S(2)}) copy-start(f32[256,16]{1,0:T(8,128)} %get-tuple-element.147) | copy-start | bytes 49156
  808.6 25.2 %copy-start.29 = (bf16[256,1024]{1,0:T(8,128)(2,1)S(1)}, bf16[256,1024]{1,0:T(8,128)(2,1)}, u32[]{:S(2)}) copy-start(bf16[256,1024]{1,0:T(8,128)(2,1)} %copy-done.28) | copy-start | bytes 1572868
  811.3 23.6 %copy-start.7 = (f32[256,1024]{1,0:T(8,128)S(1)}, f32[256,1024]{1,0:T(8,128)}, u32[]{:S(2)}) copy-start(f32[256,1024]{1,0:T(8,128)} %copy-done.6) | copy-start | bytes 3145732
  811.3 23.6 %copy-start.70 = (f32[1,1024]{1,0:T(1,128)S(1)}, f32[1,1024]{1,0:T(1,128)}, u32[]{:S(2)}) copy-start(f32[1,1024]{1,0:T(1,128)} %copy-done.69) | copy-start | bytes 12292
  811.3 23.6 %copy-start.79 = (f32[256]{0:T(256)S(1)}, f32[256]{0:T(256)}, u32[]{:S(2)}) copy-start(f32[256]{0:T(256)} %copy-done.78) | copy-start | bytes 3076
  832.6 5.0 copy-start.83
  852.7 8.5 copy-start.18
  874.8 15.4 %copy-start.12 = (bf16[1280,512]{0,1:T(8,128)(2,1)S(1)}, bf16[1280,512]{0,1:T(8,128)(2,1)}, u32[]{:S(2)}) copy-start(bf16[1280,512]{0,1:T(8,128)(2,1)} %copy.212) | copy-start | bytes 3932164
  890.2 4.0 copy-start.5
  890.3 5.0 copy-start.20
  904.9 4.2 copy-start.36
  912.3 59.2 %copy-start.9 = (f32[256,1024]{1,0:T(8,128)S(1)}, f32[256,1024]{1,0:T(8,128)}, u32[]{:S(2)}) copy-start(f32[256,1024]{1,0:T(8,128)} %param.22) | copy-start | bytes 3145732
  912.3 59.2 %copy-start.51 = (bf16[256,1024]{1,0:T(8,128)(2,1)S(1)}, bf16[256,1024]{1,0:T(8,128)(2,1)}, u32[]{:S(2)}) copy-start(bf16[256,1024]{1,0:T(8,128)(2,1)} %copy.239) | copy-start | bytes 1572868
  912.3 59.2 %copy-start.68 = (f32[1,1024]{1,0:T(1,128)S(1)}, f32[1,1024]{1,0:T(1,128)}, u32[]{:S(2)}) copy-start(f32[1,1024]{1,0:T(1,128)} %copy-done.67) | copy-start | bytes 12292
  912.3 59.2 %copy-start.74 = (f32[256]{0:T(256)S(1)}, f32[256]{0:T(256)}, u32[]{:S(2)}) copy-start(f32[256]{0:T(256)} %copy-done.73) | copy-start | bytes 3076
  971.5 4.9 copy-start.47
  971.5 6.6 copy-start.58
  976.5 4.3 copy-start.23
  1135.0 4.9 copy-start.81
  1135.1 4.9 copy-start.85
  1135.1 4.9 copy-start.86
  1135.1 4.9 copy-start.87
  1135.1 5.5 copy-start.72
  1135.1 5.5 copy-start.76
  1135.1 5.5 copy-start.77
  1138.5 4.1 copy-start.26
  1138.5 4.1 copy-start.57
  1144.8 4.1 copy-start.55
  1156.4 4.0 copy-start.27
  1160.5 6.7 copy-start.15
  1160.5 6.7 copy-start.38
  1160.5 8.2 copy-start.39
  1168.7 7.4 copy-start.1
  (28 other events, 64.8 us)
Sparse Core Ops, SparseCore 0:
  12.0 237.3 all-gather.4
  252.2 196.1 all-gather.6
  519.1 290.0 reduce-scatter.4
  812.6 256.2 reduce-scatter.2

commit v4 on v3

--- a/solution.py
+++ b/solution.py
@@ -228,94 +228,119 @@
 
 
 def gather_dense_kernel(
-    n, rows, x_ref, o_ref, ring_send, ring_recv, pair_send, pair_recv, own_sem
+    n, owners, rows, x_ref, o_ref,
+    ring_send, ring_recv, pair_send, pair_recv, far_send, far_recv, own_sem,
 ):
     e, s = lax.axis_index("expert"), lax.axis_index("shard")
-    core = lax.rem(e, 2)
-    partner = e + 1 - 2 * core
+    partner = e + 1 - 2 * lax.rem(e, 2)
+    chips = owners // 2
     p = ring_place(s, n)
     ways = (ring_shard(lax.rem(p + 1, n), n), ring_shard(lax.rem(p + n - 1, n), n))
     barrier = pltpu.get_barrier_semaphore()
     signal(barrier, {"expert": partner})
     signal(barrier, {"shard": ways[0]})
     signal(barrier, {"shard": ways[1]})
-    pl.semaphore_wait(barrier, 3)
-    quarter = rows // 4
-
-    def part(side, way):
-        return pl.ds(pl.multiple_of(side * 2 * quarter + way * quarter, quarter), quarter)
-
-    def block(way, k):
-        return ring_shard(lax.rem(p + (n - k if way == 0 else k), n), n)
+    for d in range(1, chips):
+        signal(barrier, {"expert": lax.rem(e + 2 * d, owners)})
+    pl.semaphore_wait(barrier, 2 + chips)
+    half, wide = rows // 2, x_ref.shape[1] // owners
+
+    def columns(owner):
+        return pl.ds(pl.multiple_of(owner * wide, 128), wide)
+
+    def region(way, k, owner):
+        block = ring_shard(lax.rem(p + (n - k if way == 0 else k), n), n)
+        return o_ref.at[block, pl.ds(way * half, half), columns(owner)]
 
     def ring_copy(way, k, src):
         return pltpu.make_async_remote_copy(
             src_ref=src,
-            dst_ref=o_ref.at[block(way, k), part(core, way)],
+            dst_ref=region(way, k, e),
             send_sem=ring_send.at[way, k],
             recv_sem=ring_recv.at[way, k],
             device_id={"shard": ways[way]},
             device_id_type=MESH,
         )
 
-    def pair_copy(way, k, side):
-        there = o_ref.at[block(way, k), part(side, way)]
+    def far_copy(d, way, k):
+        return pltpu.make_async_remote_copy(
+            src_ref=region(way, k, e),
+            dst_ref=region(way, k, e),
+            send_sem=far_send.at[d - 1, way, k - 1],
+            recv_sem=far_recv.at[d - 1, way, k - 1],
+            device_id={"expert": lax.rem(e + 2 * d, owners)},
+            device_id_type=MESH,
+        )
+
+    def pair_copy(d, way, k):
+        there = region(way, k, lax.rem(e + owners - 2 * d, owners))
         return pltpu.make_async_remote_copy(
             src_ref=there,
             dst_ref=there,
-            send_sem=pair_send.at[way, k - 1],
-            recv_sem=pair_recv.at[way, k - 1],
+            send_sem=pair_send.at[d, way, k - 1],
+            recv_sem=pair_recv.at[d, way, k - 1],
             device_id={"expert": partner},
             device_id_type=MESH,
         )
 
+    def hand_on(k):
+        for way in range(2):
+            for d in range(1, chips):
+                far_copy(d, way, k).wait_recv()
+                pair_copy(d, way, k).start()
+
     for way in range(2):
-        ring_copy(way, 0, x_ref.at[part(core, way)]).start()
+        ring_copy(way, 0, x_ref.at[pl.ds(way * half, half), columns(e)]).start()
     own = pltpu.make_async_copy(x_ref, o_ref.at[s], own_sem)
     own.start()
 
     def step(k, carry):
         for way in range(2):
-            came = o_ref.at[block(way, k), part(core, way)]
-            pltpu.make_async_remote_copy(
-                src_ref=came,
-                dst_ref=came,
-                send_sem=ring_send.at[way, k - 1],
-                recv_sem=ring_recv.at[way, k - 1],
-                device_id={"shard": ways[way]},
-                device_id_type=MESH,
-            ).wait_recv()
+            came = region(way, k, e)
+            ring_copy(way, k - 1, came).wait_recv()
 
             @pl.when(k < n - 1)
             def _():
                 ring_copy(way, k, came).start()
 
-            pair_copy(way, k, core).start()
+            for d in range(1, chips):
+                far_copy(d, way, k).start()
+            pair_copy(0, way, k).start()
+
+        @pl.when(k > 1)
+        def _():
+            hand_on(k - 1)
+
         return carry
 
     lax.fori_loop(1, n, step, 0)
+    hand_on(n - 1)
 
     def finish(k, carry):
         for way in range(2):
-            ring_copy(way, k - 1, x_ref.at[part(core, way)]).wait_send()
-            pair_copy(way, k, core).wait_send()
-            pair_copy(way, k, 1 - core).wait_recv()
+            ring_copy(way, k - 1, region(way, k, e)).wait_send()
+            for d in range(chips):
+                pair_copy(d, way, k).wait()
+            for d in range(1, chips):
+                far_copy(d, way, k).wait_send()
         return carry
 
     lax.fori_loop(1, n, finish, 0)
     own.wait()
 
 
-def gather_dense(piece, n):
+def gather_dense(piece, n, owners):
     rows, columns = piece.shape
     dma = pltpu.SemaphoreType.DMA
+    chips = owners // 2
     return pl.pallas_call(
-        functools.partial(gather_dense_kernel, n, rows),
+        functools.partial(gather_dense_kernel, n, owners, rows),
         out_shape=jax.ShapeDtypeStruct((n, rows, columns), piece.dtype),
         in_specs=[pl.BlockSpec(memory_space=pltpu.VMEM)],
         out_specs=pl.BlockSpec(memory_space=pl.ANY),
         scratch_shapes=[
-            dma((2, n - 1)), dma((2, n - 1)), dma((2, n - 1)), dma((2, n - 1)), dma,
+            dma((2, n - 1)), dma((2, n - 1)), dma((chips, 2, n - 1)), dma((chips, 2, n - 1)),
+            dma((chips - 1, 2, n - 1)), dma((chips - 1, 2, n - 1)), dma,
         ],
         compiler_params=pltpu.CompilerParams(
             collective_id=3, has_side_effects=True, vmem_limit_bytes=VMEM_LIMIT
@@ -747,6 +772,105 @@
         ),
         name="halo_back",
     )(grads)
+
+
+def attend_kernel(q_ref, k_ref, v_ref, bias_ref, o_ref, total_ref):
+    for h in range(q_ref.shape[1] // HEAD):
+        at = pl.ds(h * HEAD, HEAD)
+        kv_at = pl.ds(h // (HEADS // KV_HEADS) * HEAD, HEAD)
+        query = q_ref[:, at] * jnp.asarray(HEAD**-0.5, BF16)
+        scores = outer_cols(k_ref[:, kv_at], query) + bias_ref[...]
+        top = jnp.max(scores, axis=0, keepdims=True)
+        powers = jnp.exp(scores - top)
+        total = jnp.sum(powers, axis=0, keepdims=True)
+        value = inner_rows(v_ref[:, kv_at], powers.astype(BF16)) / total
+        o_ref[:, at] = value.T.astype(BF16)
+        total_ref[0, h : h + 1, :] = top + jnp.log(total)
+
+
+def attention_specs(tok_rows, key_count):
+    span = 2 * HEAD
+    groups = HEADS // KV_HEADS
+    steps = KV_HEADS // 2
+    return steps, [
+        pl.BlockSpec((tok_rows, groups * span), lambda j: (0, j)),
+        pl.BlockSpec((key_count, span), lambda j: (0, j)),
+        pl.BlockSpec((key_count, span), lambda j: (0, j + steps)),
+        pl.BlockSpec((key_count, tok_rows), lambda j: (0, 0)),
+    ]
+
+
+def attend(qkv_rows, ext, bias):
+    key_count, tok_rows = bias.shape
+    steps, specs = attention_specs(tok_rows, key_count)
+    return pl.pallas_call(
+        attend_kernel,
+        grid=(steps,),
+        in_specs=specs,
+        out_specs=[specs[0], pl.BlockSpec((1, 8, tok_rows), lambda j: (j, 0, 0))],
+        out_shape=[
+            jax.ShapeDtypeStruct((tok_rows, HEADS * HEAD), BF16),
+            jax.ShapeDtypeStruct((steps, 8, tok_rows), F32),
+        ],
+        compiler_params=pltpu.CompilerParams(vmem_limit_bytes=VMEM_LIMIT),
+        cost_estimate=pl.CostEstimate(
+            flops=4 * HEADS * HEAD * tok_rows * key_count,
+            bytes_accessed=4 * key_count * tok_rows + 4 * key_count * KV_HEADS * HEAD,
+            transcendentals=HEADS * tok_rows * key_count,
+        ),
+        name="attend",
+    )(qkv_rows, ext, ext, bias)
+
+
+def attend_back_kernel(
+    q_ref, k_ref, v_ref, bias_ref, d_ref, total_ref, d_query_ref, d_kv_ref
+):
+    groups = HEADS // KV_HEADS
+    scale = jnp.asarray(HEAD**-0.5, BF16)
+    span = k_ref.shape[1]
+    for kv in range(span // HEAD):
+        kv_at = pl.ds(kv * HEAD, HEAD)
+        key, value = k_ref[:, kv_at], v_ref[:, kv_at]
+        d_key = d_value = None
+        for h in range(kv * groups, (kv + 1) * groups):
+            at = pl.ds(h * HEAD, HEAD)
+            query = q_ref[:, at] * scale
+            d_out = d_ref[:, at]
+            scores = outer_cols(key, query) + bias_ref[...]
+            probs = jnp.exp(scores - total_ref[0, h : h + 1, :])
+            d_probs = outer_cols(value, d_out)
+            mean_d = jnp.sum(probs * d_probs, axis=0, keepdims=True)
+            d_scores = (probs * (d_probs - mean_d)).astype(BF16)
+            d_query = inner_rows(key, d_scores) * (HEAD**-0.5)
+            d_query_ref[:, at] = d_query.T.astype(BF16)
+            more_key = jnp.dot(d_scores, query, preferred_element_type=F32)
+            more_value = jnp.dot(probs.astype(BF16), d_out, preferred_element_type=F32)
+            d_key = more_key if d_key is None else d_key + more_key
+            d_value = more_value if d_value is None else d_value + more_value
+        d_kv_ref[:, kv * HEAD : (kv + 1) * HEAD] = d_key.astype(BF16)
+        d_kv_ref[:, span + kv * HEAD : span + (kv + 1) * HEAD] = d_value.astype(BF16)
+
+
+def attend_back(qkv_rows, ext, bias, d_attended, totals):
+    key_count, tok_rows = bias.shape
+    steps, specs = attention_specs(tok_rows, key_count)
+    return pl.pallas_call(
+        attend_back_kernel,
+        grid=(steps,),
+        in_specs=specs + [specs[0], pl.BlockSpec((1, 8, tok_rows), lambda j: (j, 0, 0))],
+        out_specs=[specs[0], pl.BlockSpec((key_count, 4 * HEAD), lambda j: (0, j))],
+        out_shape=[
+            jax.ShapeDtypeStruct((tok_rows, HEADS * HEAD), BF16),
+            jax.ShapeDtypeStruct((key_count, 2 * KV_HEADS * HEAD), BF16),
+        ],
+        compiler_params=pltpu.CompilerParams(vmem_limit_bytes=VMEM_LIMIT),
+        cost_estimate=pl.CostEstimate(
+            flops=10 * HEADS * HEAD * tok_rows * key_count,
+            bytes_accessed=4 * key_count * tok_rows + 8 * key_count * KV_HEADS * HEAD,
+            transcendentals=HEADS * tok_rows * key_count,
+        ),
+        name="attend_back",
+    )(qkv_rows, ext, ext, bias, d_attended, totals)
 
 
 def column_of(extra, index, experts_total):
@@ -966,8 +1090,6 @@
     q_width = HEADS * HEAD
     kv_width = KV_HEADS * HEAD
     qkv_width = q_width + 2 * kv_width
-    groups = HEADS // KV_HEADS
-    score_scale = HEAD ** (-0.5)
     extra = -(-2 * experts_total // 128) * 128
     my_owner = lax.axis_index("expert")
     first_expert = my_owner * local_experts
@@ -981,15 +1103,17 @@
         (query_rows[:, None] % seq_len >= doc_ends[None, :]).astype(jnp.int32), axis=1
     )
     key_docs = jnp.sum((key_rows[:, None] % seq_len >= doc_ends[None, :]).astype(jnp.int32), axis=1)
-    distance = query_rows[:, None] - key_rows[None, :]
+    distance = query_rows[None, :] - key_rows[:, None]
     allowed = (
-        (query_rows[:, None] // seq_len == key_rows[None, :] // seq_len)
-        & (query_docs[:, None] == key_docs[None, :])
+        (query_rows[None, :] // seq_len == key_rows[:, None] // seq_len)
+        & (query_docs[None, :] == key_docs[:, None])
         & (distance >= 0)
         & (distance < WINDOW)
     )
+    bias = jnp.where(allowed, 0.0, masked_score).astype(F32)
     expert_ids = jnp.arange(experts_total, dtype=jnp.int32)
     side = 128
+    layer_columns = qkv_width + width
 
     def dense_piece():
         rows = w_qkv.shape[1]
@@ -998,7 +1122,8 @@
             parts += [w_qkv[layer_no].astype(BF16), w_out[layer_no].astype(BF16)]
         for layer_no in range(LAYERS):
             parts += [router[layer_no].astype(BF16), gains[layer_no].T.astype(BF16)]
-        parts.append(jnp.zeros((rows, side - LAYERS * (experts_total + 2)), BF16))
+        filled = LAYERS * (layer_columns + experts_total + 2)
+        parts.append(jnp.zeros((rows, -filled % (128 * owners)), BF16))
         return jnp.concatenate(parts, 1)
 
     def expert_piece(layer_no):
@@ -1006,13 +1131,12 @@
             [w_in[layer_no].astype(BF16), w_down[layer_no].astype(BF16)], 1
         )
 
-    layer_columns = qkv_width + width
     expert_full = []
     for layer_no in range(LAYERS):
         expert_full.append(
             lax.all_gather(expert_piece(layer_no), "shard", axis=0, tiled=False)
         )
-    dense = gather_dense(dense_piece(), shards).reshape(width, -1)
+    dense = gather_dense(dense_piece(), shards, owners).reshape(width, -1)
 
     kept_layers = []
     stream = hidden_in
@@ -1026,23 +1150,8 @@
         gain_pair = small[:, experts_total : experts_total + 2].astype(F32).T
         normed_one = rms_scale(stream, gain_pair[0]).astype(BF16)
         qkv_rows = jnp.dot(normed_one, w_qkv_full, preferred_element_type=F32).astype(BF16)
-        queries = qkv_rows[:, :q_width].reshape(tok_rows, KV_HEADS, groups, HEAD)
         ext = halo(qkv_rows[:, q_width:], shards, hop_count + 1).reshape(key_count, 2 * kv_width)
-        ext_keys = ext[:, :kv_width].reshape(key_count, KV_HEADS, HEAD)
-        ext_values = ext[:, kv_width:].reshape(key_count, KV_HEADS, HEAD)
-        scores = (
-            jnp.einsum("tngd,snd->ngts", queries, ext_keys, preferred_element_type=F32)
-            * score_scale
-        )
-        masked = jnp.where(allowed, scores, masked_score)
-        row_top = jnp.max(masked, axis=-1, keepdims=True)
-        log_total = row_top + jnp.log(jnp.sum(jnp.exp(masked - row_top), axis=-1, keepdims=True))
-        prob_rows = jnp.exp(masked - log_total).astype(BF16)
-        attended = (
-            jnp.einsum("ngts,snd->tngd", prob_rows, ext_values, preferred_element_type=F32)
-            .astype(BF16)
-            .reshape(tok_rows, q_width)
-        )
+        attended, log_total = attend(qkv_rows, ext, bias)
         mixed = stream + jnp.dot(attended, w_out_full, preferred_element_type=F32)
         normed_two = rms_scale(mixed, gain_pair[1]).astype(BF16)
         logits = jnp.dot(normed_two, router_full, preferred_element_type=F32)
@@ -1056,7 +1165,7 @@
             [normed_two, high, low, jnp.zeros((tok_rows, extra - 2 * experts_total), BF16)], 1
         )
         x_all = spread(wide_rows, owners, 1).reshape(owners * tok_rows, width + extra)
-        if layer_no + 1 == LAYERS:
+        if layer_no == 0:
             g_rows, x_all = lax.optimization_barrier((cotangent.astype(BF16), x_all))
             g_all = spread(g_rows, owners, 8).reshape(owners * tok_rows, width)
             g_all, x_all = lax.optimization_barrier((g_all, x_all))
@@ -1071,7 +1180,7 @@
         moe_out = collect(partial.reshape(owners, tok_rows, width), 2)
         kept_layers.append(
             (
-                stream, normed_one, queries, ext_keys, ext_values, log_total, attended, mixed,
+                stream, normed_one, qkv_rows, ext, log_total, attended, mixed,
                 x_all, gate_up, normed_two, weights, w_qkv_full, w_out_full, router_full,
                 gain_pair,
             )
@@ -1083,7 +1192,7 @@
     small_parts = [None] * LAYERS
     for layer_no in reversed(range(LAYERS)):
         (
-            layer_input, normed_one, queries, ext_keys, ext_values, log_total, attended, mixed,
+            layer_input, normed_one, qkv_rows, ext, log_total, attended, mixed,
             x_all, gate_up, normed_two, weights, w_qkv_full, w_out_full, router_full,
             gain_pair,
         ) = kept_layers[layer_no]
@@ -1107,34 +1216,18 @@
         grad_mixed = grad_stream + d_mixed_norm
         d_att = grad_mixed.astype(BF16)
         d_w_out = inner_rows(attended, d_att)
-        d_attended = (
-            outer_cols(d_att, w_out_full).astype(BF16).reshape(tok_rows, KV_HEADS, groups, HEAD)
-        )
-        scores = (
-            jnp.einsum("tngd,snd->ngts", queries, ext_keys, preferred_element_type=F32)
-            * score_scale
-        )
-        prob_rows = jnp.exp(jnp.where(allowed, scores, masked_score) - log_total)
-        d_probs = jnp.einsum("tngd,snd->ngts", d_attended, ext_values, preferred_element_type=F32)
-        d_scores = (
-            prob_rows * (d_probs - jnp.sum(prob_rows * d_probs, axis=-1, keepdims=True))
-        ).astype(BF16)
-        d_queries = (
-            jnp.einsum("ngts,snd->tngd", d_scores, ext_keys, preferred_element_type=F32)
-            * score_scale
-        )
-        d_keys = (
-            jnp.einsum("ngts,tngd->snd", d_scores, queries, preferred_element_type=F32)
-            * score_scale
-        )
-        d_values = jnp.einsum(
-            "ngts,tngd->snd", prob_rows.astype(BF16), d_attended, preferred_element_type=F32
-        )
-        blocks = jnp.concatenate(
-            [d_keys.reshape(key_count, kv_width), d_values.reshape(key_count, kv_width)], 1
-        ).reshape(hop_count + 1, tok_rows, 2 * kv_width)
-        carried = halo_back(blocks.astype(BF16), shards)
-        d_qkv = jnp.concatenate([d_queries.reshape(tok_rows, q_width), carried], 1).astype(BF16)
+        d_attended = outer_cols(d_att, w_out_full).astype(BF16)
+        d_queries, d_kv = attend_back(qkv_rows, ext, bias, d_attended, log_total)
+        d_kv = halo_back(d_kv.reshape(hop_count + 1, tok_rows, 2 * kv_width), shards)
+        d_kv = d_kv.astype(BF16).reshape(tok_rows, KV_HEADS // 2, 2, 2 * HEAD)
+        d_qkv = jnp.concatenate(
+            [
+                d_queries,
+                d_kv[:, :, 0].reshape(tok_rows, kv_width),
+                d_kv[:, :, 1].reshape(tok_rows, kv_width),
+            ],
+            1,
+        )
         d_w_qkv = inner_rows(normed_one, d_qkv)
         d_normed_one = outer_cols(d_qkv, w_qkv_full)
         _, norm_back = jax.vjp(rms_scale, layer_input, gain_pair[0])

time: 1190 us -> 1110 us (0.933)
  matrix products: 133 us -> 48.5 us
  Pallas kernels: 849 us -> 897 us
  local copies, waits for them, and re-layouts: 93.5 us -> 50.7 us
  waiting for transfers between devices: 0.13 us -> 37.7 us
  other arithmetic: 91.9 us -> 54.7 us
    dot_general x12 -> x0, matrix products: 86.6 us -> none  [the longest x2 27.5 us: on_device(): jnp.einsum('tngd,snd->ngts', d_attended, ext_values, preferred_element_ty...]
    all_gather x2, waiting for transfers between devices: 0.04 us -> 37.6 us  [on_device(): lax.all_gather(expert_piece(layer_no), 'shard', axis=0, tiled=False)]
    pallas_call x1, Pallas kernels: 142 us -> 178 us  [reduce_dense(): pl.pallas_call(functools.partial(reduce_dense_kernel, n, owners, rows, tu...]
    concatenate x8 -> x0, local copies, waits for them, and re-layouts: 29.8 us -> none  [on_device(): jnp.concatenate([d_keys.reshape(key_count, kv_width), d_values.reshape(ke...]
    convert_element_type x2, other arithmetic: 30 us -> 3.39 us  [on_device(): d_kv = d_kv.astype(BF16).reshape(tok_rows, KV_HEADS // 2, 2, 2 * HEAD)]
    pallas_call x2, Pallas kernels: 165 us -> 146 us  [halo_back(): pl.pallas_call(functools.partial(halo_back_kernel, n, rows, cuts), out_sh...]
    pallas_call x1 -> x5, Pallas kernels: 168 us -> 183 us  [the longest x1 105 us: gather_dense(): pl.pallas_call(functools.partial(gather_dense_kernel, n, owners, rows), o...]
    pallas_call x2, Pallas kernels: 93.5 us -> 106 us  [halo(): pl.pallas_call(functools.partial(halo_kernel, n, rows, cuts), out_shape=j...]
  transfers between devices with their start and end apart: 4 -> 4, of which waited for: 0 -> 2; matrix products, arithmetic and copies ran while one was open for 23% -> 11% of each run, Pallas kernels for 66% -> 75%
where the time goes in v4:
time: 1110 us; the launch traced here: 1100 us
  Pallas kernels  897 us (81%)
  other arithmetic  54.7 us (5%)
  local copies, waits for them, and re-layouts  50.7 us (5%)
  matrix products  48.5 us (4%)
  waiting for transfers between devices  37.7 us (3%)
  between operations  15.6 us (1%)
    pallas_call x1, Pallas kernels, reduce_dense(): pl.pallas_call(functools.partial(reduce_dense_kernel, n, owners, rows, tu...  178 us
    pallas_call x2, Pallas kernels, halo_back(): pl.pallas_call(functools.partial(halo_back_kernel, n, rows, cuts), out_sh...  146 us
    pallas_call x2, Pallas kernels, halo(): pl.pallas_call(functools.partial(halo_kernel, n, rows, cuts), out_shape=j...  106 us
    pallas_call x1, Pallas kernels, gather_dense(): pl.pallas_call(functools.partial(gather_dense_kernel, n, owners, rows), o...  105 us
    pallas_call x2, Pallas kernels, ffn_backward(): pl.pallas_call(functools.partial(ffn_backward_kernel, 256, width, in_rows...  84.7 us
    pallas_call x4, Pallas kernels, collect(): pl.pallas_call(functools.partial(collect_kernel, owners, cuts), out_shape...  78.4 us
    pallas_call x4, Pallas kernels, spread(): pl.pallas_call(functools.partial(spread_kernel, owners, cuts), out_shape=...  73.7 us
    pallas_call x2, Pallas kernels, ffn_forward(): pl.pallas_call(functools.partial(ffn_forward_kernel, 256, width, in_rows,...  46.7 us
  transfers between devices with their start and end apart: 4, of which 2 were waited for; matrix products, arithmetic and copies ran while one was open for 11% of the time, Pallas kernels for 75%

profile of v4, /device:TPU:0, one launch (start us, length us, event | category | flops | bytes accessed | tf_op | source)
XLA Modules:
  0.0 1104.9 jit_solution(7387595077521682691)
XLA Ops:
  7.3 1.9 convert.53
  11.9 2.6 pad_maximum_fusion.2
  16.6 2.0 concatenate.25.x_ref
  18.5 104.5 %gather_dense.1 = bf16[8,128,6656]{2,1,0:T(8,128)(2,1)} custom-call(bf16[128,6656]{1,0:T(8,128)(2,1)} %concatenate.25.x_ref), custom_call_target="tpu_custom_call" | custom-call | tf_op jit(solution)/shard_map/gather_dense/pallas_call | solution.py:336
  123.1 2.1 slice_convert_fusion
  126.1 3.5 fusion.9.q_ref
  130.5 30.2 %halo.2 = bf16[5,256,1024]{2,1,0:T(8,128)(2,1)} custom-call(bf16[256,1024]{1,0:T(8,128)(2,1)} %slice.245.kv_ref), custom_call_target="tpu_custom_call" | custom-call | tf_op jit(solution)/shard_map/halo/pallas_call | solution.py:642
  162.2 1.8 fusion.33.bias_ref
  164.0 16.8 %attend.2 = (bf16[256,1024]{1,0:T(8,128)(2,1)}, f32[4,8,256]{2,1,0:T(8,128)}) custom-call(bf16[256,2048]{1,0:T(8,128)(2,1)} %copy-done.46, bf16[1280,1024]{1,0:T(8,128)(2,1)} %bitcast.127, bf16[1280,1024]{1,0:T(8,128)(2,1)} %bitcast.128, f32[1280,256]{1,0:T(8,128)} %fusion.33.bias_ref), custom_call_target="tpu_custom_call" | custom-call | flops 1342177280 | bytes 3932160 | tf_op jit(solution)/shard_map/attend/pallas_call | solution.py:806
  180.8 2.6 multiply_reduce_fusion.10
  187.1 18.7 %spread.4 = bf16[4,256,1152]{2,1,0:T(8,128)(2,1)} custom-call(bf16[256,1152]{1,0:T(8,128)(2,1)} %concatenate.26.x_ref), custom_call_target="tpu_custom_call" | custom-call | tf_op jit(solution)/shard_map/spread/pallas_call | solution.py:125
  205.9 17.9 %spread.5 = bf16[4,256,1024]{2,1,0:T(8,128)(2,1)} custom-call(bf16[256,1024]{1,0:T(8,128)(2,1)} %convert_element_type.169.x_ref), custom_call_target="tpu_custom_call" | custom-call | tf_op jit(solution)/shard_map/spread/pallas_call | solution.py:125
  224.2 5.1 all-gather.5.cloned.1.call-done
  229.2 23.3 %ffn_forward.2 = (bf16[1024,1024]{1,0:T(8,128)(2,1)}, bf16[4,1024,1024]{2,1,0:T(8,128)(2,1)}) custom-call(s32[1]{0:T(128)} %bitcast.16.first_ref, bf16[1024,1152]{1,0:T(8,128)(2,1)} %bitcast.135, bf16[8,4,192,1024]{3,2,1,0:T(8,128)(2,1)} %bitcast.172), custom_call_target="tpu_custom_call" | custom-call | flops 12884901888 | bytes 25690112 | tf_op jit(solution)/shard_map/ffn_forward/pallas_call | solution.py:917
  252.6 18.6 %collect.4 = f32[256,1024]{1,0:T(8,128)} custom-call(bf16[4,256,1024]{2,1,0:T(8,128)(2,1)} %bitcast.144), custom_call_target="tpu_custom_call" | custom-call | tf_op jit(solution)/shard_map/collect/pallas_call | solution.py:202
  271.2 1.5 multiply_reduce_fusion.9
  272.7 3.5 fusion.12.q_ref
  278.1 75.7 %halo.3 = bf16[5,256,1024]{2,1,0:T(8,128)(2,1)} custom-call(bf16[256,1024]{1,0:T(8,128)(2,1)} %slice.254.kv_ref), custom_call_target="tpu_custom_call" | custom-call | tf_op jit(solution)/shard_map/halo/pallas_call | solution.py:642
  353.8 16.8 %attend.3 = (bf16[256,1024]{1,0:T(8,128)(2,1)}, f32[4,8,256]{2,1,0:T(8,128)}) custom-call(bf16[256,2048]{1,0:T(8,128)(2,1)} %copy-done.47, bf16[1280,1024]{1,0:T(8,128)(2,1)} %bitcast.131, bf16[1280,1024]{1,0:T(8,128)(2,1)} %bitcast.132, f32[1280,256]{1,0:T(8,128)} %fusion.33.bias_ref), custom_call_target="tpu_custom_call" | custom-call | flops 1342177280 | bytes 3932160 | tf_op jit(solution)/shard_map/attend/pallas_call | solution.py:806
  370.6 2.6 multiply_reduce_fusion.8
  377.3 1.6 subtract_convert_fusion
  378.9 1.9 concatenate.28.x_ref
  380.8 19.3 %spread.6 = bf16[4,256,1152]{2,1,0:T(8,128)(2,1)} custom-call(bf16[256,1152]{1,0:T(8,128)(2,1)} %concatenate.28.x_ref), custom_call_target="tpu_custom_call" | custom-call | tf_op jit(solution)/shard_map/spread/pallas_call | solution.py:125
  400.1 32.5 %all-gather.7.cloned.1.call-done = bf16[32,192,1024]{2,1,0:T(8,128)(2,1)} async-done(((bf16[4,192,1024]{2,1,0:T(8,128)(2,1)}), bf16[32,192,1024]{2,1,0:T(8,128)(2,1)}) %all-gather.7.cloned.1.call-update) | async-done | bytes 12582928 | tf_op jit(solution)/shard_map/all_gather | solution.py:1137
  432.6 23.3 %ffn_forward.3 = (bf16[1024,1024]{1,0:T(8,128)(2,1)}, bf16[4,1024,1024]{2,1,0:T(8,128)(2,1)}) custom-call(s32[1]{0:T(128)} %bitcast.16.first_ref, bf16[1024,1152]{1,0:T(8,128)(2,1)} %bitcast.139, bf16[8,4,192,1024]{3,2,1,0:T(8,128)(2,1)} %bitcast.174), custom_call_target="tpu_custom_call" | custom-call | flops 12884901888 | bytes 25690112 | tf_op jit(solution)/shard_map/ffn_forward/pallas_call | solution.py:917
  456.0 42.5 %ffn_backward.2 = (bf16[1024,1152]{1,0:T(8,128)(2,1)}, bf16[8,4,192,1024]{3,2,1,0:T(8,128)(2,1)}) custom-call(s32[1]{0:T(128)} %bitcast.16.first_ref, bf16[1024,1152]{1,0:T(8,128)(2,1)} %bitcast.140, bf16[1024,1024]{1,0:T(8,128)(2,1)} %bitcast.141, bf16[4,1024,1024]{2,1,0:T(8,128)(2,1)} %get-tuple-element.56.gate_up_ref, bf16[8,4,192,1024]{3,2,1,0:T(8,128)(2,1)} %bitcast.175), custom_call_target="tpu_custom_call" | custom-call | flops 25769803776 | bytes 42991616 | tf_op jit(solution)/shard_map/ffn_backward/pallas_call | solution.py:1021
  498.5 22.9 %collect.6 = f32[256,1152]{1,0:T(8,128)} custom-call(bf16[4,256,1152]{2,1,0:T(8,128)(2,1)} %bitcast.137), custom_call_target="tpu_custom_call" | custom-call | tf_op jit(solution)/shard_map/collect/pallas_call | solution.py:202
  521.4 17.1 %collect.5 = f32[256,1024]{1,0:T(8,128)} custom-call(bf16[4,256,1024]{2,1,0:T(8,128)(2,1)} %bitcast.143), custom_call_target="tpu_custom_call" | custom-call | tf_op jit(solution)/shard_map/collect/pallas_call | solution.py:202
  538.5 1.4 multiply_reduce_fusion.13
  541.1 2.8 multiply_reduce_fusion
  546.2 3.2 fusion.37.d_ref
  549.4 22.5 %attend_back.2 = (bf16[256,1024]{1,0:T(8,128)(2,1)}, bf16[1280,1024]{1,0:T(8,128)(2,1)}) custom-call(bf16[256,2048]{1,0:T(8,128)(2,1)} %copy-done.47, bf16[1280,1024]{1,0:T(8,128)(2,1)} %bitcast.133, bf16[1280,1024]{1,0:T(8,128)(2,1)} %bitcast.134, f32[1280,256]{1,0:T(8,128)} %fusion.33.bias_ref, bf16[256,1024]{1,0:T(8,128)(2,1)} %fusion.37.d_ref, ...), custom_call_target="tpu_custom_call" | custom-call | flops 3355443200 | bytes 6553600 | tf_op jit(solution)/shard_map/attend_back/pallas_call | solution.py:857
  571.9 83.1 %halo_back.2 = f32[256,1024]{1,0:T(8,128)} custom-call(bf16[5,256,1024]{2,1,0:T(8,128)(2,1)} %bitcast.126), custom_call_target="tpu_custom_call" | custom-call | tf_op jit(solution)/shard_map/halo_back/pallas_call | solution.py:759
  655.0 2.1 convert_element_type.187
  657.1 2.2 reshape.372
  659.4 3.1 fusion.88
  662.5 2.0 copy.185
  665.6 1.9 copy.184
  667.5 1.8 copy.166
  669.3 4.6 multiply_reduce_fusion.1
  674.0 1.4 fusion.83
  675.4 17.8 %spread.7 = bf16[4,256,1024]{2,1,0:T(8,128)(2,1)} custom-call(bf16[256,1024]{1,0:T(8,128)(2,1)} %get-tuple-element.154.x_ref), custom_call_target="tpu_custom_call" | custom-call | tf_op jit(solution)/shard_map/spread/pallas_call | solution.py:125
  693.2 42.3 %ffn_backward.3 = (bf16[1024,1152]{1,0:T(8,128)(2,1)}, bf16[8,4,192,1024]{3,2,1,0:T(8,128)(2,1)}) custom-call(s32[1]{0:T(128)} %bitcast.16.first_ref, bf16[1024,1152]{1,0:T(8,128)(2,1)} %bitcast.136, bf16[1024,1024]{1,0:T(8,128)(2,1)} %bitcast.142, bf16[4,1024,1024]{2,1,0:T(8,128)(2,1)} %get-tuple-element.63.gate_up_ref, bf16[8,4,192,1024]{3,2,1,0:T(8,128)(2,1)} %bitcast.173), custom_call_target="tpu_custom_call" | custom-call | flops 25769803776 | bytes 42991616 | tf_op jit(solution)/shard_map/ffn_backward/pallas_call | solution.py:1021
  735.5 19.9 %collect.7 = f32[256,1152]{1,0:T(8,128)} custom-call(bf16[4,256,1152]{2,1,0:T(8,128)(2,1)} %bitcast.138), custom_call_target="tpu_custom_call" | custom-call | tf_op jit(solution)/shard_map/collect/pallas_call | solution.py:202
  757.9 1.9 multiply_reduce_fusion.2
  761.1 3.1 fusion.34.d_ref
  764.2 22.3 %attend_back.3 = (bf16[256,1024]{1,0:T(8,128)(2,1)}, bf16[1280,1024]{1,0:T(8,128)(2,1)}) custom-call(bf16[256,2048]{1,0:T(8,128)(2,1)} %copy-done.46, bf16[1280,1024]{1,0:T(8,128)(2,1)} %bitcast.129, bf16[1280,1024]{1,0:T(8,128)(2,1)} %bitcast.130, f32[1280,256]{1,0:T(8,128)} %fusion.33.bias_ref, bf16[256,1024]{1,0:T(8,128)(2,1)} %fusion.34.d_ref, ...), custom_call_target="tpu_custom_call" | custom-call | flops 3355443200 | bytes 6553600 | tf_op jit(solution)/shard_map/attend_back/pallas_call | solution.py:857
  786.5 63.4 %halo_back.3 = f32[256,1024]{1,0:T(8,128)} custom-call(bf16[5,256,1024]{2,1,0:T(8,128)(2,1)} %bitcast.125), custom_call_target="tpu_custom_call" | custom-call | tf_op jit(solution)/shard_map/halo_back/pallas_call | solution.py:759
  851.6 1.7 fusion.87
  853.3 1.5 copy.187
  854.9 2.0 copy.186
  859.1 5.4 multiply_reduce_fusion.3
  870.0 2.6 concatenate.32
  872.6 3.3 convolution_convert_fusion.3
  875.8 2.1 convolution_convert_fusion.2
  877.9 3.4 convolution_convert_fusion.1
  881.3 3.4 convolution_convert_fusion
  884.7 178.4 %reduce_dense.1 = bf16[128,6272]{1,0:T(8,128)(2,1)} custom-call(bf16[8,128,2048]{2,1,0:T(8,128)(2,1)} %bitcast.108, bf16[8,128,1024]{2,1,0:T(8,128)(2,1)} %bitcast.123, bf16[8,128,2048]{2,1,0:T(8,128)(2,1)} %bitcast.109, bf16[8,128,1024]{2,1,0:T(8,128)(2,1)} %bitcast.124, bf16[8,128,128]{2,1,0:T(8,128)(2,1)} %bitcast.149), custom_call_target="tpu_custom_call" | custom-call | tf_op jit(solution)/shard_map/reduce_dense/pallas_call | solution.py:496
  1063.3 1.7 convert_element_type.199
  1067.0 2.6 fusion.43
  1069.6 2.3 add_multiply_fusion.3
  1074.2 4.0 add_multiply_fusion.2
  1083.0 10.8 add_multiply_fusion
  1093.8 4.0 add_multiply_fusion.1
  (249 shorter events, 44.5 us)
Async XLA Ops:
  7.2 153.5 %copy-start = (s32[4,4]{1,0:T(4,128)S(1)}, s32[4,4]{1,0:T(4,128)}, u32[]{:S(2)}) copy-start(s32[4,4]{1,0:T(4,128)} %param.24) | copy-start | bytes 196
  7.2 222.0 %all-gather.5.cloned.1.call-start = ((), (), s32[]{:S(2)}) async-start(), calls=%async_computation.4 | async-start | bytes 14155776 | tf_op jit(solution)/shard_map/all_gather | solution.py:1137
  7.3 2.8 copy-start.2
  11.9 420.7 %all-gather.7.cloned.1.call-start = ((), (), s32[]{:S(2)}) async-start(), calls=%async_computation.5 | async-start | bytes 14155776 | tf_op jit(solution)/shard_map/all_gather | solution.py:1137
  11.9 2.7 copy-start.18
  14.5 1063.6 %reduce-scatter.5.cloned.1.call-start = ((), (), s32[]{:S(2)}) async-start(), calls=%async_computation.3 | async-start | bytes 14155776 | tf_op jit(solution)/shard_map/reduce_scatter | solution.py:1204
  123.1 2.3 copy-start.3
  125.6 4.1 copy-start.50
  129.7 31.1 %copy-start.46 = (bf16[256,2048]{1,0:T(8,128)(2,1)}, bf16[256,2048]{1,0:T(8,128)(2,1)S(1)}, u32[]{:S(2)}) copy-start(bf16[256,2048]{1,0:T(8,128)(2,1)S(1)} %fusion.9.q_ref) | copy-start | bytes 3145732
  129.7 31.3 %copy-start.22 = (f32[256,1024]{1,0:T(8,128)S(1)}, f32[256,1024]{1,0:T(8,128)}, u32[]{:S(2)}) copy-start(f32[256,1024]{1,0:T(8,128)} %param.23) | copy-start | bytes 3145732
  130.5 31.3 %copy-start.54 = (s32[2,256,8]{1,2,0:T(8,128)S(1)}, s32[2,256,8]{1,2,0:T(8,128)}, u32[]{:S(2)}) copy-start(s32[2,256,8]{1,2,0:T(8,128)} %param.25) | copy-start | bytes 49156
  183.6 22.3 %copy-start.14 = (bf16[256,1024]{1,0:T(8,128)(2,1)}, bf16[256,1024]{1,0:T(8,128)(2,1)S(1)}, u32[]{:S(2)}) copy-start(bf16[256,1024]{1,0:T(8,128)(2,1)S(1)} %multiply_convert_fusion.2) | copy-start | bytes 1572868
  187.1 36.7 %copy-start.27 = (f32[1024,2]{1,0:T(8,128)S(1)}, f32[1024,2]{1,0:T(8,128)}, u32[]{:S(2)}) copy-start(f32[1024,2]{1,0:T(8,128)} %get-tuple-element.164) | copy-start | bytes 24580
  224.1 152.5 %copy-start.45 = (pred[256,16]{1,0:T(8,128)(4,1)}, pred[256,16]{1,0:T(8,128)(4,1)S(1)}, u32[]{:S(2)}) copy-start(pred[256,16]{1,0:T(8,128)(4,1)S(1)} %copy.163) | copy-start | bytes 12292
  272.7 3.6 copy-start.63
  272.7 3.5 copy-start.52
  498.4 582.1 %reduce-scatter.3.cloned.1.call-start = ((), (), s32[]{:S(2)}) async-start(), calls=%async_computation.2 | async-start | bytes 14155776 | tf_op jit(solution)/shard_map/reduce_scatter | solution.py:1204
  521.4 19.7 %copy-start.60 = (f32[256]{0:T(256)S(1)}, f32[256]{0:T(256)}, u32[]{:S(2)}) copy-start(f32[256]{0:T(256)} %copy-done.59) | copy-start | bytes 3076
  538.5 5.5 copy-start.72
  538.5 5.5 copy-start.12
  538.5 5.5 copy-start.21
  538.5 5.5 copy-start.23
  541.1 2.8 copy-start.37
  659.3 10.0 copy-start.53
  669.3 4.6 copy-start.64
  669.3 4.6 copy-start.6
  735.5 22.4 %copy-start.58 = (f32[256]{0:T(256)S(1)}, f32[256]{0:T(256)}, u32[]{:S(2)}) copy-start(f32[256]{0:T(256)} %copy-done.57) | copy-start | bytes 3076
  755.4 4.3 copy-start.70
  755.4 4.4 copy-start.20
  757.9 1.9 copy-start.39
  851.6 6.4 copy-start.15
  851.6 6.4 copy-start.40
  853.3 5.8 copy-start.51
  854.9 9.6 copy-start.31
  858.0 6.5 copy-start.33
  859.1 7.2 copy-start.17
  859.1 7.2 copy-start.38
  859.1 8.3 copy-start.73
  859.1 9.2 copy-start.68
  865.4 7.1 copy-start.9
  872.5 3.3 copy-start.7
  872.5 3.3 copy-start.42
  875.8 2.1 copy-start.32
  875.8 2.1 copy-start.34
  875.8 2.1 copy-start.44
  877.9 3.4 copy-start.30
  877.9 3.4 copy-start.43
  1063.2 2.2 copy-start.62
  1063.2 2.2 copy-start.76
  1063.2 2.3 copy-start.67
  1063.2 2.3 copy-start.74
  1063.2 2.3 copy-start.75
  1063.2 2.9 copy-start.49
  1063.3 2.9 copy-start.55
  1063.3 2.8 copy-start.56
  1067.0 2.6 copy-start.24
  1067.0 2.6 copy-start.35
  1067.0 2.6 copy-start.36
  1069.6 2.6 copy-start.29
  1072.0 2.2 copy-start.28
  1083.0 10.8 copy-start.13
  1083.0 10.8 copy-start.25
  1083.0 10.8 copy-start.26
  1093.8 4.0 copy-start.1
  (17 other events, 19.4 us)
Sparse Core Ops, SparseCore 0:
  12.0 217.1 all-gather.4
  232.0 200.5 all-gather.6
  498.6 261.3 reduce-scatter.4
  763.4 277.4 reduce-scatter.2

commit v5 on v4

--- a/solution.py
+++ b/solution.py
@@ -354,7 +354,7 @@
 ):
     g_refs = refs[: len(places)]
     (
-        o_ref, paired, came, going, crossed, last_in, pair_send, pair_recv, ring_send,
+        h_ref, o_ref, h_out, h_came, h_going, h_send, h_recv, paired, came, going, crossed, last_in, pair_send, pair_recv, ring_send,
         ring_recv, cross_send, cross_recv, last_send, last_recv,
     ) = refs[len(places) :]
     e, s = lax.axis_index("expert"), lax.axis_index("shard")
@@ -409,6 +409,21 @@
                 total = total + more[:, at : at + wide].astype(F32)
             target[:, at : at + wide] = total.astype(BF16)
 
+    few = h_ref.shape[1] // 2
+
+    def solo_copy(way, k, src):
+        return pltpu.make_async_remote_copy(
+            src_ref=src,
+            dst_ref=h_came.at[way, k],
+            send_sem=h_send.at[way, k],
+            recv_sem=h_recv.at[way, k],
+            device_id={"shard": ways[way]},
+            device_id_type=MESH,
+        )
+
+    def solo(way, b):
+        return h_ref.at[b, pl.ds(way * few, few)]
+
     order = []
     for k in range(n):
         for place in (k, n - 2 - k):
@@ -416,6 +431,8 @@
             if place not in order:
                 order.append(place)
     every = range(len(places))
+    for way in range(2):
+        solo_copy(way, 0, solo(way, block(way, 0))).start()
     for k in order:
         for i in every:
             pair_copy(k, i).start()
@@ -434,6 +451,12 @@
             ring_copy(way, k - 1).wait_recv()
             put(going.at[way, k], way, block(way, k), came.at[way, k - 1])
             ring_copy(way, k).start()
+        for way in range(2):
+            solo_copy(way, k - 1, h_going.at[way, k]).wait_recv()
+            h_going[way, k] = (
+                h_came[way, k - 1].astype(F32) + solo(way, block(way, k))[...].astype(F32)
+            ).astype(BF16)
+            solo_copy(way, k, h_going.at[way, k]).start()
         return carry
 
     lax.fori_loop(1, n - 1, step, 0)
@@ -442,6 +465,12 @@
         put(
             crossed.at[x, pl.ds(way * quarter, quarter)], way, s, came.at[way, n - 2]
         )
+
+    for way in range(2):
+        solo_copy(way, n - 2, h_going.at[way, 0]).wait_recv()
+        h_out[way * few : (way + 1) * few] = (
+            h_came[way, n - 2].astype(F32) + solo(way, s)[...].astype(F32)
+        ).astype(BF16)
 
     def cross_copy(d):
         return pltpu.make_async_remote_copy(
@@ -478,6 +507,7 @@
     def finish(k, carry):
         for way in range(2):
             ring_copy(way, k).wait_send()
+            solo_copy(way, k, h_going.at[way, k]).wait_send()
         return carry
 
     lax.fori_loop(0, n - 1, finish, 0)
@@ -485,7 +515,7 @@
     o_ref[pl.ds(pl.multiple_of((1 - core) * half, half), half), :] = last_in[...]
 
 
-def reduce_dense(grads, n, owners):
+def reduce_dense(grads, downs, n, owners):
     rows = grads[0].shape[1]
     places, columns = [], 0
     for grad in grads:
@@ -493,12 +523,20 @@
         columns += grad.shape[2]
     dma = pltpu.SemaphoreType.DMA
     across = owners // 2
+    some = (downs.shape[1] // 2,) + downs.shape[2:]
     return pl.pallas_call(
         functools.partial(reduce_dense_kernel, n, owners, rows, tuple(places)),
-        out_shape=jax.ShapeDtypeStruct((rows, columns), BF16),
-        in_specs=[pl.BlockSpec(memory_space=pltpu.VMEM)] * len(places),
-        out_specs=pl.BlockSpec(memory_space=pltpu.VMEM),
+        out_shape=[
+            jax.ShapeDtypeStruct((rows, columns), BF16),
+            jax.ShapeDtypeStruct(downs.shape[1:], BF16),
+        ],
+        in_specs=[pl.BlockSpec(memory_space=pltpu.VMEM)] * (len(places) + 1),
+        out_specs=[pl.BlockSpec(memory_space=pltpu.VMEM)] * 2,
         scratch_shapes=[
+            pltpu.VMEM((2, n - 1) + some, BF16),
+            pltpu.VMEM((2, n - 1) + some, BF16),
+            dma((2, n - 1)),
+            dma((2, n - 1)),
             pltpu.VMEM((n, rows // 2, columns), BF16),
             pltpu.VMEM((2, n - 1, rows // 4, columns), BF16),
             pltpu.VMEM((2, n - 1, rows // 4, columns), BF16),
@@ -511,7 +549,7 @@
             collective_id=4, has_side_effects=True, vmem_limit_bytes=VMEM_LIMIT
         ),
         name="reduce_dense",
-    )(*grads)
+    )(*grads, downs)
 
 
 def halo_links(n, s):
@@ -652,7 +690,7 @@
     )(kv)
 
 
-def halo_back_kernel(n, rows, cuts, g_ref, o_ref, own, came, sends, recvs):
+def halo_back_kernel(n, rows, cuts, q_ref, g_ref, o_ref, own, came, total, sends, recvs):
     s = lax.axis_index("shard")
     odd, mate, ahead, behind = halo_links(n, s)
     even = odd == 0
@@ -672,7 +710,17 @@
         here = pl.ds(cut * size, size)
         return ref[here, :].astype(F32)
 
+    def put(here):
+        pair, after = 2 * HEAD, q_ref.shape[1]
+        for j in range(KV_HEADS // 2):
+            for part in range(2):
+                at = after + part * KV_HEADS * HEAD + j * pair
+                o_ref[here, at : at + pair] = total[
+                    :, (2 * j + part) * pair : (2 * j + part + 1) * pair
+                ].astype(BF16)
+
     halo_barrier(s, odd, mate, ahead, behind, True)
+    width = q_ref.shape[1]
     for cut in range(cuts):
 
         @pl.when(s >= 3)
@@ -683,6 +731,7 @@
         def _():
             copy(2, cut, g_ref.at[3], mate).start()
 
+    o_ref[:, :width] = q_ref[...]
     for cut in range(cuts):
         here = pl.ds(cut * size, size)
 
@@ -723,17 +772,19 @@
 
     for cut in range(cuts):
         here = pl.ds(cut * size, size)
-        o_ref[here, :] = there(g_ref.at[4], cut)
+        total[...] = there(g_ref.at[4], cut)
 
         @pl.when(even)
         def _():
             copy(2, cut, g_ref.at[3], mate).wait_recv()
-            o_ref[here, :] += there(came.at[2], cut)
+            total[...] += there(came.at[2], cut)
 
         @pl.when(ahead)
         def _():
             copy(0, cut, own.at[1], s).wait_recv()
-            o_ref[here, :] += there(came.at[0], cut)
+            total[...] += there(came.at[0], cut)
+
+        put(here)
 
         @pl.when(s >= 3)
         def _():
@@ -752,18 +803,19 @@
             copy(0, cut, own.at[1], mate).wait_send()
 
 
-def halo_back(grads, n):
+def halo_back(d_queries, grads, n):
     slots, rows, columns = grads.shape
     dma = pltpu.SemaphoreType.DMA
     cuts = 2
     return pl.pallas_call(
         functools.partial(halo_back_kernel, n, rows, cuts),
-        out_shape=jax.ShapeDtypeStruct((rows, columns), F32),
-        in_specs=[pl.BlockSpec(memory_space=pltpu.VMEM)],
+        out_shape=jax.ShapeDtypeStruct((rows, d_queries.shape[1] + columns), BF16),
+        in_specs=[pl.BlockSpec(memory_space=pltpu.VMEM)] * 2,
         out_specs=pl.BlockSpec(memory_space=pltpu.VMEM),
         scratch_shapes=[
-            pltpu.VMEM((3, rows, columns), BF16),
+            pltpu.VMEM((2, rows, columns), BF16),
             pltpu.VMEM((4, rows, columns), BF16),
+            pltpu.VMEM((rows // cuts, columns), F32),
             dma((4, cuts)),
             dma((4, cuts)),
         ],
@@ -771,7 +823,7 @@
             collective_id=6, has_side_effects=True, vmem_limit_bytes=VMEM_LIMIT
         ),
         name="halo_back",
-    )(grads)
+    )(d_queries, grads)
 
 
 def attend_kernel(q_ref, k_ref, v_ref, bias_ref, o_ref, total_ref):
@@ -954,12 +1006,11 @@
     gate_up_ref,
     w_ref,
     part_ref,
-    grad_ref,
-    acc,
-    d_gate_up,
-    hidden_all,
-    d_weights,
+    *refs,
 ):
+    acc, d_gate_up, hidden_all, d_weights = refs[-4:]
+    grad_in = refs[0].at[:, 0, :in_rows]
+    grad_down = refs[0].at[:, 0, in_rows:] if len(refs) == 5 else refs[1].at[:, 0]
     e = pl.program_id(0)
     inner = w_ref.shape[-1]
     w_in = w_ref[:, 0, :in_rows, :].reshape(width, inner)
@@ -1004,18 +1055,19 @@
             part_ref[rows, :width] = acc[rows, :].astype(BF16)
             part_ref[rows, width:] = d_weights[rows, :].astype(BF16)
 
-    grad_ref[:, 0, :in_rows, :] = (
+    grad_in[...] = (
         inner_rows(x_ref[:, :width], d_gate_up[...]).astype(BF16).reshape(-1, in_rows, inner)
     )
-    grad_ref[:, 0, in_rows:, :] = (
+    grad_down[...] = (
         inner_rows(hidden_all[...], g_ref[...])
         .astype(BF16)
         .reshape(-1, w_ref.shape[2] - in_rows, width)
     )
 
 
-def ffn_backward(first, x_all, g_all, gate_up, w_all, experts_total, in_rows):
+def ffn_backward(first, x_all, g_all, gate_up, w_all, experts_total, in_rows, apart):
     shards, local, piece, inner = w_all.shape
+    pieces = (in_rows, piece - in_rows) if apart else (piece,)
     tokens, wide = x_all.shape
     width = in_rows * shards
     return pl.pallas_call(
@@ -1031,8 +1083,8 @@
             ],
             out_specs=[
                 pl.BlockSpec((tokens, wide), lambda e, f: (0, 0)),
-                pl.BlockSpec((shards, 1, piece, inner), lambda e, f: (0, e, 0, 0)),
-            ],
+            ]
+            + [pl.BlockSpec((shards, 1, some, inner), lambda e, f: (0, e, 0, 0)) for some in pieces],
             scratch_shapes=[
                 pltpu.VMEM((tokens, width), F32),
                 pltpu.VMEM((tokens, inner), BF16),
@@ -1042,8 +1094,8 @@
         ),
         out_shape=[
             jax.ShapeDtypeStruct((tokens, wide), BF16),
-            jax.ShapeDtypeStruct(w_all.shape, BF16),
-        ],
+        ]
+        + [jax.ShapeDtypeStruct((shards, local, some, inner), BF16) for some in pieces],
         compiler_params=pltpu.CompilerParams(vmem_limit_bytes=VMEM_LIMIT),
         cost_estimate=pl.CostEstimate(
             flops=4 * local * tokens * width * (inner + inner // 2),
@@ -1174,7 +1226,8 @@
         )
         if layer_no + 1 == LAYERS:
             d_partial, d_experts = ffn_backward(
-                first_array, x_all, g_all, gate_up, expert_full[layer_no], experts_total, in_rows
+                first_array, x_all, g_all, gate_up, expert_full[layer_no], experts_total,
+                in_rows, False,
             )
             partial, d_partial = lax.optimization_barrier((partial, d_partial))
         moe_out = collect(partial.reshape(owners, tok_rows, width), 2)
@@ -1198,8 +1251,9 @@
         ) = kept_layers[layer_no]
         if layer_no + 1 < LAYERS:
             g_all = spread(grad_stream.astype(BF16), owners, 8).reshape(owners * tok_rows, width)
-            d_partial, d_experts = ffn_backward(
-                first_array, x_all, g_all, gate_up, expert_full[layer_no], experts_total, in_rows
+            d_partial, d_experts, d_down_parts = ffn_backward(
+                first_array, x_all, g_all, gate_up, expert_full[layer_no], experts_total,
+                in_rows, True,
             )
         d_experts = lax.psum_scatter(d_experts, "shard", scatter_dimension=0, tiled=True)[0]
         d_all = collect(d_partial.reshape(owners, tok_rows, -1), 7)
@@ -1218,15 +1272,8 @@
         d_w_out = inner_rows(attended, d_att)
         d_attended = outer_cols(d_att, w_out_full).astype(BF16)
         d_queries, d_kv = attend_back(qkv_rows, ext, bias, d_attended, log_total)
-        d_kv = halo_back(d_kv.reshape(hop_count + 1, tok_rows, 2 * kv_width), shards)
-        d_kv = d_kv.astype(BF16).reshape(tok_rows, KV_HEADS // 2, 2, 2 * HEAD)
-        d_qkv = jnp.concatenate(
-            [
-                d_queries,
-                d_kv[:, :, 0].reshape(tok_rows, kv_width),
-                d_kv[:, :, 1].reshape(tok_rows, kv_width),
-            ],
-            1,
+        d_qkv = halo_back(
+            d_queries, d_kv.reshape(hop_count + 1, tok_rows, 2 * kv_width), shards
         )
         d_w_qkv = inner_rows(normed_one, d_qkv)
         d_normed_one = outer_cols(d_qkv, w_qkv_full)
@@ -1240,13 +1287,15 @@
         ]
         collected[layer_no] = (
             d_experts[:, :in_rows, :].astype(F32),
-            d_experts[:, in_rows:, :].astype(F32),
+            d_experts[:, in_rows:, :].astype(F32) if layer_no + 1 == LAYERS else None,
         )
     small = sum(small_parts, [])
     small.append(jnp.zeros((width, side - LAYERS * (experts_total + 2)), BF16))
     parts = sum(dense_parts, []) + [jnp.concatenate(small, 1)]
     d_dense = [part.reshape(shards, width // shards, -1) for part in parts]
-    d_dense = reduce_dense(d_dense, shards, owners).astype(F32)
+    d_dense, d_down = reduce_dense(d_dense, d_down_parts, shards, owners)
+    d_dense = d_dense.astype(F32)
+    collected[0] = (collected[0][0], d_down.astype(F32))
     for layer_no in range(LAYERS):
         at = layer_no * layer_columns
         d_main = d_dense[:, at : at + layer_columns]

time: 1110 us -> 1100 us (level)
  local copies, waits for them, and re-layouts: 50.7 us -> 31.3 us
  transfers between devices with their start and end apart: 4 -> 4, of which waited for: 2 -> 2; matrix products, arithmetic and copies ran while one was open for 11% -> 10% of each run, Pallas kernels for 75% -> 77%
where the time goes in v5:
time: 1100 us; the launch traced here: 1090 us
  Pallas kernels  900 us (82%)
  other arithmetic  54.5 us (5%)
  matrix products  50.2 us (5%)
  waiting for transfers between devices  35.1 us (3%)
  local copies, waits for them, and re-layouts  31.3 us (3%)
  between operations  15.1 us (1%)
    pallas_call x1, Pallas kernels, reduce_dense(): pl.pallas_call(functools.partial(reduce_dense_kernel, n, owners, rows, tu...  183 us
    pallas_call x2, Pallas kernels, halo_back(): pl.pallas_call(functools.partial(halo_back_kernel, n, rows, cuts), out_sh...  144 us
    pallas_call x2, Pallas kernels, halo(): pl.pallas_call(functools.partial(halo_kernel, n, rows, cuts), out_shape=j...  107 us
    pallas_call x1, Pallas kernels, gather_dense(): pl.pallas_call(functools.partial(gather_dense_kernel, n, owners, rows), o...  105 us
    pallas_call x2, Pallas kernels, ffn_backward(): pl.pallas_call(functools.partial(ffn_backward_kernel, 256, width, in_rows...  85.2 us
    pallas_call x4, Pallas kernels, collect(): pl.pallas_call(functools.partial(collect_kernel, owners, cuts), out_shape...  76.6 us
    pallas_call x4, Pallas kernels, spread(): pl.pallas_call(functools.partial(spread_kernel, owners, cuts), out_shape=...  73.7 us
    pallas_call x2, Pallas kernels, ffn_forward(): pl.pallas_call(functools.partial(ffn_forward_kernel, 256, width, in_rows,...  46.7 us
  transfers between devices with their start and end apart: 4, of which 2 were waited for; matrix products, arithmetic and copies ran while one was open for 10% of the time, Pallas kernels for 77%

profile of v5, /device:TPU:0, one launch (start us, length us, event | category | flops | bytes accessed | tf_op | source)
XLA Modules:
  0.0 1086.1 jit_solution(4420162089469441350)
XLA Ops:
  7.3 1.9 convert.52
  10.6 1.3 pad_maximum_fusion.1
  11.9 2.6 pad_maximum_fusion.2
  14.8 1.3 convert.48
  16.6 2.0 concatenate.19.x_ref
  18.5 104.5 %gather_dense.1 = bf16[8,128,6656]{2,1,0:T(8,128)(2,1)} custom-call(bf16[128,6656]{1,0:T(8,128)(2,1)} %concatenate.19.x_ref), custom_call_target="tpu_custom_call" | custom-call | tf_op jit(solution)/shard_map/gather_dense/pallas_call | solution.py:336
  123.1 1.3 slice_convert_fusion
  125.3 3.5 fusion.9.q_ref
  130.7 30.1 %halo.2 = bf16[5,256,1024]{2,1,0:T(8,128)(2,1)} custom-call(bf16[256,1024]{1,0:T(8,128)(2,1)} %slice.221.kv_ref), custom_call_target="tpu_custom_call" | custom-call | tf_op jit(solution)/shard_map/halo/pallas_call | solution.py:680
  162.3 1.8 fusion.33.bias_ref
  164.1 16.8 %attend.2 = (bf16[256,1024]{1,0:T(8,128)(2,1)}, f32[4,8,256]{2,1,0:T(8,128)}) custom-call(bf16[256,2048]{1,0:T(8,128)(2,1)} %copy-done.35, bf16[1280,1024]{1,0:T(8,128)(2,1)} %bitcast.121, bf16[1280,1024]{1,0:T(8,128)(2,1)} %bitcast.122, f32[1280,256]{1,0:T(8,128)} %fusion.33.bias_ref), custom_call_target="tpu_custom_call" | custom-call | flops 1342177280 | bytes 3932160 | tf_op jit(solution)/shard_map/attend/pallas_call | solution.py:858
  180.9 2.6 multiply_reduce_fusion.10
  184.2 1.4 select_reduce_fusion.1
  186.7 1.7 concatenate.20.x_ref
  188.4 18.6 %spread.4 = bf16[4,256,1152]{2,1,0:T(8,128)(2,1)} custom-call(bf16[256,1152]{1,0:T(8,128)(2,1)} %concatenate.20.x_ref), custom_call_target="tpu_custom_call" | custom-call | tf_op jit(solution)/shard_map/spread/pallas_call | solution.py:125
  207.1 18.0 %spread.5 = bf16[4,256,1024]{2,1,0:T(8,128)(2,1)} custom-call(bf16[256,1024]{1,0:T(8,128)(2,1)} %convert_element_type.164.x_ref), custom_call_target="tpu_custom_call" | custom-call | tf_op jit(solution)/shard_map/spread/pallas_call | solution.py:125
  225.4 3.8 all-gather.5.cloned.1.call-done
  229.2 23.3 %ffn_forward.2 = (bf16[1024,1024]{1,0:T(8,128)(2,1)}, bf16[4,1024,1024]{2,1,0:T(8,128)(2,1)}) custom-call(s32[1]{0:T(128)} %bitcast.16.first_ref, bf16[1024,1152]{1,0:T(8,128)(2,1)} %bitcast.131, bf16[8,4,192,1024]{3,2,1,0:T(8,128)(2,1)} %bitcast.163), custom_call_target="tpu_custom_call" | custom-call | flops 12884901888 | bytes 25690112 | tf_op jit(solution)/shard_map/ffn_forward/pallas_call | solution.py:969
  252.6 18.6 %collect.4 = f32[256,1024]{1,0:T(8,128)} custom-call(bf16[4,256,1024]{2,1,0:T(8,128)(2,1)} %bitcast.140), custom_call_target="tpu_custom_call" | custom-call | tf_op jit(solution)/shard_map/collect/pallas_call | solution.py:202
  271.2 1.5 multiply_reduce_fusion.9
  272.7 3.5 fusion.12.q_ref
  278.0 77.1 %halo.3 = bf16[5,256,1024]{2,1,0:T(8,128)(2,1)} custom-call(bf16[256,1024]{1,0:T(8,128)(2,1)} %slice.230.kv_ref), custom_call_target="tpu_custom_call" | custom-call | tf_op jit(solution)/shard_map/halo/pallas_call | solution.py:680
  355.1 16.8 %attend.3 = (bf16[256,1024]{1,0:T(8,128)(2,1)}, f32[4,8,256]{2,1,0:T(8,128)}) custom-call(bf16[256,2048]{1,0:T(8,128)(2,1)} %copy-done.36, bf16[1280,1024]{1,0:T(8,128)(2,1)} %bitcast.125, bf16[1280,1024]{1,0:T(8,128)(2,1)} %bitcast.126, f32[1280,256]{1,0:T(8,128)} %fusion.33.bias_ref), custom_call_target="tpu_custom_call" | custom-call | flops 1342177280 | bytes 3932160 | tf_op jit(solution)/shard_map/attend/pallas_call | solution.py:858
  372.0 2.6 multiply_reduce_fusion.8
  376.5 1.4 select_reduce_fusion
  378.6 1.6 subtract_convert_fusion
  380.2 1.9 concatenate.22.x_ref
  382.1 19.3 %spread.6 = bf16[4,256,1152]{2,1,0:T(8,128)(2,1)} custom-call(bf16[256,1152]{1,0:T(8,128)(2,1)} %concatenate.22.x_ref), custom_call_target="tpu_custom_call" | custom-call | tf_op jit(solution)/shard_map/spread/pallas_call | solution.py:125
  401.4 31.2 %all-gather.7.cloned.1.call-done = bf16[32,192,1024]{2,1,0:T(8,128)(2,1)} async-done(((bf16[4,192,1024]{2,1,0:T(8,128)(2,1)}), bf16[32,192,1024]{2,1,0:T(8,128)(2,1)}) %all-gather.7.cloned.1.call-update) | async-done | bytes 12582928 | tf_op jit(solution)/shard_map/all_gather | solution.py:1189
  432.6 23.4 %ffn_forward.3 = (bf16[1024,1024]{1,0:T(8,128)(2,1)}, bf16[4,1024,1024]{2,1,0:T(8,128)(2,1)}) custom-call(s32[1]{0:T(128)} %bitcast.16.first_ref, bf16[1024,1152]{1,0:T(8,128)(2,1)} %bitcast.135, bf16[8,4,192,1024]{3,2,1,0:T(8,128)(2,1)} %bitcast.165), custom_call_target="tpu_custom_call" | custom-call | flops 12884901888 | bytes 25690112 | tf_op jit(solution)/shard_map/ffn_forward/pallas_call | solution.py:969
  456.0 42.4 %ffn_backward.2 = (bf16[1024,1152]{1,0:T(8,128)(2,1)}, bf16[8,4,192,1024]{3,2,1,0:T(8,128)(2,1)}) custom-call(s32[1]{0:T(128)} %bitcast.16.first_ref, bf16[1024,1152]{1,0:T(8,128)(2,1)} %bitcast.136, bf16[1024,1024]{1,0:T(8,128)(2,1)} %bitcast.137, bf16[4,1024,1024]{2,1,0:T(8,128)(2,1)} %get-tuple-element.59.gate_up_ref, bf16[8,4,192,1024]{3,2,1,0:T(8,128)(2,1)} %bitcast.166), custom_call_target="tpu_custom_call" | custom-call | flops 25769803776 | bytes 42991616 | tf_op jit(solution)/shard_map/ffn_backward/pallas_call | solution.py:1073
  498.5 19.9 %collect.6 = f32[256,1152]{1,0:T(8,128)} custom-call(bf16[4,256,1152]{2,1,0:T(8,128)(2,1)} %bitcast.133), custom_call_target="tpu_custom_call" | custom-call | tf_op jit(solution)/shard_map/collect/pallas_call | solution.py:202
  518.4 18.1 %collect.5 = f32[256,1024]{1,0:T(8,128)} custom-call(bf16[4,256,1024]{2,1,0:T(8,128)(2,1)} %bitcast.139), custom_call_target="tpu_custom_call" | custom-call | tf_op jit(solution)/shard_map/collect/pallas_call | solution.py:202
  536.6 1.3 multiply_reduce_fusion.13
  539.0 3.5 multiply_reduce_fusion
  542.6 1.3 fusion.40
  544.8 3.1 fusion.37.d_ref
  548.0 22.4 %attend_back.2 = (bf16[256,1024]{1,0:T(8,128)(2,1)}, bf16[1280,1024]{1,0:T(8,128)(2,1)}) custom-call(bf16[256,2048]{1,0:T(8,128)(2,1)} %copy-done.36, bf16[1280,1024]{1,0:T(8,128)(2,1)} %bitcast.127, bf16[1280,1024]{1,0:T(8,128)(2,1)} %bitcast.128, f32[1280,256]{1,0:T(8,128)} %fusion.33.bias_ref, bf16[256,1024]{1,0:T(8,128)(2,1)} %fusion.37.d_ref, ...), custom_call_target="tpu_custom_call" | custom-call | flops 3355443200 | bytes 6553600 | tf_op jit(solution)/shard_map/attend_back/pallas_call | solution.py:909
  570.4 85.7 %halo_back.2 = bf16[256,2048]{1,0:T(8,128)(2,1)} custom-call(bf16[256,1024]{1,0:T(8,128)(2,1)} %get-tuple-element.64.q_ref, bf16[5,256,1024]{2,1,0:T(8,128)(2,1)} %bitcast.130), custom_call_target="tpu_custom_call" | custom-call | tf_op jit(solution)/shard_map/halo_back/pallas_call | solution.py:810
  656.2 4.7 multiply_reduce_fusion.1
  660.9 1.4 fusion.79
  662.4 17.9 %spread.7 = bf16[4,256,1024]{2,1,0:T(8,128)(2,1)} custom-call(bf16[256,1024]{1,0:T(8,128)(2,1)} %get-tuple-element.160.x_ref), custom_call_target="tpu_custom_call" | custom-call | tf_op jit(solution)/shard_map/spread/pallas_call | solution.py:125
  680.2 42.8 %ffn_backward.3 = (bf16[1024,1152]{1,0:T(8,128)(2,1)}, bf16[8,4,128,1024]{3,2,1,0:T(8,128)(2,1)}, bf16[8,4,64,1024]{3,2,1,0:T(8,128)(2,1)}) custom-call(s32[1]{0:T(128)} %bitcast.16.first_ref, bf16[1024,1152]{1,0:T(8,128)(2,1)} %bitcast.132, bf16[1024,1024]{1,0:T(8,128)(2,1)} %bitcast.138, bf16[4,1024,1024]{2,1,0:T(8,128)(2,1)} %get-tuple-element.66.gate_up_ref, ...), custom_call_target="tpu_custom_call" | custom-call | flops 25769803776 | bytes 42991616 | tf_op jit(solution)/shard_map/ffn_backward/pallas_call | solution.py:1073
  723.0 20.0 %collect.7 = f32[256,1152]{1,0:T(8,128)} custom-call(bf16[4,256,1152]{2,1,0:T(8,128)(2,1)} %bitcast.134), custom_call_target="tpu_custom_call" | custom-call | tf_op jit(solution)/shard_map/collect/pallas_call | solution.py:202
  747.1 2.0 multiply_reduce_fusion.2
  751.7 3.1 fusion.34.d_ref
  754.8 22.3 %attend_back.3 = (bf16[256,1024]{1,0:T(8,128)(2,1)}, bf16[1280,1024]{1,0:T(8,128)(2,1)}) custom-call(bf16[256,2048]{1,0:T(8,128)(2,1)} %copy-done.35, bf16[1280,1024]{1,0:T(8,128)(2,1)} %bitcast.123, bf16[1280,1024]{1,0:T(8,128)(2,1)} %bitcast.124, f32[1280,256]{1,0:T(8,128)} %fusion.33.bias_ref, bf16[256,1024]{1,0:T(8,128)(2,1)} %fusion.34.d_ref, ...), custom_call_target="tpu_custom_call" | custom-call | flops 3355443200 | bytes 6553600 | tf_op jit(solution)/shard_map/attend_back/pallas_call | solution.py:909
  777.1 58.5 %halo_back.3 = bf16[256,2048]{1,0:T(8,128)(2,1)} custom-call(bf16[256,1024]{1,0:T(8,128)(2,1)} %get-tuple-element.69.q_ref, bf16[5,256,1024]{2,1,0:T(8,128)(2,1)} %bitcast.129), custom_call_target="tpu_custom_call" | custom-call | tf_op jit(solution)/shard_map/halo_back/pallas_call | solution.py:810
  835.6 5.6 multiply_reduce_fusion.3
  846.7 2.7 concatenate.24
  849.4 3.2 convolution_convert_fusion.3
  852.7 2.1 convolution_convert_fusion.2
  854.7 3.4 convolution_convert_fusion.1
  858.1 3.4 convolution_convert_fusion
  861.5 183.2 %reduce_dense.1 = (bf16[128,6272]{1,0:T(8,128)(2,1)}, bf16[4,64,1024]{2,1,0:T(8,128)(2,1)}) custom-call(bf16[8,128,2048]{2,1,0:T(8,128)(2,1)} %bitcast.104, bf16[8,128,1024]{2,1,0:T(8,128)(2,1)} %bitcast.119, bf16[8,128,2048]{2,1,0:T(8,128)(2,1)} %bitcast.105, bf16[8,128,1024]{2,1,0:T(8,128)(2,1)} %bitcast.120, bf16[8,128,128]{2,1,0:T(8,128)(2,1)} %bitcast.143, ...), custom_call_target="tpu_custom_call" | custom-call | tf_op jit(solution)/shard_map/reduce_dense/pallas_call | solution.py:527
  1044.8 1.7 convert_element_type.192
  1048.5 2.6 fusion.43
  1051.2 2.3 add_multiply_fusion.3
  1053.8 1.3 copy-done.19
  1055.7 4.0 add_multiply_fusion.2
  1059.7 1.2 slice_bitcast_fusion.5
  1060.9 1.3 slice_bitcast_fusion
  1062.3 6.3 add_multiply_fusion.1
  1068.6 10.7 add_multiply_fusion
  (207 shorter events, 30.2 us)
Async XLA Ops:
  7.2 153.6 %copy-start = (s32[4,4]{1,0:T(4,128)S(1)}, s32[4,4]{1,0:T(4,128)}, u32[]{:S(2)}) copy-start(s32[4,4]{1,0:T(4,128)} %param.24) | copy-start | bytes 196
  7.2 222.0 %all-gather.5.cloned.1.call-start = ((), (), s32[]{:S(2)}) async-start(), calls=%async_computation.4 | async-start | bytes 14155776 | tf_op jit(solution)/shard_map/all_gather | solution.py:1189
  7.3 2.8 copy-start.2
  11.9 420.7 %all-gather.7.cloned.1.call-start = ((), (), s32[]{:S(2)}) async-start(), calls=%async_computation.5 | async-start | bytes 14155776 | tf_op jit(solution)/shard_map/all_gather | solution.py:1189
  11.9 2.7 copy-start.18
  14.5 1045.2 %reduce-scatter.5.cloned.1.call-start = ((), (), s32[]{:S(2)}) async-start(), calls=%async_computation.3 | async-start | bytes 14155776 | tf_op jit(solution)/shard_map/reduce_scatter | solution.py:1258
  14.6 1.5 copy-start.37
  14.6 1.6 copy-start.54
  123.1 1.5 copy-start.3
  124.8 4.1 copy-start.39
  128.9 1.0 copy-start.35
  129.8 31.2 %copy-start.22 = (f32[256,1024]{1,0:T(8,128)S(1)}, f32[256,1024]{1,0:T(8,128)}, u32[]{:S(2)}) copy-start(f32[256,1024]{1,0:T(8,128)} %param.23) | copy-start | bytes 3145732
  130.7 31.2 %copy-start.43 = (s32[2,256,8]{1,2,0:T(8,128)S(1)}, s32[2,256,8]{1,2,0:T(8,128)}, u32[]{:S(2)}) copy-start(s32[2,256,8]{1,2,0:T(8,128)} %param.25) | copy-start | bytes 49156
  183.5 4.9 copy-start.46
  184.2 22.9 %copy-start.14 = (bf16[256,1024]{1,0:T(8,128)(2,1)}, bf16[256,1024]{1,0:T(8,128)(2,1)S(1)}, u32[]{:S(2)}) copy-start(bf16[256,1024]{1,0:T(8,128)(2,1)S(1)} %multiply_convert_fusion.2) | copy-start | bytes 1572868
  186.7 20.4 %copy-start.31 = (bf16[256,96]{1,0:T(8,128)(2,1)}, bf16[256,96]{1,0:T(8,128)(2,1)S(1)}, u32[]{:S(2)}) copy-start(bf16[256,96]{1,0:T(8,128)(2,1)S(1)} %broadcast.296) | copy-start | bytes 147460
  225.4 152.6 %copy-start.34 = (pred[256,16]{1,0:T(8,128)(4,1)}, pred[256,16]{1,0:T(8,128)(4,1)S(1)}, u32[]{:S(2)}) copy-start(pred[256,16]{1,0:T(8,128)(4,1)S(1)} %copy.147) | copy-start | bytes 12292
  272.7 3.6 copy-start.51
  272.7 3.5 copy-start.41
  276.2 1.0 copy-start.36
  374.5 1.0 copy-start.11
  374.6 3.3 copy-start.58
  374.6 3.3 copy-start.47
  498.4 570.2 %reduce-scatter.3.cloned.1.call-start = ((), (), s32[]{:S(2)}) async-start(), calls=%async_computation.2 | async-start | bytes 9437184 | tf_op jit(solution)/shard_map/reduce_scatter | solution.py:1258
  518.4 20.6 %copy-start.48 = (f32[256]{0:T(256)S(1)}, f32[256]{0:T(256)}, u32[]{:S(2)}) copy-start(f32[256]{0:T(256)} %copy-done.47) | copy-start | bytes 3076
  536.5 6.0 copy-start.59
  536.5 6.0 copy-start.12
  536.6 6.0 copy-start.21
  536.6 6.0 copy-start.23
  543.9 1.0 copy-start.5
  570.4 85.7 %copy-start.42 = (f32[256]{0:T(256)S(1)}, f32[256]{0:T(256)}, u32[]{:S(2)}) copy-start(f32[256]{0:T(256)} %copy-done.41) | copy-start | bytes 3076
  656.2 4.7 copy-start.52
  656.2 4.7 copy-start.6
  723.0 22.3 %copy-start.15 = (bf16[256,1024]{1,0:T(8,128)(2,1)S(1)}, bf16[256,1024]{1,0:T(8,128)(2,1)}, u32[]{:S(2)}) copy-start(bf16[256,1024]{1,0:T(8,128)(2,1)} %copy-done.14) | copy-start | bytes 1572868
  747.1 2.7 copy-start.20
  750.7 1.0 copy-start.8
  777.1 58.5 %copy-start.40 = (f32[256]{0:T(256)S(1)}, f32[256]{0:T(256)}, u32[]{:S(2)}) copy-start(f32[256]{0:T(256)} %copy-done.39) | copy-start | bytes 3076
  835.6 7.5 copy-start.17
  835.6 8.5 copy-start.60
  835.6 9.4 copy-start.56
  842.1 7.2 copy-start.9
  849.4 3.3 copy-start.7
  849.4 3.3 copy-start.32
  852.7 2.1 copy-start.25
  854.7 3.4 copy-start.24
  1044.7 2.2 copy-start.50
  1044.7 2.3 copy-start.63
  1044.7 2.3 copy-start.55
  1044.8 2.3 copy-start.61
  1044.8 2.3 copy-start.62
  1044.8 2.9 copy-start.38
  1044.8 2.9 copy-start.44
  1044.8 2.8 copy-start.45
  1046.9 1.5 copy-start.4
  1046.9 1.6 copy-start.10
  1048.5 2.6 copy-start.26
  1048.5 2.6 copy-start.29
  1048.5 2.6 copy-start.30
  1051.2 2.6 copy-start.28
  1053.5 1.6 copy-start.19
  1053.5 2.2 copy-start.27
  1059.7 2.5 copy-start.13
  1059.7 2.5 copy-start.33
  1068.6 10.7 copy-start.1
  (4 other events, 2.5 us)
Sparse Core Ops, SparseCore 0:
  12.0 217.1 all-gather.4
  232.0 200.5 all-gather.6
  498.6 262.5 reduce-scatter.4
  764.7 187.2 reduce-scatter.2
